TPU v7x, 256 devices: a whole 4x4x8 slice. The times are simulated.
256 devices in a mesh: grp: 4 (over x), row: 64 (over y, z, core).
Axes of the slice: x: 4, y: 4, z: 8, core: 2. Of those that a mesh axis runs over, the one named last changes fastest.
Arguments:
- snapshots: float32 [229376, 2048], P('row', 'grp'), may hold values from -24 to 24, as said below
- test_block: float32 [229376, 512], P('row', 'grp'), may hold values from -24 to 24, as said below
- start_block: float32 [2048, 64], P('grp'), may hold values from -6 to 6
- start_merge: float32 [256, 64], replicated, may hold values from -6 to 6
Outputs:
- projected: float32 [229376, 512], P('row', 'grp')
Inputs may be any that keep to these rules, and one draw needn't show every extreme that they name: snapshots are float32 values of order one, full rank. test_block holds float32 values of order one.
All inputs are finite; a program needn't handle non-finite values.
Results may differ from a plain program's by a relative error of at most 0.0003.
Values sent between devices are 32-bit elements; how exact they have to be, the bound alone decides.
No kernel may reach another device: no remote copies, remote signals or barrier semaphores. Data moves between devices by JAX's collectives and lax.ppermute only.
A program may use at most 64 MiB of HBM per device.

v0:
```python
import functools
import math

import jax
import jax.numpy as jnp
from jax import lax
from jax.sharding import Mesh
from jax.sharding import PartitionSpec as P

ITERS = 6
ROW = ("row_0", "row_1", "row_2")


def in_blocks(array, dim, length):
    shape = array.shape
    blocks = array.reshape(*shape[:dim], length, shape[dim] // length, *shape[dim + 1 :])
    return jnp.moveaxis(blocks, dim, 0)


def sent_and_summed(array, axis, dim):
    length = lax.axis_size(axis)
    blocks = lax.all_to_all(in_blocks(array, dim, length), axis, 0, 0, tiled=True)
    return jnp.sum(blocks, axis=0)


def sum_in_two_steps(array, axes, dim):
    far, near = axes
    blocks = in_blocks(array, dim, lax.axis_size(far))
    nearer = sent_and_summed(blocks, near, dim + 1)
    arrived = lax.all_to_all(nearer, far, split_axis=0, concat_axis=0, tiled=True)
    return arrived.sum(axis=0)


def sent_to_all(array, axis):
    copies = jnp.broadcast_to(array, (lax.axis_size(axis), *array.shape))
    return lax.all_to_all(copies, axis, split_axis=0, concat_axis=0, tiled=True)


def laid_out(blocks, dim):
    blocks = jnp.moveaxis(blocks, 0, dim)
    shape = blocks.shape
    return blocks.reshape(*shape[:dim], shape[dim] * shape[dim + 1], *shape[dim + 2 :])


def gathered_copies(array, axis, dim):
    blocks = sent_to_all(array, axis)
    return laid_out(blocks, dim)


def filled_up(lines, length):
    spare = -lines.shape[0] % length
    if not spare:
        return lines
    return jnp.concatenate([lines, jnp.zeros((spare, *lines.shape[1:]), lines.dtype)])


def nested_sum(array, axes):
    lines = array.reshape(-1, array.shape[-1])
    own = sent_and_summed(filled_up(lines, lax.axis_size(axes)), axes, 0)
    whole = gathered_copies(own, axes, 0)
    return whole[: len(lines)].reshape(array.shape)


def by_axis(array, axes):
    return functools.reduce(lax.psum, axes, array)


def highdot(left, right):
    return jnp.dot(left, right, precision=lax.Precision.HIGHEST, preferred_element_type=jnp.float32)


def orthonormal(tall_block):
    small_gram = highdot(tall_block.T, tall_block)
    lower_factor = jnp.linalg.cholesky(small_gram)
    return lax.linalg.triangular_solve(
        lower_factor, tall_block, left_side=False, lower=True, transpose_a=True
    )


def merge_solve(merged_gram, start_merge):
    merge_coef = orthonormal(start_merge)
    for sweep_index in range(ITERS):
        merge_coef = orthonormal(highdot(merged_gram, merge_coef))
    energy = highdot(merge_coef.T, highdot(merged_gram, merge_coef))
    lower_factor = jnp.linalg.cholesky(energy)
    return lax.linalg.triangular_solve(
        lower_factor, merge_coef, left_side=False, lower=True, transpose_a=True
    )


def on_device(snapshots, test_block, start_block, start_merge):
    rows_dev, snap_width = snapshots.shape
    row_total = rows_dev * lax.axis_size(ROW)
    gram_rows = (
        sum_in_two_steps(highdot(snapshots.T, snapshots), (("row_0", "row_1"), "row_2"), 0)
        / row_total
    )
    iterate = orthonormal(start_block)
    for sweep_index in range(ITERS):
        product = highdot(gram_rows, iterate)
        iterate = orthonormal(gathered_copies(product, ROW, 0))
    group_basis = highdot(snapshots, iterate)
    joined = gathered_copies(group_basis, "grp", 1)
    merged_gram = nested_sum(highdot(joined.T, joined), ROW) / row_total
    merge_coef = merge_solve(merged_gram, start_merge)
    merged_modes = highdot(joined, merge_coef) / math.sqrt(row_total)
    test_coeffs = by_axis(highdot(merged_modes.T, test_block), ROW)
    return highdot(merged_modes, test_coeffs)


def solution(mesh):
    finer = Mesh(
        mesh.devices.reshape(mesh.shape["grp"], 4, 8, 2), ("grp", "row_0", "row_1", "row_2")
    )
    placed = (P(ROW, "grp"), P(ROW, "grp"), P("grp", None), P())
    return jax.shard_map(
        on_device, mesh=finer, in_specs=placed, out_specs=P(ROW, "grp"), check_vma=False
    )
```

profile of v0, /device:TPU:1, one launch (start us, length us, event | category | flops | bytes accessed | tf_op | source)
XLA Modules:
  0.0 490.3 jit_solution(1117492669274309695)
XLA Ops:
  0.0 17.3 %fusion.95 = f32[512,512]{1,0:T(8,128)S(1)} fusion(f32[3584,512]{1,0:T(8,128)} %param.9), kind=kOutput, calls=%fused_computation.176 | convolution fusion | flops 11274289152 | bytes 8388608 | tf_op jit(solution)/shard_map/dot_general | solution.py:69
  17.4 7.4 %all_to_all.55 = f32[2,32,8,512]{3,2,1,0:T(8,128)S(1)} all-to-all(f32[2,32,8,512]{3,2,1,0:T(8,128)S(1)} %bitcast.269), channel_id=1, replica_groups=mesh['grp'=4,'row_0'=4,'row_1'=8,'row_2'=2] {'row_2'}, dimensions={0} | all-to-all | bytes 2097152 | tf_op jit(solution)/shard_map/all_to_all | solution.py:22
  25.7 9.5 %all-to-all-start.1 = ((f32[32,8,512]{2,1,0:T(8,128)}), f32[32,8,512]{2,1,0:T(8,128)S(1)}, u32[]{:S(2)}, u32[]{:S(2)}) async-start(f32[32,8,512]{2,1,0:T(8,128)} %reduce_sum.27), calls=%async_computation.1 | async-start | bytes 1048576 | tf_op jit(solution)/shard_map/all_to_all | solution.py:30
  35.5 5.8 %cholesky.239 = f32[64,64]{1,0:T(8,128)S(1)} custom-call(f32[64,64]{1,0:T(8,128)S(1)} %fusion.58), custom_call_target="Cholesky" | custom-call | tf_op jit(solution)/shard_map/jit(cholesky)/cholesky | solution.py:74
  49.8 20.0 %all_to_all.56 = f32[64,1,512]{2,1,0:T(1,128)S(1)} all-to-all(f32[64,1,512]{2,1,0:T(1,128)S(1)} %reshape.113), channel_id=1, replica_groups=mesh['grp'=4,'row_0'=4,'row_1'=8,'row_2'=2] {'row_0','row_1','row_2'}, dimensions={0} | all-to-all | bytes 262144 | tf_op jit(solution)/shard_map/all_to_all | solution.py:36
  72.1 5.8 %cholesky.250 = f32[64,64]{1,0:T(8,128)S(1)} custom-call(f32[64,64]{1,0:T(8,128)S(1)} %fusion.56), custom_call_target="Cholesky" | custom-call | tf_op jit(solution)/shard_map/jit(cholesky)/cholesky | solution.py:74
  85.2 15.0 %all_to_all.57 = f32[64,1,512]{2,1,0:T(1,128)S(1)} all-to-all(f32[64,1,512]{2,1,0:T(1,128)S(1)} %reshape.115), channel_id=1, replica_groups=mesh['grp'=4,'row_0'=4,'row_1'=8,'row_2'=2] {'row_0','row_1','row_2'}, dimensions={0} | all-to-all | bytes 262144 | tf_op jit(solution)/shard_map/all_to_all | solution.py:36
  101.9 5.8 %cholesky.261 = f32[64,64]{1,0:T(8,128)S(1)} custom-call(f32[64,64]{1,0:T(8,128)S(1)} %fusion.54), custom_call_target="Cholesky" | custom-call | tf_op jit(solution)/shard_map/jit(cholesky)/cholesky | solution.py:74
  115.0 15.0 %all_to_all.58 = f32[64,1,512]{2,1,0:T(1,128)S(1)} all-to-all(f32[64,1,512]{2,1,0:T(1,128)S(1)} %reshape.117), channel_id=1, replica_groups=mesh['grp'=4,'row_0'=4,'row_1'=8,'row_2'=2] {'row_0','row_1','row_2'}, dimensions={0} | all-to-all | bytes 262144 | tf_op jit(solution)/shard_map/all_to_all | solution.py:36
  131.8 5.8 %cholesky.272 = f32[64,64]{1,0:T(8,128)S(1)} custom-call(f32[64,64]{1,0:T(8,128)S(1)} %fusion.52), custom_call_target="Cholesky" | custom-call | tf_op jit(solution)/shard_map/jit(cholesky)/cholesky | solution.py:74
  144.9 15.2 %all_to_all.59 = f32[64,1,512]{2,1,0:T(1,128)S(1)} all-to-all(f32[64,1,512]{2,1,0:T(1,128)S(1)} %reshape.119), channel_id=1, replica_groups=mesh['grp'=4,'row_0'=4,'row_1'=8,'row_2'=2] {'row_0','row_1','row_2'}, dimensions={0} | all-to-all | bytes 262144 | tf_op jit(solution)/shard_map/all_to_all | solution.py:36
  161.8 5.8 %cholesky.283 = f32[64,64]{1,0:T(8,128)S(1)} custom-call(f32[64,64]{1,0:T(8,128)S(1)} %fusion.50), custom_call_target="Cholesky" | custom-call | tf_op jit(solution)/shard_map/jit(cholesky)/cholesky | solution.py:74
  174.9 15.0 %all_to_all.60 = f32[64,1,512]{2,1,0:T(1,128)S(1)} all-to-all(f32[64,1,512]{2,1,0:T(1,128)S(1)} %reshape.121), channel_id=1, replica_groups=mesh['grp'=4,'row_0'=4,'row_1'=8,'row_2'=2] {'row_0','row_1','row_2'}, dimensions={0} | all-to-all | bytes 262144 | tf_op jit(solution)/shard_map/all_to_all | solution.py:36
  191.7 5.8 %cholesky.294 = f32[64,64]{1,0:T(8,128)S(1)} custom-call(f32[64,64]{1,0:T(8,128)S(1)} %fusion.48), custom_call_target="Cholesky" | custom-call | tf_op jit(solution)/shard_map/jit(cholesky)/cholesky | solution.py:74
  204.8 15.2 %all_to_all.61 = f32[64,1,512]{2,1,0:T(1,128)S(1)} all-to-all(f32[64,1,512]{2,1,0:T(1,128)S(1)} %reshape.123), channel_id=1, replica_groups=mesh['grp'=4,'row_0'=4,'row_1'=8,'row_2'=2] {'row_0','row_1','row_2'}, dimensions={0} | all-to-all | bytes 262144 | tf_op jit(solution)/shard_map/all_to_all | solution.py:36
  221.8 5.8 %cholesky.305 = f32[64,64]{1,0:T(8,128)S(1)} custom-call(f32[64,64]{1,0:T(8,128)S(1)} %fusion.46), custom_call_target="Cholesky" | custom-call | tf_op jit(solution)/shard_map/jit(cholesky)/cholesky | solution.py:74
  234.3 9.2 %convolution_bitcast_fusion = f32[3584,64]{0,1:T(8,128)S(1)} fusion(f32[512,64]{0,1:T(8,128)S(1)} %convolution_bitcast_fusion.1, f32[3584,512]{1,0:T(8,128)} %param.9), kind=kOutput, calls=%fused_computation.1 | convolution fusion | flops 1409286144 | bytes 8388608 | tf_op jit(solution)/shard_map/dot_general | solution.py:69
  244.0 46.2 %all_to_all.62 = f32[4,3584,64]{1,2,0:T(8,128)} all-to-all(f32[4,3584,64]{1,2,0:T(8,128)S(1)} %broadcast_in_dim.31), channel_id=1, replica_groups=mesh['grp'=4,'row_0'=4,'row_1'=8,'row_2'=2] {'grp'}, dimensions={0} | all-to-all | bytes 7340032 | tf_op jit(solution)/shard_map/all_to_all | solution.py:36
  295.4 7.1 %fusion = f32[64,4,256]{2,0,1:T(8,128)S(1)} fusion(f32[3584,256,1]{0,1,2:T(8,128)} %bitcast.267, f32[64,4,3584]{2,1,0:T(4,128)} %dot_general.125), kind=kOutput, calls=%fused_computation.2 | convolution fusion | flops 2818572288 | bytes 7602176 | tf_op jit(solution)/shard_map/dot_general | solution.py:69
  303.3 6.2 %all-to-all-start.9 = ((f32[64,4,256]{2,1,0:T(4,128)}), f32[64,4,256]{2,1,0:T(4,128)S(1)}, u32[]{:S(2)}, u32[]{:S(2)}) async-start(f32[64,4,256]{2,1,0:T(4,128)} %copy.110), calls=%async_computation.9 | async-start | bytes 524288 | tf_op jit(solution)/shard_map/all_to_all | solution.py:22
  309.8 5.8 %cholesky.316 = f32[64,64]{1,0:T(8,128)S(1)} custom-call(f32[64,64]{1,0:T(8,128)S(1)} %fusion.44), custom_call_target="Cholesky" | custom-call | tf_op jit(solution)/shard_map/jit(cholesky)/cholesky | solution.py:74
  322.3 6.5 %all-to-all-start.10 = ((f32[64,4,256]{2,1,0:T(4,128)}), f32[64,4,256]{2,1,0:T(4,128)S(1)}, u32[]{:S(2)}, u32[]{:S(2)}) async-start(f32[64,4,256]{2,1,0:T(4,128)} %broadcast_in_dim.32), calls=%async_computation.10 | async-start | bytes 524288 | tf_op jit(solution)/shard_map/all_to_all | solution.py:36
  341.2 5.8 %cholesky.327 = f32[64,64]{1,0:T(8,128)S(1)} custom-call(f32[64,64]{1,0:T(8,128)S(1)} %fusion.42), custom_call_target="Cholesky" | custom-call | tf_op jit(solution)/shard_map/jit(cholesky)/cholesky | solution.py:74
  354.2 5.8 %cholesky.338 = f32[64,64]{1,0:T(8,128)S(1)} custom-call(f32[64,64]{1,0:T(8,128)S(1)} %fusion.40), custom_call_target="Cholesky" | custom-call | tf_op jit(solution)/shard_map/jit(cholesky)/cholesky | solution.py:74
  367.3 5.8 %cholesky.349 = f32[64,64]{1,0:T(8,128)S(1)} custom-call(f32[64,64]{1,0:T(8,128)S(1)} %fusion.38), custom_call_target="Cholesky" | custom-call | tf_op jit(solution)/shard_map/jit(cholesky)/cholesky | solution.py:74
  380.3 5.8 %cholesky.360 = f32[64,64]{1,0:T(8,128)S(1)} custom-call(f32[64,64]{1,0:T(8,128)S(1)} %fusion.36), custom_call_target="Cholesky" | custom-call | tf_op jit(solution)/shard_map/jit(cholesky)/cholesky | solution.py:74
  393.4 5.8 %cholesky.371 = f32[64,64]{1,0:T(8,128)S(1)} custom-call(f32[64,64]{1,0:T(8,128)S(1)} %fusion.34), custom_call_target="Cholesky" | custom-call | tf_op jit(solution)/shard_map/jit(cholesky)/cholesky | solution.py:74
  406.5 5.8 %cholesky.382 = f32[64,64]{1,0:T(8,128)S(1)} custom-call(f32[64,64]{1,0:T(8,128)S(1)} %fusion.32), custom_call_target="Cholesky" | custom-call | tf_op jit(solution)/shard_map/jit(cholesky)/cholesky | solution.py:74
  419.6 5.8 %cholesky.393 = f32[64,64]{1,0:T(8,128)S(1)} custom-call(f32[64,64]{1,0:T(8,128)S(1)} %fusion.30), custom_call_target="Cholesky" | custom-call | tf_op jit(solution)/shard_map/jit(cholesky)/cholesky | solution.py:85
  437.7 13.2 %psum.21 = f32[64,128]{1,0:T(8,128)S(1)} all-reduce(f32[64,128]{1,0:T(8,128)S(1)} %fusion.112), channel_id=1, replica_groups=mesh['grp'=4,'row_0'=4,'row_1'=8,'row_2'=2] {'row_0'}, use_global_device_ids=true, to_apply=%region_5.9 | all-reduce | flops 8192 | bytes 65536 | tf_op jit(solution)/shard_map/psum | solution.py:65
  450.9 20.9 %psum.22 = f32[64,128]{1,0:T(8,128)S(1)} all-reduce(f32[64,128]{1,0:T(8,128)S(1)} %psum.21), channel_id=1, replica_groups=mesh['grp'=4,'row_0'=4,'row_1'=8,'row_2'=2] {'row_1'}, use_global_device_ids=true, to_apply=%region_6.10 | all-reduce | flops 8192 | bytes 65536 | tf_op jit(solution)/shard_map/psum | solution.py:65
  471.8 14.1 %psum.23 = f32[64,128]{1,0:T(8,128)S(1)} all-reduce(f32[64,128]{1,0:T(8,128)S(1)} %psum.22), channel_id=1, replica_groups=mesh['grp'=4,'row_0'=4,'row_1'=8,'row_2'=2] {'row_2'}, use_global_device_ids=true, to_apply=%region_7.11 | all-reduce | flops 8192 | bytes 65536 | tf_op jit(solution)/shard_map/psum | solution.py:65
  (180 shorter events, 148.6 us)
Async XLA Ops:
  0.0 436.4 %copy-start = (f32[3584,128]{1,0:T(8,128)S(1)}, f32[3584,128]{1,0:T(8,128)}, u32[]{:S(2)}) copy-start(f32[3584,128]{1,0:T(8,128)} %param.10) | copy-start | bytes 5505028
  17.3 17.9 %copy-start.1 = (f32[512,64]{0,1:T(8,128)S(1)}, f32[512,64]{0,1:T(8,128)}, u32[]{:S(2)}) copy-start(f32[512,64]{0,1:T(8,128)} %param.11) | copy-start | bytes 393220
  25.7 23.7 %all-to-all-start.1 = ((f32[32,8,512]{2,1,0:T(8,128)}), f32[32,8,512]{2,1,0:T(8,128)S(1)}, u32[]{:S(2)}, u32[]{:S(2)}) async-start(f32[32,8,512]{2,1,0:T(8,128)} %reduce_sum.27), calls=%async_computation.1 | async-start | bytes 1048576 | tf_op jit(solution)/shard_map/all_to_all | solution.py:30
  295.4 14.1 %copy-start.2 = (f32[256,64]{0,1:T(8,128)S(1)}, f32[256,64]{0,1:T(8,128)}, u32[]{:S(2)}) copy-start(f32[256,64]{0,1:T(8,128)} %param.12) | copy-start | bytes 196612
  303.3 18.1 %all-to-all-start.9 = ((f32[64,4,256]{2,1,0:T(4,128)}), f32[64,4,256]{2,1,0:T(4,128)S(1)}, u32[]{:S(2)}, u32[]{:S(2)}) async-start(f32[64,4,256]{2,1,0:T(4,128)} %copy.110), calls=%async_computation.9 | async-start | bytes 524288 | tf_op jit(solution)/shard_map/all_to_all | solution.py:22
  322.3 18.0 %all-to-all-start.10 = ((f32[64,4,256]{2,1,0:T(4,128)}), f32[64,4,256]{2,1,0:T(4,128)S(1)}, u32[]{:S(2)}, u32[]{:S(2)}) async-start(f32[64,4,256]{2,1,0:T(4,128)} %broadcast_in_dim.32), calls=%async_computation.10 | async-start | bytes 524288 | tf_op jit(solution)/shard_map/all_to_all | solution.py:36
where the time goes:
time: 499 us; the launch traced here: 490 us
  blocking collectives  197 us (39%)
  other arithmetic  189 us (38%)
  matrix products  57.8 us (12%)
  starting transfers between devices  22.2 us (4%)
  waiting for transfers between devices  12.2 us (2%)
  local copies, waits for them, and re-layouts  11.1 us (2%)
    all_to_all x7, blocking collectives, sent_to_all(): return lax.all_to_all(copies, axis, split_axis=0, concat_axis=0, tiled=True)  142 us
    another operation x42, other arithmetic, orthonormal(): lower_factor = jnp.linalg.cholesky(small_gram)  91.8 us
    another operation x28, other arithmetic, orthonormal(): lax.linalg.triangular_solve(lower_factor, tall_block, left_side=False, lo...  78 us
    dot_general x34, matrix products, highdot(): jnp.dot(left, right, precision=lax.Precision.HIGHEST, preferred_element_t...  52.6 us
    psum x3, blocking collectives, by_axis(): return functools.reduce(lax.psum, axes, array)  48.2 us
  transfers between devices with their start and end apart: 3, of which 3 were waited for; matrix products, arithmetic and copies ran while one was open for 5% of the time, Pallas kernels for 0%

commit v1 on v0

v1 whole, which is shorter than its diff:
```python
import jax
import jax.numpy as jnp
from jax import lax
from jax.experimental import pallas as pl
from jax.experimental.pallas import tpu as pltpu
from jax.sharding import Mesh
from jax.sharding import PartitionSpec as P

ITERS = 6
ROW = ("row_0", "row_1", "row_2")
CHIPS = ("row_0", "row_1")
CORE = "row_2"
BLOCK = 128
VMEM = pl.BlockSpec(memory_space=pltpu.VMEM)
SMEM = pl.BlockSpec(memory_space=pltpu.SMEM)

NT = (((1,), (1,)), ((), ()))
NN = (((1,), (0,)), ((), ()))
TN = (((0,), (0,)), ((), ()))


def dot(left, right, dims):
    return lax.dot_general(left, right, dims, preferred_element_type=jnp.float32)


def parts(x, count):
    found = []
    for _ in range(count - 1):
        piece = x.astype(jnp.bfloat16)
        found.append(piece)
        x = x - piece.astype(jnp.float32)
    found.append(x.astype(jnp.bfloat16))
    return found


def dot_parts(left, right, dims):
    count = len(left)
    rows = left[0].shape[0]
    total = None
    for j in reversed(range(count)):
        stack = jnp.concatenate(left[: count - j], axis=0) if j < count - 1 else left[0]
        product = dot(stack, right[j], dims)
        for i in reversed(range(count - j)):
            piece = product[i * rows : (i + 1) * rows]
            total = piece if total is None else total + piece
    return total


def lower_inverse(matrix):
    size = matrix.shape[0]
    bands = size // 8
    sub = lax.broadcasted_iota(jnp.int32, (8, 2 * size), 0)
    lane = lax.broadcasted_iota(jnp.int32, (8, 2 * size), 1)
    wide = jnp.concatenate([matrix, jnp.zeros_like(matrix)], axis=1)
    work = [
        jnp.where(lane == size + 8 * b + sub, 1.0, wide[8 * b : 8 * b + 8]) for b in range(bands)
    ]

    def column(value, j):
        return jnp.broadcast_to(value[:, j : j + 1], value.shape)

    def line(value, j):
        return jnp.broadcast_to(value[j : j + 1, :], value.shape)

    for b in range(bands):
        cols = {i: [column(work[i], 8 * b + j) for j in range(8)] for i in range(b, bands)}
        scale = None
        for j in range(8):
            pivot = line(cols[b][j], j)
            inverse = 1.0 / pivot
            root = lax.rsqrt(pivot)
            scale = root if scale is None else jnp.where(sub == j, root, scale)
            factor = jnp.where(sub > j, cols[b][j] * inverse, 0.0)
            ahead = {k: line(cols[b][k], j) for k in range(j + 1, 8)}
            pivot_row = line(work[b], j)
            for k in range(j + 1, 8):
                cols[b][k] = cols[b][k] - factor * ahead[k]
            work[b] = work[b] - factor * pivot_row
            for i in range(b + 1, bands):
                below = cols[i][j] * inverse
                for k in range(j + 1, 8):
                    cols[i][k] = cols[i][k] - below * ahead[k]
                work[i] = work[i] - below * pivot_row
        work[b] = work[b] * scale
    return jnp.concatenate(work, axis=0)[:, size:]


def orthonormal(rows):
    split = parts(rows, 3)
    return dot_parts(parts(lower_inverse(dot_parts(split, split, NT)), 3), split, NN)


def upper_pairs(count):
    return [(a, b) for a in range(count) for b in range(a, count)]


def cut(index):
    return slice(index * BLOCK, (index + 1) * BLOCK)


def gram_kernel(core_ref, x_ref, o_ref, held_ref, arrived, *sum_refs):
    steps, deep, width = held_ref.shape
    half = width // 2
    copies = [
        pltpu.make_async_copy(
            x_ref.at[pl.ds(n * deep, deep), :], held_ref.at[n], arrived.at[n]
        )
        for n in range(steps)
    ]
    for copy in copies:
        copy.start()
    left, right = slice(None, half), slice(half, None)
    for n, copy in enumerate(copies):
        copy.wait()
        high, low = parts(held_ref[n], 2)
        high_t, low_t = high.T, low.T
        found = [
            dot(high_t[left], high[:, left], NN) + dot(low_t[left], low[:, left], NN),
            dot(high_t[left], high[:, right], NN) + dot(low_t[left], low[:, right], NN),
            dot(high_t[right], high[:, right], NN) + dot(low_t[right], low[:, right], NN),
            dot(high_t[left], low[:, left], NN),
            dot(high_t[left], low[:, right], NN),
            dot(high_t[right], low[:, left], NN),
            dot(high_t[right], low[:, right], NN),
        ]
        for ref, value in zip(sum_refs, found):
            ref[...] = value if n == 0 else ref[...] + value
    aa, ab, bb, ll, lr, rl, rr = [ref[...] for ref in sum_refs]
    place = {(0, 0): aa + ll + ll.T, (0, 1): ab + lr + rl.T, (1, 1): bb + rr + rr.T}
    pairs = upper_pairs(width // BLOCK)
    held = len(pairs) // 2
    for n, (a, b) in enumerate(pairs):
        block = place[a // 2, b // 2][cut(a % 2), cut(b % 2)]
        o_ref[(n // held) ^ core_ref[0], cut(n % held), :] = block


def gram(snapshots, core):
    rows, width = snapshots.shape
    steps = 4
    held = len(upper_pairs(width // BLOCK)) // 2 * BLOCK
    return pl.pallas_call(
        gram_kernel,
        in_specs=[SMEM, pl.BlockSpec(memory_space=pl.ANY)],
        out_specs=VMEM,
        out_shape=jax.ShapeDtypeStruct((2, held, BLOCK), jnp.float32),
        scratch_shapes=[
            pltpu.VMEM((steps, rows // steps, width), jnp.float32),
            pltpu.SemaphoreType.DMA((steps,)),
        ]
        + [pltpu.VMEM((width // 2, width // 2), jnp.float32)] * 7,
        compiler_params=pltpu.CompilerParams(vmem_limit_bytes=48 * 2**20),
        name="gram",
    )(core, snapshots)


def in_order(core_ref, mine_ref, other_ref):
    first = core_ref[0] == 0
    mine, other = mine_ref[...], other_ref[...]
    return jnp.where(first, mine, other), jnp.where(first, other, mine)


def sweep(basis_ref, next_ref, gram_refs, last):
    basis = orthonormal(next_ref[...])
    basis_ref[...] = basis

    @pl.when(jnp.logical_not(last))
    def _():
        next_ref[...] = dot_parts(parts(basis, 3), [r[...] for r in gram_refs], NN)


def solve_kernel(row_total, core_ref, mine_ref, other_ref, start_ref, o_ref, next_ref, *gram_refs):
    width = gram_refs[0].shape[0]
    pairs = upper_pairs(width // BLOCK)
    held = len(pairs) // 2
    halves = in_order(core_ref, mine_ref, other_ref)
    for n, (a, b) in enumerate(pairs):
        block = halves[n // held][cut(n % held)] / row_total
        for ref, piece in zip(gram_refs, parts(block, 3)):
            ref[cut(a), cut(b)] = piece
        if a != b:
            for ref, piece in zip(gram_refs, parts(block.T, 3)):
                ref[cut(b), cut(a)] = piece
    next_ref[...] = start_ref[...].T

    def step(index, carry):
        sweep(o_ref, next_ref, gram_refs, index == ITERS)
        return carry

    lax.fori_loop(0, ITERS + 1, step, 0)


def group_solve(core, mine, other, start, row_total):
    width, rank = start.shape
    return pl.pallas_call(
        lambda *refs: solve_kernel(row_total, *refs),
        in_specs=[SMEM, VMEM, VMEM, VMEM],
        out_specs=VMEM,
        out_shape=jax.ShapeDtypeStruct((rank, width), jnp.float32),
        scratch_shapes=[pltpu.VMEM((rank, width), jnp.float32)]
        + [pltpu.VMEM((width, width), jnp.bfloat16)] * 3,
        compiler_params=pltpu.CompilerParams(vmem_limit_bytes=32 * 2**20),
        name="group_solve",
    )(core, mine, other, start)


def basis_kernel(q_ref, x_ref, o_ref):
    o_ref[...] = dot_parts(parts(q_ref[...], 2), parts(x_ref[...], 2), NT)


def group_basis(basis, snapshots):
    rank, width = basis.shape
    rows = snapshots.shape[0]
    step = rows // 4
    return pl.pallas_call(
        basis_kernel,
        grid=(rows // step,),
        in_specs=[
            pl.BlockSpec((rank, width), lambda i: (0, 0)),
            pl.BlockSpec((step, width), lambda i: (i, 0)),
        ],
        out_specs=pl.BlockSpec((rank, step), lambda i: (0, i)),
        out_shape=jax.ShapeDtypeStruct((rank, rows), jnp.float32),
        compiler_params=pltpu.CompilerParams(
            dimension_semantics=("arbitrary",), vmem_limit_bytes=48 * 2**20
        ),
        name="group_basis",
    )(basis, snapshots)


def merge_kernel(core_ref, joined_ref, test_ref, o_ref, gram_ref, side_ref):
    step = pl.program_id(0)

    @pl.when(step == 0)
    def _():
        gram_ref[...] = jnp.zeros_like(gram_ref)
        side_ref[...] = jnp.zeros_like(side_ref)

    left = parts(joined_ref[...], 2)
    gram_ref[...] += dot_parts(left, left, NT)
    side_ref[...] += dot_parts(left, parts(test_ref[...], 2), NN)

    @pl.when(step == pl.num_programs(0) - 1)
    def _():
        blocks = [gram_ref[cut(a), cut(b)] for a, b in upper_pairs(2)]
        blocks += [side_ref[cut(a), :] for a in range(2)]
        pieces = [block[i * 64 : (i + 1) * 64] for block in blocks for i in range(2)]
        for n, piece in enumerate(pieces):
            o_ref[(n // 5) ^ core_ref[0], (n % 5) * 64 : (n % 5 + 1) * 64, :] = piece


def merge_partials(core, joined, test_block):
    wide, rows = joined.shape
    step = rows // 4
    return pl.pallas_call(
        merge_kernel,
        grid=(rows // step,),
        in_specs=[
            SMEM,
            pl.BlockSpec((wide, step), lambda i: (0, i)),
            pl.BlockSpec((step, BLOCK), lambda i: (i, 0)),
        ],
        out_specs=pl.BlockSpec((2, 320, BLOCK), lambda i: (0, 0, 0)),
        out_shape=jax.ShapeDtypeStruct((2, 320, BLOCK), jnp.float32),
        scratch_shapes=[
            pltpu.VMEM((wide, wide), jnp.float32),
            pltpu.VMEM((wide, BLOCK), jnp.float32),
        ],
        compiler_params=pltpu.CompilerParams(
            dimension_semantics=("arbitrary",), vmem_limit_bytes=48 * 2**20
        ),
        name="merge_partials",
    )(core, joined, test_block)


def finish_kernel(
    row_total, core_ref, mine_ref, other_ref, start_ref, joined_ref, o_ref,
    next_ref, coef_ref, weight_ref, *gram_refs
):
    step_index = pl.program_id(0)

    @pl.when(step_index == 0)
    def _():
        halves = in_order(core_ref, mine_ref, other_ref)
        pieces = [halves[n // 5][(n % 5) * 64 : (n % 5 + 1) * 64] for n in range(10)]
        blocks = [jnp.concatenate(pieces[2 * n : 2 * n + 2], axis=0) for n in range(5)]
        for (a, b), block in zip(upper_pairs(2), blocks[:3]):
            block = block / row_total
            for ref, piece in zip(gram_refs, parts(block, 3)):
                ref[cut(a), cut(b)] = piece
            if a != b:
                for ref, piece in zip(gram_refs, parts(block.T, 3)):
                    ref[cut(b), cut(a)] = piece
        next_ref[...] = start_ref[...].T

        def step(index, carry):
            sweep(coef_ref, next_ref, gram_refs, index > ITERS)
            return carry

        lax.fori_loop(0, ITERS + 1, step, 0)
        coef = parts(coef_ref[...], 3)
        energy = dot_parts(parts(next_ref[...], 3), coef, NT)
        coef = dot_parts(parts(lower_inverse(energy), 3), coef, NN)
        coef_parts = parts(coef, 3)
        side = jnp.concatenate(blocks[3:], axis=0)
        test_coeffs = dot_parts(coef_parts, parts(side, 3), NN)
        weight_ref[...] = dot_parts(parts(coef.T, 3), parts(test_coeffs, 3), NN) / row_total

    o_ref[...] = dot_parts(parts(joined_ref[...].T, 2), parts(weight_ref[...], 2), NN)


def finish(core, mine, other, start, joined, row_total):
    wide, rows = joined.shape
    rank = start.shape[1]
    step = rows // 4
    return pl.pallas_call(
        lambda *refs: finish_kernel(row_total, *refs),
        grid=(rows // step,),
        in_specs=[SMEM, VMEM, VMEM, VMEM, pl.BlockSpec((wide, step), lambda i: (0, i))],
        out_specs=pl.BlockSpec((step, BLOCK), lambda i: (i, 0)),
        out_shape=jax.ShapeDtypeStruct((rows, BLOCK), jnp.float32),
        scratch_shapes=[
            pltpu.VMEM((rank, wide), jnp.float32),
            pltpu.VMEM((rank, wide), jnp.float32),
            pltpu.VMEM((wide, BLOCK), jnp.float32),
        ]
        + [pltpu.VMEM((wide, wide), jnp.bfloat16)] * 3,
        compiler_params=pltpu.CompilerParams(
            dimension_semantics=("arbitrary",), vmem_limit_bytes=48 * 2**20
        ),
        name="finish",
    )(core, mine, other, start, joined)


def swap_cores(array):
    return lax.ppermute(array, CORE, [(0, 1), (1, 0)])


def sum_over_rows(halves):
    kept = halves[0] + swap_cores(halves[1])
    chips = lax.axis_size(CHIPS)
    cuts = kept.reshape(chips, kept.shape[0] // chips, BLOCK)
    own = jnp.sum(lax.all_to_all(cuts, CHIPS, 0, 0, tiled=True), axis=0)
    copies = jnp.broadcast_to(own, (chips, *own.shape))
    mine = lax.all_to_all(copies, CHIPS, 0, 0, tiled=True).reshape(kept.shape)
    return mine, swap_cores(mine)


def on_device(snapshots, test_block, start_block, start_merge):
    row_total = snapshots.shape[0] * lax.axis_size(ROW)
    core = lax.axis_index(CORE).reshape(1)
    mine, other = sum_over_rows(gram(snapshots, core))
    basis = group_solve(core, mine, other, start_block, row_total)
    own = group_basis(basis, snapshots)
    joined = lax.all_gather(own, "grp", axis=0, tiled=True)
    mine, other = sum_over_rows(merge_partials(core, joined, test_block))
    return finish(core, mine, other, start_merge, joined, row_total)


def solution(mesh):
    finer = Mesh(
        mesh.devices.reshape(mesh.shape["grp"], 4, 8, 2), ("grp", "row_0", "row_1", "row_2")
    )
    placed = (P(ROW, "grp"), P(ROW, "grp"), P("grp", None), P())
    return jax.shard_map(
        on_device, mesh=finer, in_specs=placed, out_specs=P(ROW, "grp"), check_vma=False
    )
```

time: 499 us -> 214 us (0.43); the launches traced: 490 us -> 214 us
  other arithmetic: 189 us -> 0.13 us
  blocking collectives: 197 us -> 74.6 us
  Pallas kernels: 0 us -> 61.4 us
  matrix products: 57.8 us -> 0 us
  waiting for transfers between devices: 12.2 us -> 47 us
  between operations: 1.05 us -> 13.5 us
  starting transfers between devices: 22.2 us -> 12.6 us
  local copies, waits for them, and re-layouts: 11.1 us -> 4.48 us
    another operation x75 -> x0, other arithmetic: 182 us -> none  [the longest x42 91.8 us: orthonormal(): lower_factor = jnp.linalg.cholesky(small_gram)]
    all_to_all x8 -> x4, blocking collectives: 149 us -> 74.6 us  [the longest x2 40.2 us: sum_over_rows(): own = jnp.sum(lax.all_to_all(cuts, CHIPS, 0, 0, tiled=True), axis=0)]
    pallas_call x0 -> x5, Pallas kernels: none -> 61.4 us  [the longest x1 23.4 us: finish(): pl.pallas_call(lambda *refs: finish_kernel(row_total, *refs), grid=(rows...]
    dot_general x34 -> x0, matrix products: 52.6 us -> none  [highdot(): jnp.dot(left, right, precision=lax.Precision.HIGHEST, preferred_element_t...]
    psum x3 -> x0, blocking collectives: 48.2 us -> none  [by_axis(): return functools.reduce(lax.psum, axes, array)]
    all_gather x0 -> x1, waiting for transfers between devices: none -> 42.7 us  [on_device(): joined = lax.all_gather(own, 'grp', axis=0, tiled=True)]
    all_to_all x3 -> x0, starting transfers between devices: 22.2 us -> none  [the longest x1 9.5 us: sum_in_two_steps(): lax.all_to_all(nearer, far, split_axis=0, concat_axis=0, tiled=True)]
    ppermute x0 -> x4, starting transfers between devices: none -> 12.6 us  [swap_cores(): return lax.ppermute(array, CORE, [(0, 1), (1, 0)])]
  transfers between devices with their start and end apart: 3 -> 5, of which waited for: 3 -> 5; matrix products, arithmetic and copies ran while one was open for 5% -> 0% of each run, Pallas kernels for 0% -> 0%
where the time goes in v1:
time: 214 us
  blocking collectives  74.6 us (35%)
  Pallas kernels  61.4 us (29%)
  waiting for transfers between devices  47 us (22%)
  between operations  13.5 us (6%)
  starting transfers between devices  12.6 us (6%)
  local copies, waits for them, and re-layouts  4.48 us (2%)
    all_gather x1, waiting for transfers between devices, on_device(): joined = lax.all_gather(own, 'grp', axis=0, tiled=True)  42.7 us
    all_to_all x2, blocking collectives, sum_over_rows(): own = jnp.sum(lax.all_to_all(cuts, CHIPS, 0, 0, tiled=True), axis=0)  40.2 us
    all_to_all x2, blocking collectives, sum_over_rows(): mine = lax.all_to_all(copies, CHIPS, 0, 0, tiled=True).reshape(kept.shape)  34.5 us
    pallas_call x1, Pallas kernels, finish(): pl.pallas_call(lambda *refs: finish_kernel(row_total, *refs), grid=(rows...  23.4 us
    pallas_call x1, Pallas kernels, group_solve(): pl.pallas_call(lambda *refs: solve_kernel(row_total, *refs), in_specs=[SM...  20.1 us
    ppermute x4, starting transfers between devices, swap_cores(): return lax.ppermute(array, CORE, [(0, 1), (1, 0)])  12.6 us
    pallas_call x1, Pallas kernels, gram(): pl.pallas_call(gram_kernel, in_specs=[SMEM, pl.BlockSpec(memory_space=pl....  7.64 us
    pallas_call x1, Pallas kernels, group_basis(): pl.pallas_call(basis_kernel, grid=(rows // step,), in_specs=[pl.BlockSpec...  6.11 us
  transfers between devices with their start and end apart: 5, of which 5 were waited for; matrix products, arithmetic and copies ran while one was open for 0% of the time, Pallas kernels for 0%

profile of v1, /device:TPU:1, one launch (start us, length us, event | category | flops | bytes accessed | tf_op | source)
XLA Modules:
  0.0 213.7 jit_solution(12934779499339761259)
XLA Ops:
  6.5 0.0 all-gather.2.cloned.1.call-start
  6.5 7.6 %gram.1 = f32[2,640,128]{2,1,0:T(8,128)S(1)} custom-call(s32[1]{0:T(128)} %bitcast.core_ref.refs_0_, f32[3584,512]{1,0:T(8,128)} %x_ref.3), custom_call_target="tpu_custom_call" | custom-call | tf_op jit(solution)/shard_map/gram/pallas_call | solution.py:141
  14.2 0.0 copy-start.3
  14.2 3.3 %collective-permute-start = (f32[640,128]{1,0:T(8,128)S(1)}, f32[640,128]{1,0:T(8,128)S(1)}, u32[]{:S(2)}, u32[]{:S(2)}) collective-permute-start(f32[640,128]{1,0:T(8,128)S(1)} %slice_bitcast_fusion), channel_id=1, source_target_pairs={{0,1},{1,0},{2,3},{3,2},{4,5},{5,4},{6,7},{7,6},{8,9},{9,8},{10,11... | collective-permute-start | bytes 983048 | tf_op jit(solution)/shard_map/ppermute | solution.py:335
  17.5 1.3 collective-permute-done
  18.8 21.1 %all_to_all.20 = f32[32,20,128]{2,1,0:T(8,128)S(1)} all-to-all(f32[32,20,128]{2,1,0:T(8,128)S(1)} %reshape.16), channel_id=1, replica_groups=mesh['grp'=4,'row_0'=4,'row_1'=8,'row_2'=2] {'row_0','row_1'}, dimensions={0} | all-to-all | bytes 655360 | tf_op jit(solution)/shard_map/all_to_all | solution.py:342
  40.0 18.3 %all_to_all.21 = f32[32,20,128]{2,1,0:T(8,128)S(1)} all-to-all(f32[32,20,128]{2,1,0:T(8,128)S(1)} %broadcast_in_dim.6), channel_id=1, replica_groups=mesh['grp'=4,'row_0'=4,'row_1'=8,'row_2'=2] {'row_0','row_1'}, dimensions={0} | all-to-all | bytes 655360 | tf_op jit(solution)/shard_map/all_to_all | solution.py:344
  58.4 4.6 %collective-permute-start.1 = (f32[640,128]{1,0:T(8,128)S(1)}, f32[640,128]{1,0:T(8,128)S(1)}, u32[]{:S(2)}, u32[]{:S(2)}) collective-permute-start(f32[640,128]{1,0:T(8,128)S(1)} %reshape.17.refs_1_), channel_id=1, source_target_pairs={{0,1},{1,0},{2,3},{3,2},{4,5},{5,4},{6,7},{7,6},{8,9},{9,8},{10,11... | collective-permute-start | bytes 983048 | tf_op jit(solution)/shard_map/ppermute | solution.py:335
  63.0 0.0 copy-done.3
  63.0 0.1 copy.7.refs_3_
  63.1 1.1 collective-permute-done.1.refs_2_
  64.2 20.1 %group_solve.1.q_ref = f32[64,512]{1,0:T(8,128)S(1)} custom-call(s32[1]{0:T(128)} %bitcast.core_ref.refs_0_, f32[640,128]{1,0:T(8,128)S(1)} %reshape.17.refs_1_, f32[640,128]{1,0:T(8,128)S(1)} %collective-permute-done.1.refs_2_, f32[512,64]{1,0:T(8,128)S(1)} %copy.7.refs_3_), custom_call_target="tpu_custom_call" | custom-call | tf_op jit(solution)/shard_map/group_solve/pallas_call | solution.py:194
  84.3 0.0 copy-start.2
  84.3 6.1 %group_basis.1 = f32[64,3584]{1,0:T(8,128)} custom-call(f32[64,512]{1,0:T(8,128)S(1)} %group_solve.1.q_ref, f32[3584,512]{1,0:T(8,128)} %x_ref.3), custom_call_target="tpu_custom_call" | custom-call | tf_op jit(solution)/shard_map/group_basis/pallas_call | solution.py:214
  90.4 0.0 all-gather.2.cloned.1.call-update
  90.5 42.7 %all-gather.2.cloned.1.call-done.joined_ref.refs_4_ = f32[256,3584]{1,0:T(8,128)} async-done(((f32[64,3584]{1,0:T(8,128)}), f32[256,3584]{1,0:T(8,128)}) %all-gather.2.cloned.1.call-update) | async-done | bytes 3670032 | tf_op jit(solution)/shard_map/all_gather | solution.py:354
  133.2 0.0 copy-done.2
  133.2 0.0 copy-start
  133.2 2.0 copy-done
  135.2 0.0 copy-start.4
  135.2 4.1 %merge_partials.1 = f32[2,320,128]{2,1,0:T(8,128)S(1)} custom-call(s32[1]{0:T(128)} %bitcast.core_ref.refs_0_, f32[256,3584]{1,0:T(8,128)S(1)} %copy-done, f32[3584,128]{1,0:T(8,128)S(1)} %copy-done.2), custom_call_target="tpu_custom_call" | custom-call | tf_op jit(solution)/shard_map/merge_partials/pallas_call | solution.py:254
  139.4 0.9 collective-permute-start.2
  140.3 1.0 collective-permute-done.2
  141.4 19.0 %all_to_all.22 = f32[32,10,128]{2,1,0:T(8,128)S(1)} all-to-all(f32[32,10,128]{2,1,0:T(8,128)S(1)} %reshape.18), channel_id=1, replica_groups=mesh['grp'=4,'row_0'=4,'row_1'=8,'row_2'=2] {'row_0','row_1'}, dimensions={0} | all-to-all | bytes 327680 | tf_op jit(solution)/shard_map/all_to_all | solution.py:342
  160.5 16.2 %all_to_all.23 = f32[32,10,128]{2,1,0:T(8,128)S(1)} all-to-all(f32[32,10,128]{2,1,0:T(8,128)S(1)} %broadcast_in_dim.7), channel_id=1, replica_groups=mesh['grp'=4,'row_0'=4,'row_1'=8,'row_2'=2] {'row_0','row_1'}, dimensions={0} | all-to-all | bytes 327680 | tf_op jit(solution)/shard_map/all_to_all | solution.py:344
  176.7 3.7 %collective-permute-start.3 = (f32[320,128]{1,0:T(8,128)S(1)}, f32[320,128]{1,0:T(8,128)S(1)}, u32[]{:S(2)}, u32[]{:S(2)}) collective-permute-start(f32[320,128]{1,0:T(8,128)S(1)} %reshape.19.refs_1_), channel_id=1, source_target_pairs={{0,1},{1,0},{2,3},{3,2},{4,5},{5,4},{6,7},{7,6},{8,9},{9,8},{10,11... | collective-permute-start | bytes 491528 | tf_op jit(solution)/shard_map/ppermute | solution.py:335
  180.4 0.0 copy-done.4
  180.4 0.1 copy.8.refs_3_
  180.5 0.9 collective-permute-done.3.refs_2_
  181.4 0.0 copy-start.1
  181.4 2.0 copy-done.1
  183.5 23.4 %finish.1 = f32[3584,128]{1,0:T(8,128)} custom-call(s32[1]{0:T(128)} %bitcast.core_ref.refs_0_, f32[320,128]{1,0:T(8,128)S(1)} %reshape.19.refs_1_, f32[320,128]{1,0:T(8,128)S(1)} %collective-permute-done.3.refs_2_, f32[256,64]{1,0:T(8,128)S(1)} %copy.8.refs_3_, f32[256,3584]{1,0:T(8,128)S(1)} %copy-done.1), custom_call_target="tpu_custom_call" | custom-call | tf_op jit(solution)/shard_map/finish/pallas_call | solution.py:315
  (12 shorter events, 0.3 us)
Async XLA Ops:
  6.5 126.6 %all-gather.2.cloned.1.call-start = ((), (), s32[]{:S(2)}) async-start(), calls=%async_computation.4 | async-start | bytes 4587520 | tf_op jit(solution)/shard_map/all_gather | solution.py:354
  14.2 48.8 %copy-start.3 = (f32[512,64]{0,1:T(8,128)S(1)}, f32[512,64]{0,1:T(8,128)}, u32[]{:S(2)}) copy-start(f32[512,64]{0,1:T(8,128)} %param.6) | copy-start | bytes 393220
  14.2 4.5 %collective-permute-start = (f32[640,128]{1,0:T(8,128)S(1)}, f32[640,128]{1,0:T(8,128)S(1)}, u32[]{:S(2)}, u32[]{:S(2)}) collective-permute-start(f32[640,128]{1,0:T(8,128)S(1)} %slice_bitcast_fusion), channel_id=1, source_target_pairs={{0,1},{1,0},{2,3},{3,2},{4,5},{5,4},{6,7},{7,6},{8,9},{9,8},{10,11... | collective-permute-start | bytes 983048 | tf_op jit(solution)/shard_map/ppermute | solution.py:335
  58.4 5.9 %collective-permute-start.1 = (f32[640,128]{1,0:T(8,128)S(1)}, f32[640,128]{1,0:T(8,128)S(1)}, u32[]{:S(2)}, u32[]{:S(2)}) collective-permute-start(f32[640,128]{1,0:T(8,128)S(1)} %reshape.17.refs_1_), channel_id=1, source_target_pairs={{0,1},{1,0},{2,3},{3,2},{4,5},{5,4},{6,7},{7,6},{8,9},{9,8},{10,11... | collective-permute-start | bytes 983048 | tf_op jit(solution)/shard_map/ppermute | solution.py:335
  84.3 48.8 %copy-start.2 = (f32[3584,128]{1,0:T(8,128)S(1)}, f32[3584,128]{1,0:T(8,128)}, u32[]{:S(2)}) copy-start(f32[3584,128]{1,0:T(8,128)} %test_ref.1) | copy-start | bytes 5505028
  133.2 2.0 copy-start
  135.2 45.2 %copy-start.4 = (f32[256,64]{0,1:T(8,128)S(1)}, f32[256,64]{0,1:T(8,128)}, u32[]{:S(2)}) copy-start(f32[256,64]{0,1:T(8,128)} %param.7) | copy-start | bytes 196612
  139.4 2.0 collective-permute-start.2
  176.7 4.8 %collective-permute-start.3 = (f32[320,128]{1,0:T(8,128)S(1)}, f32[320,128]{1,0:T(8,128)S(1)}, u32[]{:S(2)}, u32[]{:S(2)}) collective-permute-start(f32[320,128]{1,0:T(8,128)S(1)} %reshape.19.refs_1_), channel_id=1, source_target_pairs={{0,1},{1,0},{2,3},{3,2},{4,5},{5,4},{6,7},{7,6},{8,9},{9,8},{10,11... | collective-permute-start | bytes 491528 | tf_op jit(solution)/shard_map/ppermute | solution.py:335
  181.4 2.0 copy-start.1
Sparse Core Ops, SparseCore 0:
  90.6 42.5 all-gather.1

commit v2 on v1

--- a/solution.py
+++ b/solution.py
@@ -57,7 +57,8 @@
     ]
 
     def column(value, j):
-        return jnp.broadcast_to(value[:, j : j + 1], value.shape)
+        place = jnp.full(value.shape, j, jnp.int32)
+        return jnp.take_along_axis(value, place, axis=1, mode="promise_in_bounds")
 
     def line(value, j):
         return jnp.broadcast_to(value[j : j + 1, :], value.shape)
@@ -67,8 +68,8 @@
         scale = None
         for j in range(8):
             pivot = line(cols[b][j], j)
-            inverse = 1.0 / pivot
             root = lax.rsqrt(pivot)
+            inverse = root * root
             scale = root if scale is None else jnp.where(sub == j, root, scale)
             factor = jnp.where(sub > j, cols[b][j] * inverse, 0.0)
             ahead = {k: line(cols[b][k], j) for k in range(j + 1, 8)}
@@ -159,13 +160,14 @@
     return jnp.where(first, mine, other), jnp.where(first, other, mine)
 
 
-def sweep(basis_ref, next_ref, gram_refs, last):
-    basis = orthonormal(next_ref[...])
-    basis_ref[...] = basis
-
-    @pl.when(jnp.logical_not(last))
-    def _():
-        next_ref[...] = dot_parts(parts(basis, 3), [r[...] for r in gram_refs], NN)
+def sweep(rows, gram_refs):
+    split = parts(rows, 3)
+    ahead = dot_parts(split, [ref[...] for ref in gram_refs], NN)
+    return lower_inverse(dot_parts(split, split, NT)), ahead
+
+
+def normalised(inverse, rows):
+    return dot_parts(parts(inverse, 3), parts(rows, 3), NN)
 
 
 def solve_kernel(row_total, core_ref, mine_ref, other_ref, start_ref, o_ref, next_ref, *gram_refs):
@@ -183,10 +185,11 @@
     next_ref[...] = start_ref[...].T
 
     def step(index, carry):
-        sweep(o_ref, next_ref, gram_refs, index == ITERS)
+        next_ref[...] = normalised(*sweep(next_ref[...], gram_refs))
         return carry
 
-    lax.fori_loop(0, ITERS + 1, step, 0)
+    lax.fori_loop(0, ITERS, step, 0)
+    o_ref[...] = orthonormal(next_ref[...])
 
 
 def group_solve(core, mine, other, start, row_total):
@@ -203,23 +206,38 @@
     )(core, mine, other, start)
 
 
-def basis_kernel(q_ref, x_ref, o_ref):
-    o_ref[...] = dot_parts(parts(q_ref[...], 2), parts(x_ref[...], 2), NT)
+def basis_kernel(q_ref, x_ref, near_ref, far_ref):
+    step = pl.program_id(0)
+    half = pl.num_programs(0) // 2
+    found = dot_parts(parts(q_ref[...], 2), parts(x_ref[...], 2), NT)
+
+    @pl.when(step < half)
+    def _():
+        near_ref[...] = found
+
+    @pl.when(step >= half)
+    def _():
+        far_ref[...] = found
 
 
 def group_basis(basis, snapshots):
     rank, width = basis.shape
     rows = snapshots.shape[0]
-    step = rows // 4
+    steps = 4
+    deep = rows // steps
+    half = steps // 2
     return pl.pallas_call(
         basis_kernel,
-        grid=(rows // step,),
+        grid=(steps,),
         in_specs=[
             pl.BlockSpec((rank, width), lambda i: (0, 0)),
-            pl.BlockSpec((step, width), lambda i: (i, 0)),
+            pl.BlockSpec((deep, width), lambda i: (i, 0)),
         ],
-        out_specs=pl.BlockSpec((rank, step), lambda i: (0, i)),
-        out_shape=jax.ShapeDtypeStruct((rank, rows), jnp.float32),
+        out_specs=[
+            pl.BlockSpec((rank, deep), lambda i: (0, jnp.minimum(i, half - 1))),
+            pl.BlockSpec((rank, deep), lambda i: (0, jnp.maximum(i - half, 0))),
+        ],
+        out_shape=[jax.ShapeDtypeStruct((rank, rows // 2), jnp.float32)] * 2,
         compiler_params=pltpu.CompilerParams(
             dimension_semantics=("arbitrary",), vmem_limit_bytes=48 * 2**20
         ),
@@ -227,108 +245,88 @@
     )(basis, snapshots)
 
 
-def merge_kernel(core_ref, joined_ref, test_ref, o_ref, gram_ref, side_ref):
-    step = pl.program_id(0)
-
-    @pl.when(step == 0)
-    def _():
-        gram_ref[...] = jnp.zeros_like(gram_ref)
-        side_ref[...] = jnp.zeros_like(side_ref)
-
-    left = parts(joined_ref[...], 2)
-    gram_ref[...] += dot_parts(left, left, NT)
-    side_ref[...] += dot_parts(left, parts(test_ref[...], 2), NN)
-
-    @pl.when(step == pl.num_programs(0) - 1)
-    def _():
-        blocks = [gram_ref[cut(a), cut(b)] for a, b in upper_pairs(2)]
-        blocks += [side_ref[cut(a), :] for a in range(2)]
-        pieces = [block[i * 64 : (i + 1) * 64] for block in blocks for i in range(2)]
-        for n, piece in enumerate(pieces):
-            o_ref[(n // 5) ^ core_ref[0], (n % 5) * 64 : (n % 5 + 1) * 64, :] = piece
-
-
-def merge_partials(core, joined, test_block):
-    wide, rows = joined.shape
-    step = rows // 4
+def merge_kernel(place_ref, test_ref, *refs):
+    joined_refs, o_ref = refs[:-1], refs[-1]
+    count = len(joined_refs) // 2
+    half = joined_refs[0].shape[1]
+    merged, side = None, None
+    for h in range(2):
+        left = parts(jnp.concatenate([r[...] for r in joined_refs[h::2]], axis=0), 2)
+        right = parts(test_ref[h * half : (h + 1) * half, :], 2)
+        own = dot_parts(left, left, NT)
+        other = dot_parts(left, right, NN)
+        merged = own if merged is None else merged + own
+        side = other if side is None else side + other
+    blocks = [merged[cut(a), cut(b)] for a, b in upper_pairs(2)]
+    blocks += [side[cut(a), :] for a in range(2)]
+    pieces = [block[i * 64 : (i + 1) * 64] for block in blocks for i in range(2)]
+    for n, piece in enumerate(pieces):
+        o_ref[(n // 5) ^ place_ref[0], (n % 5) * 64 : (n % 5 + 1) * 64, :] = piece
+
+
+def merge_partials(place, joined, test_block):
     return pl.pallas_call(
         merge_kernel,
-        grid=(rows // step,),
-        in_specs=[
-            SMEM,
-            pl.BlockSpec((wide, step), lambda i: (0, i)),
-            pl.BlockSpec((step, BLOCK), lambda i: (i, 0)),
-        ],
-        out_specs=pl.BlockSpec((2, 320, BLOCK), lambda i: (0, 0, 0)),
+        in_specs=[SMEM] + [VMEM] * (1 + len(joined)),
+        out_specs=VMEM,
         out_shape=jax.ShapeDtypeStruct((2, 320, BLOCK), jnp.float32),
-        scratch_shapes=[
-            pltpu.VMEM((wide, wide), jnp.float32),
-            pltpu.VMEM((wide, BLOCK), jnp.float32),
-        ],
-        compiler_params=pltpu.CompilerParams(
-            dimension_semantics=("arbitrary",), vmem_limit_bytes=48 * 2**20
-        ),
+        compiler_params=pltpu.CompilerParams(vmem_limit_bytes=48 * 2**20),
         name="merge_partials",
-    )(core, joined, test_block)
-
-
-def finish_kernel(
-    row_total, core_ref, mine_ref, other_ref, start_ref, joined_ref, o_ref,
-    next_ref, coef_ref, weight_ref, *gram_refs
-):
-    step_index = pl.program_id(0)
-
-    @pl.when(step_index == 0)
-    def _():
-        halves = in_order(core_ref, mine_ref, other_ref)
-        pieces = [halves[n // 5][(n % 5) * 64 : (n % 5 + 1) * 64] for n in range(10)]
-        blocks = [jnp.concatenate(pieces[2 * n : 2 * n + 2], axis=0) for n in range(5)]
-        for (a, b), block in zip(upper_pairs(2), blocks[:3]):
-            block = block / row_total
-            for ref, piece in zip(gram_refs, parts(block, 3)):
-                ref[cut(a), cut(b)] = piece
-            if a != b:
-                for ref, piece in zip(gram_refs, parts(block.T, 3)):
-                    ref[cut(b), cut(a)] = piece
-        next_ref[...] = start_ref[...].T
-
-        def step(index, carry):
-            sweep(coef_ref, next_ref, gram_refs, index > ITERS)
-            return carry
-
-        lax.fori_loop(0, ITERS + 1, step, 0)
-        coef = parts(coef_ref[...], 3)
-        energy = dot_parts(parts(next_ref[...], 3), coef, NT)
-        coef = dot_parts(parts(lower_inverse(energy), 3), coef, NN)
-        coef_parts = parts(coef, 3)
-        side = jnp.concatenate(blocks[3:], axis=0)
-        test_coeffs = dot_parts(coef_parts, parts(side, 3), NN)
-        weight_ref[...] = dot_parts(parts(coef.T, 3), parts(test_coeffs, 3), NN) / row_total
-
-    o_ref[...] = dot_parts(parts(joined_ref[...].T, 2), parts(weight_ref[...], 2), NN)
-
-
-def finish(core, mine, other, start, joined, row_total):
-    wide, rows = joined.shape
-    rank = start.shape[1]
-    step = rows // 4
+    )(place, test_block, *joined)
+
+
+def finish_kernel(row_total, place_ref, mine_ref, other_ref, start_ref, *refs):
+    *joined_refs, o_ref, next_ref, high_ref, middle_ref, low_ref = refs
+    gram_refs = [high_ref, middle_ref, low_ref]
+    halves = in_order(place_ref, mine_ref, other_ref)
+    pieces = [halves[n // 5][(n % 5) * 64 : (n % 5 + 1) * 64] for n in range(10)]
+    blocks = [jnp.concatenate(pieces[2 * n : 2 * n + 2], axis=0) for n in range(5)]
+    for (a, b), block in zip(upper_pairs(2), blocks[:3]):
+        block = block / row_total
+        for ref, piece in zip(gram_refs, parts(block, 3)):
+            ref[cut(a), cut(b)] = piece
+        if a != b:
+            for ref, piece in zip(gram_refs, parts(block.T, 3)):
+                ref[cut(b), cut(a)] = piece
+    groups = start_ref.shape[0]
+    turned = [start_ref[(place_ref[1] + k) % groups] for k in range(groups)]
+    next_ref[...] = jnp.concatenate(turned, axis=0).T
+
+    def step(index, carry):
+        next_ref[...] = normalised(*sweep(next_ref[...], gram_refs))
+        return carry
+
+    lax.fori_loop(0, ITERS, step, 0)
+    inverse, ahead = sweep(next_ref[...], gram_refs)
+    coef = parts(normalised(inverse, next_ref[...]), 3)
+    energy = dot_parts(parts(normalised(inverse, ahead), 3), coef, NT)
+    coef = dot_parts(parts(lower_inverse(energy), 3), coef, NN)
+    side = jnp.concatenate(blocks[3:], axis=0)
+    test_coeffs = dot_parts(parts(coef, 3), parts(side, 3), NN)
+    weight = dot_parts(parts(coef.T, 3), parts(test_coeffs, 3), NN) / row_total
+    weight = parts(weight.T, 2)
+    half = joined_refs[0].shape[1]
+    deep = half // 2
+    for n in range(4):
+        here = slice(n % 2 * deep, (n % 2 + 1) * deep)
+        joined = jnp.concatenate([r[:, here] for r in joined_refs[n // 2 :: 2]], axis=0)
+        o_ref[n * deep : (n + 1) * deep, :] = dot_parts(weight, parts(joined, 2), NN).T
+
+
+def finish(place, mine, other, start, joined, row_total):
+    rank = start.shape[-1]
+    wide = start.shape[0] * start.shape[1]
+    rows = 2 * joined[0].shape[1]
     return pl.pallas_call(
         lambda *refs: finish_kernel(row_total, *refs),
-        grid=(rows // step,),
-        in_specs=[SMEM, VMEM, VMEM, VMEM, pl.BlockSpec((wide, step), lambda i: (0, i))],
-        out_specs=pl.BlockSpec((step, BLOCK), lambda i: (i, 0)),
+        in_specs=[SMEM] + [VMEM] * (3 + len(joined)),
+        out_specs=VMEM,
         out_shape=jax.ShapeDtypeStruct((rows, BLOCK), jnp.float32),
-        scratch_shapes=[
-            pltpu.VMEM((rank, wide), jnp.float32),
-            pltpu.VMEM((rank, wide), jnp.float32),
-            pltpu.VMEM((wide, BLOCK), jnp.float32),
-        ]
+        scratch_shapes=[pltpu.VMEM((rank, wide), jnp.float32)]
         + [pltpu.VMEM((wide, wide), jnp.bfloat16)] * 3,
-        compiler_params=pltpu.CompilerParams(
-            dimension_semantics=("arbitrary",), vmem_limit_bytes=48 * 2**20
-        ),
+        compiler_params=pltpu.CompilerParams(vmem_limit_bytes=48 * 2**20),
         name="finish",
-    )(core, mine, other, start, joined)
+    )(place, mine, other, start, *joined)
 
 
 def swap_cores(array):
@@ -337,23 +335,40 @@
 
 def sum_over_rows(halves):
     kept = halves[0] + swap_cores(halves[1])
-    chips = lax.axis_size(CHIPS)
-    cuts = kept.reshape(chips, kept.shape[0] // chips, BLOCK)
-    own = jnp.sum(lax.all_to_all(cuts, CHIPS, 0, 0, tiled=True), axis=0)
-    copies = jnp.broadcast_to(own, (chips, *own.shape))
-    mine = lax.all_to_all(copies, CHIPS, 0, 0, tiled=True).reshape(kept.shape)
+    near, far = CHIPS
+    lanes = lax.axis_size(near)
+    cuts = kept.reshape(lanes, kept.shape[0] // lanes, BLOCK)
+    own = jnp.sum(lax.all_to_all(cuts, near, 0, 0, tiled=True), axis=0)
+    copies = jnp.broadcast_to(own, (lax.axis_size(far), *own.shape))
+    own = jnp.sum(lax.all_to_all(copies, far, 0, 0, tiled=True), axis=0)
+    copies = jnp.broadcast_to(own, (lanes, *own.shape))
+    mine = lax.all_to_all(copies, near, 0, 0, tiled=True).reshape(kept.shape)
     return mine, swap_cores(mine)
+
+
+def gathered_bases(near, far):
+    groups = lax.axis_size("grp")
+    down = [(i, (i - 1) % groups) for i in range(groups)]
+    up = [(i, (i + 1) % groups) for i in range(groups)]
+    next_near = lax.ppermute(near, "grp", down)
+    last_far = lax.ppermute(far, "grp", up)
+    next_far = lax.ppermute(far, "grp", down)
+    last_near = lax.ppermute(near, "grp", up)
+    across_near = lax.ppermute(next_near, "grp", down)
+    across_far = lax.ppermute(last_far, "grp", up)
+    return [near, far, next_near, next_far, across_near, across_far, last_near, last_far]
 
 
 def on_device(snapshots, test_block, start_block, start_merge):
     row_total = snapshots.shape[0] * lax.axis_size(ROW)
-    core = lax.axis_index(CORE).reshape(1)
-    mine, other = sum_over_rows(gram(snapshots, core))
-    basis = group_solve(core, mine, other, start_block, row_total)
-    own = group_basis(basis, snapshots)
-    joined = lax.all_gather(own, "grp", axis=0, tiled=True)
-    mine, other = sum_over_rows(merge_partials(core, joined, test_block))
-    return finish(core, mine, other, start_merge, joined, row_total)
+    place = jnp.stack([lax.axis_index(CORE), lax.axis_index("grp")])
+    groups = lax.axis_size("grp")
+    mine, other = sum_over_rows(gram(snapshots, place))
+    basis = group_solve(place, mine, other, start_block, row_total)
+    joined = gathered_bases(*group_basis(basis, snapshots))
+    mine, other = sum_over_rows(merge_partials(place, joined, test_block))
+    start = start_merge.reshape(groups, start_merge.shape[0] // groups, start_merge.shape[1])
+    return finish(place, mine, other, start, joined, row_total)
 
 
 def solution(mesh):

time: 214 us -> 185 us (0.86)
  waiting for transfers between devices: 47 us -> 29.8 us
  between operations: 13.5 us -> 0.14 us
  starting transfers between devices: 12.6 us -> 22.1 us
  Pallas kernels: 61.4 us -> 57.1 us
  blocking collectives: 74.6 us -> 71.8 us
    all_gather x1 -> x0, waiting for transfers between devices: 42.7 us -> none  [on_device(): joined = lax.all_gather(own, 'grp', axis=0, tiled=True)]
    ppermute x0 -> x6, waiting for transfers between devices: none -> 26.2 us  [the longest x1 9.54 us: gathered_bases(): last_near = lax.ppermute(near, 'grp', up)]
    ppermute x0 -> x6, starting transfers between devices: none -> 8.66 us  [the longest x1 3.41 us: gathered_bases(): across_near = lax.ppermute(next_near, 'grp', down)]
    pallas_call x3, Pallas kernels: 33.7 us -> 30.4 us  [the longest x1 21.3 us: finish(): pl.pallas_call(lambda *refs: finish_kernel(row_total, *refs), in_specs=[S...]
    all_to_all x4 -> x6, blocking collectives: 74.6 us -> 71.8 us  [the longest x2 39.4 us: sum_over_rows(): own = jnp.sum(lax.all_to_all(copies, far, 0, 0, tiled=True), axis=0)]
    unnamed x12 -> x10, local copies, waits for them, and re-layouts: 4.3 us -> 2.08 us
  transfers between devices with their start and end apart: 5 -> 10, of which waited for: 5 -> 8; matrix products, arithmetic and copies ran while one was open for 0% -> 1% of each run, Pallas kernels for 0% -> 0%
where the time goes in v2:
time: 185 us
  blocking collectives  71.8 us (39%)
  Pallas kernels  57.1 us (31%)
  waiting for transfers between devices  29.8 us (16%)
  starting transfers between devices  22.1 us (12%)
  local copies, waits for them, and re-layouts  3 us (2%)
    all_to_all x2, blocking collectives, sum_over_rows(): own = jnp.sum(lax.all_to_all(copies, far, 0, 0, tiled=True), axis=0)  39.4 us
    pallas_call x1, Pallas kernels, finish(): pl.pallas_call(lambda *refs: finish_kernel(row_total, *refs), in_specs=[S...  21.3 us
    pallas_call x1, Pallas kernels, group_solve(): pl.pallas_call(lambda *refs: solve_kernel(row_total, *refs), in_specs=[SM...  18.5 us
    all_to_all x2, blocking collectives, sum_over_rows(): own = jnp.sum(lax.all_to_all(cuts, near, 0, 0, tiled=True), axis=0)  16.6 us
    all_to_all x2, blocking collectives, sum_over_rows(): mine = lax.all_to_all(copies, near, 0, 0, tiled=True).reshape(kept.shape)  15.7 us
    ppermute x4, starting transfers between devices, swap_cores(): return lax.ppermute(array, CORE, [(0, 1), (1, 0)])  13.4 us
    ppermute x1, waiting for transfers between devices, gathered_bases(): last_near = lax.ppermute(near, 'grp', up)  9.54 us
    pallas_call x1, Pallas kernels, gram(): pl.pallas_call(gram_kernel, in_specs=[SMEM, pl.BlockSpec(memory_space=pl....  8.18 us
  transfers between devices with their start and end apart: 10, of which 8 were waited for; matrix products, arithmetic and copies ran while one was open for 1% of the time, Pallas kernels for 0%

profile of v2, /device:TPU:1, one launch (start us, length us, event | category | flops | bytes accessed | tf_op | source)
XLA Modules:
  0.0 184.7 jit_solution(18265868288031409127)
XLA Ops:
  0.1 8.2 %gram.1 = f32[2,640,128]{2,1,0:T(8,128)S(1)} custom-call(s32[2]{0:T(128)S(1)} %pad_add_fusion.core_ref.refs_0_.place_ref, f32[3584,512]{1,0:T(8,128)} %x_ref.3), custom_call_target="tpu_custom_call" | custom-call | tf_op jit(solution)/shard_map/gram/pallas_call | solution.py:142
  8.3 3.3 %collective-permute-start = (f32[640,128]{1,0:T(8,128)S(1)}, f32[640,128]{1,0:T(8,128)S(1)}, u32[]{:S(2)}, u32[]{:S(2)}) collective-permute-start(f32[640,128]{1,0:T(8,128)S(1)} %slice_bitcast_fusion), channel_id=1, source_target_pairs={{0,1},{1,0},{2,3},{3,2},{4,5},{5,4},{6,7},{7,6},{8,9},{9,8},{10,11... | collective-permute-start | bytes 983048 | tf_op jit(solution)/shard_map/ppermute | solution.py:333
  11.6 1.3 collective-permute-done
  12.9 9.2 %all_to_all.30 = f32[4,160,128]{2,1,0:T(8,128)S(1)} all-to-all(f32[4,160,128]{2,1,0:T(8,128)S(1)} %bitcast.24), channel_id=1, replica_groups=mesh['grp'=4,'row_0'=4,'row_1'=8,'row_2'=2] {'row_0'}, dimensions={0} | all-to-all | bytes 655360 | tf_op jit(solution)/shard_map/all_to_all | solution.py:341
  22.2 26.0 %all_to_all.31 = f32[8,160,128]{2,1,0:T(8,128)S(1)} all-to-all(f32[8,160,128]{2,1,0:T(8,128)S(1)} %broadcast_in_dim.12), channel_id=1, replica_groups=mesh['grp'=4,'row_0'=4,'row_1'=8,'row_2'=2] {'row_1'}, dimensions={0} | all-to-all | bytes 1310720 | tf_op jit(solution)/shard_map/all_to_all | solution.py:343
  48.2 8.3 %all_to_all.32 = f32[4,160,128]{2,1,0:T(8,128)S(1)} all-to-all(f32[4,160,128]{2,1,0:T(8,128)S(1)} %broadcast_in_dim.13), channel_id=1, replica_groups=mesh['grp'=4,'row_0'=4,'row_1'=8,'row_2'=2] {'row_0'}, dimensions={0} | all-to-all | bytes 655360 | tf_op jit(solution)/shard_map/all_to_all | solution.py:345
  56.5 4.3 %collective-permute-start.1 = (f32[640,128]{1,0:T(8,128)S(1)}, f32[640,128]{1,0:T(8,128)S(1)}, u32[]{:S(2)}, u32[]{:S(2)}) collective-permute-start(f32[640,128]{1,0:T(8,128)S(1)} %bitcast.19), channel_id=1, source_target_pairs={{0,1},{1,0},{2,3},{3,2},{4,5},{5,4},{6,7},{7,6},{8,9},{9,8},{10,11... | collective-permute-start | bytes 983048 | tf_op jit(solution)/shard_map/ppermute | solution.py:333
  60.8 0.1 copy.7.refs_3_
  60.9 1.1 collective-permute-done.1.refs_2_
  62.0 18.5 %group_solve.1.q_ref = f32[64,512]{1,0:T(8,128)S(1)} custom-call(s32[2]{0:T(128)S(1)} %pad_add_fusion.core_ref.refs_0_.place_ref, f32[640,128]{1,0:T(8,128)S(1)} %bitcast.20, f32[640,128]{1,0:T(8,128)S(1)} %collective-permute-done.1.refs_2_, f32[512,64]{1,0:T(8,128)S(1)} %copy.7.refs_3_), custom_call_target="tpu_custom_call" | custom-call | tf_op jit(solution)/shard_map/group_solve/pallas_call | solution.py:197
  80.6 5.5 %group_basis.1 = (f32[64,1792]{1,0:T(8,128)S(1)}, f32[64,1792]{1,0:T(8,128)S(1)}) custom-call(f32[64,512]{1,0:T(8,128)S(1)} %group_solve.1.q_ref, f32[3584,512]{1,0:T(8,128)} %x_ref.3), custom_call_target="tpu_custom_call" | custom-call | tf_op jit(solution)/shard_map/group_basis/pallas_call | solution.py:229
  86.1 2.5 %collective-permute-start.2 = (f32[64,1792]{1,0:T(8,128)S(1)}, f32[64,1792]{1,0:T(8,128)S(1)}, u32[]{:S(2)}, u32[]{:S(2)}) collective-permute-start(f32[64,1792]{1,0:T(8,128)S(1)} %get-tuple-element.7.refs_0_.refs_4_), channel_id=1, source_target_pairs={{0,192},{64,0},{128,64},{192,128},{1,193},{65,1},{129,65},{193,129... | collective-permute-start | bytes 1376264 | tf_op jit(solution)/shard_map/ppermute | solution.py:353
  88.6 0.2 collective-permute-start.7
  88.8 2.5 %collective-permute-start.3 = (f32[64,1792]{1,0:T(8,128)S(1)}, f32[64,1792]{1,0:T(8,128)S(1)}, u32[]{:S(2)}, u32[]{:S(2)}) collective-permute-start(f32[64,1792]{1,0:T(8,128)S(1)} %get-tuple-element.8.refs_1_.refs_5_), channel_id=1, source_target_pairs={{0,192},{64,0},{128,64},{192,128},{1,193},{65,1},{129,65},{193,129... | collective-permute-start | bytes 1376264 | tf_op jit(solution)/shard_map/ppermute | solution.py:355
  91.3 6.8 %collective-permute-done.2.refs_2_.refs_6_ = f32[64,1792]{1,0:T(8,128)S(1)} collective-permute-done((f32[64,1792]{1,0:T(8,128)S(1)}, f32[64,1792]{1,0:T(8,128)S(1)}, u32[]{:S(2)}, u32[]{:S(2)}) %collective-permute-start.2) | collective-permute-done | bytes 458784 | tf_op jit(solution)/shard_map/ppermute | solution.py:353
  98.1 3.4 %collective-permute-start.4 = (f32[64,1792]{1,0:T(8,128)S(1)}, f32[64,1792]{1,0:T(8,128)S(1)}, u32[]{:S(2)}, u32[]{:S(2)}) collective-permute-start(f32[64,1792]{1,0:T(8,128)S(1)} %collective-permute-done.2.refs_2_.refs_6_), channel_id=1, source_target_pairs={{0,192},{64,0},{128,64},{192,128},{1,193},{65,1},{129,65},{193,129... | collective-permute-start | bytes 1376264 | tf_op jit(solution)/shard_map/ppermute | solution.py:357
  101.6 9.5 %collective-permute-done.7.refs_6_.refs_10_ = f32[64,1792]{1,0:T(8,128)S(1)} collective-permute-done((f32[64,1792]{1,0:T(8,128)S(1)}, f32[64,1792]{1,0:T(8,128)S(1)}, u32[]{:S(2)}, u32[]{:S(2)}) %collective-permute-start.7) | collective-permute-done | bytes 458784 | tf_op jit(solution)/shard_map/ppermute | solution.py:356
  111.1 6.7 %collective-permute-done.4.refs_4_.refs_8_ = f32[64,1792]{1,0:T(8,128)S(1)} collective-permute-done((f32[64,1792]{1,0:T(8,128)S(1)}, f32[64,1792]{1,0:T(8,128)S(1)}, u32[]{:S(2)}, u32[]{:S(2)}) %collective-permute-start.4) | collective-permute-done | bytes 458784 | tf_op jit(solution)/shard_map/ppermute | solution.py:357
  117.8 3.1 %collective-permute-done.6.refs_5_.refs_9_ = f32[64,1792]{1,0:T(8,128)S(1)} collective-permute-done((f32[64,1792]{1,0:T(8,128)S(1)}, f32[64,1792]{1,0:T(8,128)S(1)}, u32[]{:S(2)}, u32[]{:S(2)}) %collective-permute-start.6) | collective-permute-done | bytes 458784 | tf_op jit(solution)/shard_map/ppermute | solution.py:358
  120.9 3.6 %merge_partials.1 = f32[2,320,128]{2,1,0:T(8,128)S(1)} custom-call(s32[2]{0:T(128)S(1)} %pad_add_fusion.core_ref.refs_0_.place_ref, f32[3584,128]{1,0:T(8,128)S(1)} %copy-done.2, f32[64,1792]{1,0:T(8,128)S(1)} %get-tuple-element.7.refs_0_.refs_4_, f32[64,1792]{1,0:T(8,128)S(1)} %get-tuple-element.8.refs_1_.refs_5_, ...), custom_call_target="tpu_custom_call" | custom-call | tf_op jit(solution)/shard_map/merge_partials/pallas_call | solution.py:268
  124.6 1.6 collective-permute-start.8
  126.2 1.0 collective-permute-done.8
  127.3 7.4 %all_to_all.33 = f32[4,80,128]{2,1,0:T(8,128)S(1)} all-to-all(f32[4,80,128]{2,1,0:T(8,128)S(1)} %bitcast.25), channel_id=1, replica_groups=mesh['grp'=4,'row_0'=4,'row_1'=8,'row_2'=2] {'row_0'}, dimensions={0} | all-to-all | bytes 327680 | tf_op jit(solution)/shard_map/all_to_all | solution.py:341
  134.7 13.5 %all_to_all.34 = f32[8,80,128]{2,1,0:T(8,128)S(1)} all-to-all(f32[8,80,128]{2,1,0:T(8,128)S(1)} %broadcast_in_dim.14), channel_id=1, replica_groups=mesh['grp'=4,'row_0'=4,'row_1'=8,'row_2'=2] {'row_1'}, dimensions={0} | all-to-all | bytes 655360 | tf_op jit(solution)/shard_map/all_to_all | solution.py:343
  148.2 0.6 reduce_sum.39
  148.8 0.8 broadcast_in_dim.15
  149.6 7.5 %all_to_all.35 = f32[4,80,128]{2,1,0:T(8,128)S(1)} all-to-all(f32[4,80,128]{2,1,0:T(8,128)S(1)} %broadcast_in_dim.15), channel_id=1, replica_groups=mesh['grp'=4,'row_0'=4,'row_1'=8,'row_2'=2] {'row_0'}, dimensions={0} | all-to-all | bytes 327680 | tf_op jit(solution)/shard_map/all_to_all | solution.py:345
  157.1 4.2 %collective-permute-start.9 = (f32[320,128]{1,0:T(8,128)S(1)}, f32[320,128]{1,0:T(8,128)}, u32[]{:S(2)}, u32[]{:S(2)}) collective-permute-start(f32[320,128]{1,0:T(8,128)S(1)} %bitcast.21), channel_id=1, source_target_pairs={{0,1},{1,0},{2,3},{3,2},{4,5},{5,4},{6,7},{7,6},{8,9},{9,8},{10,11... | collective-permute-start | bytes 491528 | tf_op jit(solution)/shard_map/ppermute | solution.py:333
  161.3 0.9 copy.8
  162.2 0.2 collective-permute-done.9.refs_2_
  162.5 1.0 copy-done.1
  163.5 21.3 %finish.1 = f32[3584,128]{1,0:T(8,128)} custom-call(s32[2]{0:T(128)S(1)} %pad_add_fusion.core_ref.refs_0_.place_ref, f32[320,128]{1,0:T(8,128)S(1)} %bitcast.22, f32[320,128]{1,0:T(8,128)} %collective-permute-done.9.refs_2_, f32[4,64,64]{2,1,0:T(8,128)S(1)} %bitcast.23, f32[64,1792]{1,0:T(8,128)S(1)} %get-tuple-element.7.refs_0_.refs_4_, ...), custom_call_target="tpu_custom_call" | custom-call | tf_op jit(solution)/shard_map/finish/pallas_call | solution.py:320
  (22 shorter events, 0.4 us)
Async XLA Ops:
  8.3 4.5 %collective-permute-start = (f32[640,128]{1,0:T(8,128)S(1)}, f32[640,128]{1,0:T(8,128)S(1)}, u32[]{:S(2)}, u32[]{:S(2)}) collective-permute-start(f32[640,128]{1,0:T(8,128)S(1)} %slice_bitcast_fusion), channel_id=1, source_target_pairs={{0,1},{1,0},{2,3},{3,2},{4,5},{5,4},{6,7},{7,6},{8,9},{9,8},{10,11... | collective-permute-start | bytes 983048 | tf_op jit(solution)/shard_map/ppermute | solution.py:333
  22.1 38.7 %copy-start.3 = (f32[512,64]{0,1:T(8,128)S(1)}, f32[512,64]{0,1:T(8,128)}, u32[]{:S(2)}) copy-start(f32[512,64]{0,1:T(8,128)} %param.6) | copy-start | bytes 393220
  56.5 5.6 %collective-permute-start.1 = (f32[640,128]{1,0:T(8,128)S(1)}, f32[640,128]{1,0:T(8,128)S(1)}, u32[]{:S(2)}, u32[]{:S(2)}) collective-permute-start(f32[640,128]{1,0:T(8,128)S(1)} %bitcast.19), channel_id=1, source_target_pairs={{0,1},{1,0},{2,3},{3,2},{4,5},{5,4},{6,7},{7,6},{8,9},{9,8},{10,11... | collective-permute-start | bytes 983048 | tf_op jit(solution)/shard_map/ppermute | solution.py:333
  80.6 40.4 %copy-start.2 = (f32[3584,128]{1,0:T(8,128)S(1)}, f32[3584,128]{1,0:T(8,128)}, u32[]{:S(2)}) copy-start(f32[3584,128]{1,0:T(8,128)} %test_ref.1) | copy-start | bytes 5505028
  86.1 12.1 %collective-permute-start.2 = (f32[64,1792]{1,0:T(8,128)S(1)}, f32[64,1792]{1,0:T(8,128)S(1)}, u32[]{:S(2)}, u32[]{:S(2)}) collective-permute-start(f32[64,1792]{1,0:T(8,128)S(1)} %get-tuple-element.7.refs_0_.refs_4_), channel_id=1, source_target_pairs={{0,192},{64,0},{128,64},{192,128},{1,193},{65,1},{129,65},{193,129... | collective-permute-start | bytes 1376264 | tf_op jit(solution)/shard_map/ppermute | solution.py:353
  88.6 12.9 %collective-permute-start.5 = (f32[64,1792]{1,0:T(8,128)S(1)}, f32[64,1792]{1,0:T(8,128)S(1)}, u32[]{:S(2)}, u32[]{:S(2)}) collective-permute-start(f32[64,1792]{1,0:T(8,128)S(1)} %get-tuple-element.8.refs_1_.refs_5_), channel_id=1, source_target_pairs={{0,64},{64,128},{128,192},{192,0},{1,65},{65,129},{129,193},{193,1... | collective-permute-start | bytes 1376264 | tf_op jit(solution)/shard_map/ppermute | solution.py:354
  88.6 22.5 %collective-permute-start.7 = (f32[64,1792]{1,0:T(8,128)S(1)}, f32[64,1792]{1,0:T(8,128)S(1)}, u32[]{:S(2)}, u32[]{:S(2)}) collective-permute-start(f32[64,1792]{1,0:T(8,128)S(1)} %get-tuple-element.7.refs_0_.refs_4_), channel_id=1, source_target_pairs={{0,64},{64,128},{128,192},{192,0},{1,65},{65,129},{129,193},{193,1... | collective-permute-start | bytes 1376264 | tf_op jit(solution)/shard_map/ppermute | solution.py:356
  88.8 22.3 %collective-permute-start.3 = (f32[64,1792]{1,0:T(8,128)S(1)}, f32[64,1792]{1,0:T(8,128)S(1)}, u32[]{:S(2)}, u32[]{:S(2)}) collective-permute-start(f32[64,1792]{1,0:T(8,128)S(1)} %get-tuple-element.8.refs_1_.refs_5_), channel_id=1, source_target_pairs={{0,192},{64,0},{128,64},{192,128},{1,193},{65,1},{129,65},{193,129... | collective-permute-start | bytes 1376264 | tf_op jit(solution)/shard_map/ppermute | solution.py:355
  98.1 19.7 %collective-permute-start.4 = (f32[64,1792]{1,0:T(8,128)S(1)}, f32[64,1792]{1,0:T(8,128)S(1)}, u32[]{:S(2)}, u32[]{:S(2)}) collective-permute-start(f32[64,1792]{1,0:T(8,128)S(1)} %collective-permute-done.2.refs_2_.refs_6_), channel_id=1, source_target_pairs={{0,192},{64,0},{128,64},{192,128},{1,193},{65,1},{129,65},{193,129... | collective-permute-start | bytes 1376264 | tf_op jit(solution)/shard_map/ppermute | solution.py:357
  101.6 19.4 %collective-permute-start.6 = (f32[64,1792]{1,0:T(8,128)S(1)}, f32[64,1792]{1,0:T(8,128)S(1)}, u32[]{:S(2)}, u32[]{:S(2)}) collective-permute-start(f32[64,1792]{1,0:T(8,128)S(1)} %collective-permute-done.5.refs_7_.refs_11_), channel_id=1, source_target_pairs={{0,64},{64,128},{128,192},{192,0},{1,65},{65,129},{129,193},{193,1... | collective-permute-start | bytes 1376264 | tf_op jit(solution)/shard_map/ppermute | solution.py:358
  120.9 3.6 %copy-start = (f32[64,1792]{1,0:T(8,128)}, f32[64,1792]{1,0:T(8,128)S(1)}, u32[]{:S(2)}) copy-start(f32[64,1792]{1,0:T(8,128)S(1)} %collective-permute-done.6.refs_5_.refs_9_) | copy-start | bytes 1376260
  124.6 2.6 %collective-permute-start.8 = (f32[320,128]{1,0:T(8,128)S(1)}, f32[320,128]{1,0:T(8,128)S(1)}, u32[]{:S(2)}, u32[]{:S(2)}) collective-permute-start(f32[320,128]{1,0:T(8,128)S(1)} %slice_bitcast_fusion.2), channel_id=1, source_target_pairs={{0,1},{1,0},{2,3},{3,2},{4,5},{5,4},{6,7},{7,6},{8,9},{9,8},{10,11... | collective-permute-start | bytes 491528 | tf_op jit(solution)/shard_map/ppermute | solution.py:333
  157.1 5.3 %collective-permute-start.9 = (f32[320,128]{1,0:T(8,128)S(1)}, f32[320,128]{1,0:T(8,128)}, u32[]{:S(2)}, u32[]{:S(2)}) collective-permute-start(f32[320,128]{1,0:T(8,128)S(1)} %bitcast.21), channel_id=1, source_target_pairs={{0,1},{1,0},{2,3},{3,2},{4,5},{5,4},{6,7},{7,6},{8,9},{9,8},{10,11... | collective-permute-start | bytes 491528 | tf_op jit(solution)/shard_map/ppermute | solution.py:333
  162.5 1.0 copy-start.1

commit v3 on v2

--- a/solution.py
+++ b/solution.py
@@ -11,6 +11,7 @@
 CHIPS = ("row_0", "row_1")
 CORE = "row_2"
 BLOCK = 128
+SHIFTS = (0, 1, 3, 2)
 VMEM = pl.BlockSpec(memory_space=pltpu.VMEM)
 SMEM = pl.BlockSpec(memory_space=pltpu.SMEM)
 
@@ -63,26 +64,33 @@
     def line(value, j):
         return jnp.broadcast_to(value[j : j + 1, :], value.shape)
 
+    diagonal = [column(work[0], j) for j in range(8)]
     for b in range(bands):
-        cols = {i: [column(work[i], 8 * b + j) for j in range(8)] for i in range(b, bands)}
+        cols = {i: [column(work[i], 8 * b + j) for j in range(8)] for i in range(b + 1, bands)}
+        coming = [column(work[b + 1], 8 * b + 8 + k) for k in range(8)] if cols else None
         scale = None
         for j in range(8):
-            pivot = line(cols[b][j], j)
+            pivot = line(diagonal[j], j)
             root = lax.rsqrt(pivot)
             inverse = root * root
             scale = root if scale is None else jnp.where(sub == j, root, scale)
-            factor = jnp.where(sub > j, cols[b][j] * inverse, 0.0)
-            ahead = {k: line(cols[b][k], j) for k in range(j + 1, 8)}
+            lower = jnp.where(sub > j, diagonal[j], 0.0)
+            factor = lower * inverse
+            ahead = {k: line(diagonal[k], j) for k in range(j + 1, 8)}
             pivot_row = line(work[b], j)
             for k in range(j + 1, 8):
-                cols[b][k] = cols[b][k] - factor * ahead[k]
+                change = lower * ahead[k] * inverse if k == j + 1 else factor * ahead[k]
+                diagonal[k] = diagonal[k] - change
             work[b] = work[b] - factor * pivot_row
             for i in range(b + 1, bands):
                 below = cols[i][j] * inverse
                 for k in range(j + 1, 8):
                     cols[i][k] = cols[i][k] - below * ahead[k]
                 work[i] = work[i] - below * pivot_row
+                if i == b + 1:
+                    coming = [coming[k] - below * line(cols[i][j], k) for k in range(8)]
         work[b] = work[b] * scale
+        diagonal = coming
     return jnp.concatenate(work, axis=0)[:, size:]
 
 
@@ -245,19 +253,63 @@
     )(basis, snapshots)
 
 
-def merge_kernel(place_ref, test_ref, *refs):
-    joined_refs, o_ref = refs[:-1], refs[-1]
-    count = len(joined_refs) // 2
+def stacked(refs, h):
+    return jnp.concatenate([ref[...] for ref in refs[h::2]], axis=0)
+
+
+def merge_near_kernel(test_ref, *refs):
+    *joined_refs, merged_ref, side_ref = refs
     half = joined_refs[0].shape[1]
     merged, side = None, None
     for h in range(2):
-        left = parts(jnp.concatenate([r[...] for r in joined_refs[h::2]], axis=0), 2)
+        left = parts(stacked(joined_refs, h), 2)
         right = parts(test_ref[h * half : (h + 1) * half, :], 2)
         own = dot_parts(left, left, NT)
         other = dot_parts(left, right, NN)
         merged = own if merged is None else merged + own
         side = other if side is None else side + other
-    blocks = [merged[cut(a), cut(b)] for a, b in upper_pairs(2)]
+    merged_ref[...] = merged
+    side_ref[...] = side
+
+
+def merge_near(joined, test_block):
+    wide = len(joined) // 2 * joined[0].shape[0]
+    return pl.pallas_call(
+        merge_near_kernel,
+        in_specs=[VMEM] * (1 + len(joined)),
+        out_specs=[VMEM, VMEM],
+        out_shape=[
+            jax.ShapeDtypeStruct((wide, wide), jnp.float32),
+            jax.ShapeDtypeStruct((wide, BLOCK), jnp.float32),
+        ],
+        compiler_params=pltpu.CompilerParams(vmem_limit_bytes=48 * 2**20),
+        name="merge_near",
+    )(test_block, *joined)
+
+
+def merge_kernel(place_ref, merged_ref, side_ref, test_ref, *refs):
+    *joined_refs, o_ref = refs
+    half = joined_refs[0].shape[1]
+    rank = joined_refs[0].shape[0]
+    cross, last = None, None
+    for h in range(2):
+        left = parts(stacked(joined_refs, h), 2)
+        across = [piece[-rank:] for piece in left]
+        right = parts(test_ref[h * half : (h + 1) * half, :], 2)
+        own = dot_parts(left, across, NT)
+        other = dot_parts(across, right, NN)
+        cross = own if cross is None else cross + own
+        last = other if last is None else last + other
+    merged, side = merged_ref[...], side_ref[...]
+    blocks = [
+        merged[:BLOCK, :BLOCK],
+        jnp.concatenate([merged[:BLOCK, BLOCK:], cross[:BLOCK]], axis=1),
+        jnp.concatenate(
+            [jnp.concatenate([merged[BLOCK:, BLOCK:], cross[BLOCK:-rank].T], axis=0), cross[BLOCK:]],
+            axis=1,
+        ),
+    ]
+    side = jnp.concatenate([side, last], axis=0)
     blocks += [side[cut(a), :] for a in range(2)]
     pieces = [block[i * 64 : (i + 1) * 64] for block in blocks for i in range(2)]
     for n, piece in enumerate(pieces):
@@ -267,12 +319,12 @@
 def merge_partials(place, joined, test_block):
     return pl.pallas_call(
         merge_kernel,
-        in_specs=[SMEM] + [VMEM] * (1 + len(joined)),
+        in_specs=[SMEM] + [VMEM] * (3 + len(joined)),
         out_specs=VMEM,
         out_shape=jax.ShapeDtypeStruct((2, 320, BLOCK), jnp.float32),
         compiler_params=pltpu.CompilerParams(vmem_limit_bytes=48 * 2**20),
         name="merge_partials",
-    )(place, test_block, *joined)
+    )(place, *merge_near(joined[:-2], test_block), test_block, *joined)
 
 
 def finish_kernel(row_total, place_ref, mine_ref, other_ref, start_ref, *refs):
@@ -289,7 +341,7 @@
             for ref, piece in zip(gram_refs, parts(block.T, 3)):
                 ref[cut(b), cut(a)] = piece
     groups = start_ref.shape[0]
-    turned = [start_ref[(place_ref[1] + k) % groups] for k in range(groups)]
+    turned = [start_ref[(place_ref[1] + k) % groups] for k in SHIFTS]
     next_ref[...] = jnp.concatenate(turned, axis=0).T
 
     def step(index, carry):
@@ -333,16 +385,26 @@
     return lax.ppermute(array, CORE, [(0, 1), (1, 0)])
 
 
+def reduced(array, axis):
+    length = lax.axis_size(axis)
+    cuts = array.reshape(length, array.shape[0] // length, BLOCK)
+    return jnp.sum(lax.all_to_all(cuts, axis, 0, 0, tiled=True), axis=0)
+
+
+def spread(array, axis):
+    copies = jnp.broadcast_to(array, (lax.axis_size(axis), *array.shape))
+    return lax.all_to_all(copies, axis, 0, 0, tiled=True)
+
+
 def sum_over_rows(halves):
+    near, far = CHIPS
     kept = halves[0] + swap_cores(halves[1])
-    near, far = CHIPS
-    lanes = lax.axis_size(near)
-    cuts = kept.reshape(lanes, kept.shape[0] // lanes, BLOCK)
-    own = jnp.sum(lax.all_to_all(cuts, near, 0, 0, tiled=True), axis=0)
-    copies = jnp.broadcast_to(own, (lax.axis_size(far), *own.shape))
-    own = jnp.sum(lax.all_to_all(copies, far, 0, 0, tiled=True), axis=0)
-    copies = jnp.broadcast_to(own, (lanes, *own.shape))
-    mine = lax.all_to_all(copies, near, 0, 0, tiled=True).reshape(kept.shape)
+    own = reduced(kept, near)
+    if own.shape[0] > 100:
+        own = spread(reduced(own, far), far).reshape(own.shape)
+    else:
+        own = jnp.sum(spread(own, far), axis=0)
+    mine = spread(own, near).reshape(kept.shape)
     return mine, swap_cores(mine)
 
 
@@ -356,7 +418,7 @@
     last_near = lax.ppermute(near, "grp", up)
     across_near = lax.ppermute(next_near, "grp", down)
     across_far = lax.ppermute(last_far, "grp", up)
-    return [near, far, next_near, next_far, across_near, across_far, last_near, last_far]
+    return [near, far, next_near, next_far, last_near, last_far, across_near, across_far]
 
 
 def on_device(snapshots, test_block, start_block, start_merge):

time: 185 us -> 176 us (0.951)
  Pallas kernels: 57.1 us -> 49.4 us
  waiting for transfers between devices: 29.8 us -> 27.5 us
    pallas_call x1, Pallas kernels: 21.3 us -> 16.4 us  [finish(): pl.pallas_call(lambda *refs: finish_kernel(row_total, *refs), in_specs=[S...]
    pallas_call x1, Pallas kernels: 18.5 us -> 14.3 us  [group_solve(): pl.pallas_call(lambda *refs: solve_kernel(row_total, *refs), in_specs=[SM...]
    ppermute x1, waiting for transfers between devices: 6.7 us -> 4.34 us  [gathered_bases(): across_near = lax.ppermute(next_near, 'grp', down)]
    pallas_call x1 -> x2, Pallas kernels: 3.63 us -> 4.99 us  [the longest x1 2.64 us: merge_partials(): pl.pallas_call(merge_kernel, in_specs=[SMEM] + [VMEM] * (3 + len(joined))...]
    all_to_all x6 -> x7, blocking collectives: 71.8 us -> 71.4 us  [the longest x4 39.3 us: spread(): return lax.all_to_all(copies, axis, 0, 0, tiled=True)]
  transfers between devices with their start and end apart: 10 -> 10, of which waited for: 8 -> 8; matrix products, arithmetic and copies ran while one was open for 1% -> 1% of each run, Pallas kernels for 0% -> 1%
where the time goes in v3:
time: 176 us; the launch traced here: 175 us
  blocking collectives  71.4 us (41%)
  Pallas kernels  49.4 us (28%)
  waiting for transfers between devices  27.5 us (16%)
  starting transfers between devices  22.8 us (13%)
  local copies, waits for them, and re-layouts  2.98 us (2%)
    all_to_all x4, blocking collectives, spread(): return lax.all_to_all(copies, axis, 0, 0, tiled=True)  39.3 us
    all_to_all x3, blocking collectives, reduced(): return jnp.sum(lax.all_to_all(cuts, axis, 0, 0, tiled=True), axis=0)  32.1 us
    pallas_call x1, Pallas kernels, finish(): pl.pallas_call(lambda *refs: finish_kernel(row_total, *refs), in_specs=[S...  16.4 us
    pallas_call x1, Pallas kernels, group_solve(): pl.pallas_call(lambda *refs: solve_kernel(row_total, *refs), in_specs=[SM...  14.3 us
    ppermute x4, starting transfers between devices, swap_cores(): return lax.ppermute(array, CORE, [(0, 1), (1, 0)])  14.2 us
    ppermute x1, waiting for transfers between devices, gathered_bases(): last_near = lax.ppermute(near, 'grp', up)  9.54 us
    pallas_call x1, Pallas kernels, gram(): pl.pallas_call(gram_kernel, in_specs=[SMEM, pl.BlockSpec(memory_space=pl....  8.18 us
    ppermute x1, waiting for transfers between devices, gathered_bases(): next_near = lax.ppermute(near, 'grp', down)  6.81 us
  transfers between devices with their start and end apart: 10, of which 8 were waited for; matrix products, arithmetic and copies ran while one was open for 1% of the time, Pallas kernels for 1%

profile of v3, /device:TPU:1, one launch (start us, length us, event | category | flops | bytes accessed | tf_op | source)
XLA Modules:
  0.0 175.0 jit_solution(14292401588129466537)
XLA Ops:
  0.1 8.2 %gram.1 = f32[2,640,128]{2,1,0:T(8,128)S(1)} custom-call(s32[2]{0:T(128)S(1)} %pad_add_fusion.core_ref.refs_0_.place_ref, f32[3584,512]{1,0:T(8,128)} %x_ref.3), custom_call_target="tpu_custom_call" | custom-call | tf_op jit(solution)/shard_map/gram/pallas_call | solution.py:150
  8.3 3.3 %collective-permute-start = (f32[640,128]{1,0:T(8,128)S(1)}, f32[640,128]{1,0:T(8,128)S(1)}, u32[]{:S(2)}, u32[]{:S(2)}) collective-permute-start(f32[640,128]{1,0:T(8,128)S(1)} %slice_bitcast_fusion), channel_id=1, source_target_pairs={{0,1},{1,0},{2,3},{3,2},{4,5},{5,4},{6,7},{7,6},{8,9},{9,8},{10,11... | collective-permute-start | bytes 983048 | tf_op jit(solution)/shard_map/ppermute | solution.py:385
  11.6 1.3 collective-permute-done
  12.9 9.2 %all_to_all.35 = f32[4,160,128]{2,1,0:T(8,128)S(1)} all-to-all(f32[4,160,128]{2,1,0:T(8,128)S(1)} %bitcast.24), channel_id=1, replica_groups=mesh['grp'=4,'row_0'=4,'row_1'=8,'row_2'=2] {'row_0'}, dimensions={0} | all-to-all | bytes 655360 | tf_op jit(solution)/shard_map/all_to_all | solution.py:391
  22.1 15.5 %all_to_all.36 = f32[8,20,128]{2,1,0:T(8,128)S(1)} all-to-all(f32[8,20,128]{2,1,0:T(8,128)S(1)} %reshape.22), channel_id=1, replica_groups=mesh['grp'=4,'row_0'=4,'row_1'=8,'row_2'=2] {'row_1'}, dimensions={0} | all-to-all | bytes 163840 | tf_op jit(solution)/shard_map/all_to_all | solution.py:391
  37.7 10.1 %all_to_all.37 = f32[8,20,128]{2,1,0:T(8,128)S(1)} all-to-all(f32[8,20,128]{2,1,0:T(8,128)S(1)} %broadcast_in_dim.12), channel_id=1, replica_groups=mesh['grp'=4,'row_0'=4,'row_1'=8,'row_2'=2] {'row_1'}, dimensions={0} | all-to-all | bytes 163840 | tf_op jit(solution)/shard_map/all_to_all | solution.py:396
  47.8 8.3 %all_to_all.38 = f32[4,160,128]{2,1,0:T(8,128)S(1)} all-to-all(f32[4,160,128]{2,1,0:T(8,128)S(1)} %broadcast_in_dim.13), channel_id=1, replica_groups=mesh['grp'=4,'row_0'=4,'row_1'=8,'row_2'=2] {'row_0'}, dimensions={0} | all-to-all | bytes 655360 | tf_op jit(solution)/shard_map/all_to_all | solution.py:396
  56.0 5.1 %collective-permute-start.1 = (f32[640,128]{1,0:T(8,128)S(1)}, f32[640,128]{1,0:T(8,128)S(1)}, u32[]{:S(2)}, u32[]{:S(2)}) collective-permute-start(f32[640,128]{1,0:T(8,128)S(1)} %bitcast.19), channel_id=1, source_target_pairs={{0,1},{1,0},{2,3},{3,2},{4,5},{5,4},{6,7},{7,6},{8,9},{9,8},{10,11... | collective-permute-start | bytes 983048 | tf_op jit(solution)/shard_map/ppermute | solution.py:385
  61.2 1.1 collective-permute-done.1.refs_2_
  62.4 14.3 %group_solve.1.q_ref = f32[64,512]{1,0:T(8,128)S(1)} custom-call(s32[2]{0:T(128)S(1)} %pad_add_fusion.core_ref.refs_0_.place_ref, f32[640,128]{1,0:T(8,128)S(1)} %bitcast.20, f32[640,128]{1,0:T(8,128)S(1)} %collective-permute-done.1.refs_2_, f32[512,64]{1,0:T(8,128)S(1)} %copy.9.refs_3_), custom_call_target="tpu_custom_call" | custom-call | tf_op jit(solution)/shard_map/group_solve/pallas_call | solution.py:205
  76.7 5.5 %group_basis.1 = (f32[64,1792]{1,0:T(8,128)S(1)}, f32[64,1792]{1,0:T(8,128)S(1)}) custom-call(f32[64,512]{1,0:T(8,128)S(1)} %group_solve.1.q_ref, f32[3584,512]{1,0:T(8,128)} %x_ref.3), custom_call_target="tpu_custom_call" | custom-call | tf_op jit(solution)/shard_map/group_basis/pallas_call | solution.py:237
  82.2 2.6 %collective-permute-start.2 = (f32[64,1792]{1,0:T(8,128)S(1)}, f32[64,1792]{1,0:T(8,128)S(1)}, u32[]{:S(2)}, u32[]{:S(2)}) collective-permute-start(f32[64,1792]{1,0:T(8,128)S(1)} %get-tuple-element.9.refs_0_.refs_4_), channel_id=1, source_target_pairs={{0,192},{64,0},{128,64},{192,128},{1,193},{65,1},{129,65},{193,129... | collective-permute-start | bytes 1376264 | tf_op jit(solution)/shard_map/ppermute | solution.py:415
  84.9 2.5 %collective-permute-start.3 = (f32[64,1792]{1,0:T(8,128)S(1)}, f32[64,1792]{1,0:T(8,128)S(1)}, u32[]{:S(2)}, u32[]{:S(2)}) collective-permute-start(f32[64,1792]{1,0:T(8,128)S(1)} %get-tuple-element.10.refs_1_.refs_5_), channel_id=1, source_target_pairs={{0,192},{64,0},{128,64},{192,128},{1,193},{65,1},{129,65},{193,129... | collective-permute-start | bytes 1376264 | tf_op jit(solution)/shard_map/ppermute | solution.py:417
  87.4 6.8 %collective-permute-done.2.refs_2_.refs_6_ = f32[64,1792]{1,0:T(8,128)S(1)} collective-permute-done((f32[64,1792]{1,0:T(8,128)S(1)}, f32[64,1792]{1,0:T(8,128)S(1)}, u32[]{:S(2)}, u32[]{:S(2)}) %collective-permute-start.2) | collective-permute-done | bytes 458784 | tf_op jit(solution)/shard_map/ppermute | solution.py:415
  94.2 3.4 %collective-permute-start.6 = (f32[64,1792]{1,0:T(8,128)S(1)}, f32[64,1792]{1,0:T(8,128)S(1)}, u32[]{:S(2)}, u32[]{:S(2)}) collective-permute-start(f32[64,1792]{1,0:T(8,128)S(1)} %collective-permute-done.2.refs_2_.refs_6_), channel_id=1, source_target_pairs={{0,192},{64,0},{128,64},{192,128},{1,193},{65,1},{129,65},{193,129... | collective-permute-start | bytes 1376264 | tf_op jit(solution)/shard_map/ppermute | solution.py:419
  97.7 9.5 %collective-permute-done.4.refs_4_.refs_8_ = f32[64,1792]{1,0:T(8,128)S(1)} collective-permute-done((f32[64,1792]{1,0:T(8,128)S(1)}, f32[64,1792]{1,0:T(8,128)S(1)}, u32[]{:S(2)}, u32[]{:S(2)}) %collective-permute-start.4) | collective-permute-done | bytes 458784 | tf_op jit(solution)/shard_map/ppermute | solution.py:418
  107.2 2.3 %merge_near.1 = (f32[192,192]{1,0:T(8,128)S(1)}, f32[192,128]{1,0:T(8,128)S(1)}) custom-call(f32[3584,128]{1,0:T(8,128)S(1)} %copy-done, f32[64,1792]{1,0:T(8,128)S(1)} %get-tuple-element.9.refs_0_.refs_4_, f32[64,1792]{1,0:T(8,128)S(1)} %get-tuple-element.10.refs_1_.refs_5_, f32[64,1792]{1,0:T(8,128)S(1)} %collective-permute-done.2.refs_2_.refs_6_, ...), custom_call_target="tpu_custom_call" | custom-call | tf_op jit(solution)/shard_map/merge_near/pallas_call | solution.py:277
  109.6 4.3 %collective-permute-done.6.refs_6_.refs_10_ = f32[64,1792]{1,0:T(8,128)S(1)} collective-permute-done((f32[64,1792]{1,0:T(8,128)S(1)}, f32[64,1792]{1,0:T(8,128)S(1)}, u32[]{:S(2)}, u32[]{:S(2)}) %collective-permute-start.6) | collective-permute-done | bytes 458784 | tf_op jit(solution)/shard_map/ppermute | solution.py:419
  113.9 3.1 %collective-permute-done.7.refs_7_.refs_11_ = f32[64,1792]{1,0:T(8,128)S(1)} collective-permute-done((f32[64,1792]{1,0:T(8,128)S(1)}, f32[64,1792]{1,0:T(8,128)S(1)}, u32[]{:S(2)}, u32[]{:S(2)}) %collective-permute-start.7) | collective-permute-done | bytes 458784 | tf_op jit(solution)/shard_map/ppermute | solution.py:420
  117.0 2.6 %merge_partials.1 = f32[2,320,128]{2,1,0:T(8,128)S(1)} custom-call(s32[2]{0:T(128)S(1)} %pad_add_fusion.core_ref.refs_0_.place_ref, f32[192,192]{1,0:T(8,128)S(1)} %get-tuple-element.11.merged_ref, f32[192,128]{1,0:T(8,128)S(1)} %get-tuple-element.12.side_ref, f32[3584,128]{1,0:T(8,128)S(1)} %copy-done, f32[64,1792]{1,0:T(8,128)S(1)} %get-tuple-element.9.refs_0_.refs_4_, ...), custom_call_target="tpu_custom_call" | custom-call | tf_op jit(solution)/shard_map/merge_partials/pallas_call | solution.py:320
  119.7 1.6 collective-permute-start.8
  121.3 1.0 collective-permute-done.8
  122.3 7.4 %all_to_all.39 = f32[4,80,128]{2,1,0:T(8,128)S(1)} all-to-all(f32[4,80,128]{2,1,0:T(8,128)S(1)} %bitcast.25), channel_id=1, replica_groups=mesh['grp'=4,'row_0'=4,'row_1'=8,'row_2'=2] {'row_0'}, dimensions={0} | all-to-all | bytes 327680 | tf_op jit(solution)/shard_map/all_to_all | solution.py:391
  129.8 13.5 %all_to_all.40 = f32[8,80,128]{2,1,0:T(8,128)S(1)} all-to-all(f32[8,80,128]{2,1,0:T(8,128)S(1)} %broadcast_in_dim.14), channel_id=1, replica_groups=mesh['grp'=4,'row_0'=4,'row_1'=8,'row_2'=2] {'row_1'}, dimensions={0} | all-to-all | bytes 655360 | tf_op jit(solution)/shard_map/all_to_all | solution.py:396
  143.3 0.6 reduce_sum.39
  143.9 0.8 broadcast_in_dim.15
  144.7 7.5 %all_to_all.41 = f32[4,80,128]{2,1,0:T(8,128)S(1)} all-to-all(f32[4,80,128]{2,1,0:T(8,128)S(1)} %broadcast_in_dim.15), channel_id=1, replica_groups=mesh['grp'=4,'row_0'=4,'row_1'=8,'row_2'=2] {'row_0'}, dimensions={0} | all-to-all | bytes 327680 | tf_op jit(solution)/shard_map/all_to_all | solution.py:396
  152.2 4.2 %collective-permute-start.9 = (f32[320,128]{1,0:T(8,128)S(1)}, f32[320,128]{1,0:T(8,128)}, u32[]{:S(2)}, u32[]{:S(2)}) collective-permute-start(f32[320,128]{1,0:T(8,128)S(1)} %bitcast.21), channel_id=1, source_target_pairs={{0,1},{1,0},{2,3},{3,2},{4,5},{5,4},{6,7},{7,6},{8,9},{9,8},{10,11... | collective-permute-start | bytes 491528 | tf_op jit(solution)/shard_map/ppermute | solution.py:385
  156.4 0.9 copy.10
  157.3 0.2 collective-permute-done.9.refs_2_
  157.5 1.0 copy-done.2
  158.6 16.4 %finish.1 = f32[3584,128]{1,0:T(8,128)} custom-call(s32[2]{0:T(128)S(1)} %pad_add_fusion.core_ref.refs_0_.place_ref, f32[320,128]{1,0:T(8,128)S(1)} %bitcast.22, f32[320,128]{1,0:T(8,128)} %collective-permute-done.9.refs_2_, f32[4,64,64]{2,1,0:T(8,128)S(1)} %bitcast.23, f32[64,1792]{1,0:T(8,128)S(1)} %get-tuple-element.9.refs_0_.refs_4_, ...), custom_call_target="tpu_custom_call" | custom-call | tf_op jit(solution)/shard_map/finish/pallas_call | solution.py:372
  (26 shorter events, 0.6 us)
Async XLA Ops:
  8.3 52.8 %copy-start.3 = (f32[512,64]{0,1:T(8,128)S(1)}, f32[512,64]{0,1:T(8,128)}, u32[]{:S(2)}) copy-start(f32[512,64]{0,1:T(8,128)} %param.6) | copy-start | bytes 393220
  8.3 4.5 %collective-permute-start = (f32[640,128]{1,0:T(8,128)S(1)}, f32[640,128]{1,0:T(8,128)S(1)}, u32[]{:S(2)}, u32[]{:S(2)}) collective-permute-start(f32[640,128]{1,0:T(8,128)S(1)} %slice_bitcast_fusion), channel_id=1, source_target_pairs={{0,1},{1,0},{2,3},{3,2},{4,5},{5,4},{6,7},{7,6},{8,9},{9,8},{10,11... | collective-permute-start | bytes 983048 | tf_op jit(solution)/shard_map/ppermute | solution.py:385
  56.0 6.3 %collective-permute-start.1 = (f32[640,128]{1,0:T(8,128)S(1)}, f32[640,128]{1,0:T(8,128)S(1)}, u32[]{:S(2)}, u32[]{:S(2)}) collective-permute-start(f32[640,128]{1,0:T(8,128)S(1)} %bitcast.19), channel_id=1, source_target_pairs={{0,1},{1,0},{2,3},{3,2},{4,5},{5,4},{6,7},{7,6},{8,9},{9,8},{10,11... | collective-permute-start | bytes 983048 | tf_op jit(solution)/shard_map/ppermute | solution.py:385
  76.7 30.5 %copy-start = (f32[3584,128]{1,0:T(8,128)S(1)}, f32[3584,128]{1,0:T(8,128)}, u32[]{:S(2)}) copy-start(f32[3584,128]{1,0:T(8,128)} %test_ref.3) | copy-start | bytes 5505028
  82.2 12.1 %collective-permute-start.2 = (f32[64,1792]{1,0:T(8,128)S(1)}, f32[64,1792]{1,0:T(8,128)S(1)}, u32[]{:S(2)}, u32[]{:S(2)}) collective-permute-start(f32[64,1792]{1,0:T(8,128)S(1)} %get-tuple-element.9.refs_0_.refs_4_), channel_id=1, source_target_pairs={{0,192},{64,0},{128,64},{192,128},{1,193},{65,1},{129,65},{193,129... | collective-permute-start | bytes 1376264 | tf_op jit(solution)/shard_map/ppermute | solution.py:415
  84.7 12.9 %collective-permute-start.5 = (f32[64,1792]{1,0:T(8,128)S(1)}, f32[64,1792]{1,0:T(8,128)S(1)}, u32[]{:S(2)}, u32[]{:S(2)}) collective-permute-start(f32[64,1792]{1,0:T(8,128)S(1)} %get-tuple-element.10.refs_1_.refs_5_), channel_id=1, source_target_pairs={{0,64},{64,128},{128,192},{192,0},{1,65},{65,129},{129,193},{193,1... | collective-permute-start | bytes 1376264 | tf_op jit(solution)/shard_map/ppermute | solution.py:416
  84.7 22.5 %collective-permute-start.4 = (f32[64,1792]{1,0:T(8,128)S(1)}, f32[64,1792]{1,0:T(8,128)S(1)}, u32[]{:S(2)}, u32[]{:S(2)}) collective-permute-start(f32[64,1792]{1,0:T(8,128)S(1)} %get-tuple-element.9.refs_0_.refs_4_), channel_id=1, source_target_pairs={{0,64},{64,128},{128,192},{192,0},{1,65},{65,129},{129,193},{193,1... | collective-permute-start | bytes 1376264 | tf_op jit(solution)/shard_map/ppermute | solution.py:418
  84.9 22.3 %collective-permute-start.3 = (f32[64,1792]{1,0:T(8,128)S(1)}, f32[64,1792]{1,0:T(8,128)S(1)}, u32[]{:S(2)}, u32[]{:S(2)}) collective-permute-start(f32[64,1792]{1,0:T(8,128)S(1)} %get-tuple-element.10.refs_1_.refs_5_), channel_id=1, source_target_pairs={{0,192},{64,0},{128,64},{192,128},{1,193},{65,1},{129,65},{193,129... | collective-permute-start | bytes 1376264 | tf_op jit(solution)/shard_map/ppermute | solution.py:417
  94.2 19.7 %collective-permute-start.6 = (f32[64,1792]{1,0:T(8,128)S(1)}, f32[64,1792]{1,0:T(8,128)S(1)}, u32[]{:S(2)}, u32[]{:S(2)}) collective-permute-start(f32[64,1792]{1,0:T(8,128)S(1)} %collective-permute-done.2.refs_2_.refs_6_), channel_id=1, source_target_pairs={{0,192},{64,0},{128,64},{192,128},{1,193},{65,1},{129,65},{193,129... | collective-permute-start | bytes 1376264 | tf_op jit(solution)/shard_map/ppermute | solution.py:419
  97.7 19.4 %collective-permute-start.7 = (f32[64,1792]{1,0:T(8,128)S(1)}, f32[64,1792]{1,0:T(8,128)S(1)}, u32[]{:S(2)}, u32[]{:S(2)}) collective-permute-start(f32[64,1792]{1,0:T(8,128)S(1)} %collective-permute-done.5.refs_5_.refs_9_), channel_id=1, source_target_pairs={{0,64},{64,128},{128,192},{192,0},{1,65},{65,129},{129,193},{193,1... | collective-permute-start | bytes 1376264 | tf_op jit(solution)/shard_map/ppermute | solution.py:420
  117.0 2.6 %copy-start.1 = (f32[64,1792]{1,0:T(8,128)}, f32[64,1792]{1,0:T(8,128)S(1)}, u32[]{:S(2)}) copy-start(f32[64,1792]{1,0:T(8,128)S(1)} %collective-permute-done.7.refs_7_.refs_11_) | copy-start | bytes 1376260
  119.7 2.6 %collective-permute-start.8 = (f32[320,128]{1,0:T(8,128)S(1)}, f32[320,128]{1,0:T(8,128)S(1)}, u32[]{:S(2)}, u32[]{:S(2)}) collective-permute-start(f32[320,128]{1,0:T(8,128)S(1)} %slice_bitcast_fusion.2), channel_id=1, source_target_pairs={{0,1},{1,0},{2,3},{3,2},{4,5},{5,4},{6,7},{7,6},{8,9},{9,8},{10,11... | collective-permute-start | bytes 491528 | tf_op jit(solution)/shard_map/ppermute | solution.py:385
  152.2 5.3 %collective-permute-start.9 = (f32[320,128]{1,0:T(8,128)S(1)}, f32[320,128]{1,0:T(8,128)}, u32[]{:S(2)}, u32[]{:S(2)}) collective-permute-start(f32[320,128]{1,0:T(8,128)S(1)} %bitcast.21), channel_id=1, source_target_pairs={{0,1},{1,0},{2,3},{3,2},{4,5},{5,4},{6,7},{7,6},{8,9},{9,8},{10,11... | collective-permute-start | bytes 491528 | tf_op jit(solution)/shard_map/ppermute | solution.py:385
  157.5 1.0 copy-start.2

commit v4 on v3

--- a/solution.py
+++ b/solution.py
@@ -12,6 +12,7 @@
 CORE = "row_2"
 BLOCK = 128
 SHIFTS = (0, 1, 3, 2)
+HBM = pl.BlockSpec(memory_space=pltpu.HBM)
 VMEM = pl.BlockSpec(memory_space=pltpu.VMEM)
 SMEM = pl.BlockSpec(memory_space=pltpu.SMEM)
 
@@ -122,11 +123,11 @@
     for n, copy in enumerate(copies):
         copy.wait()
         high, low = parts(held_ref[n], 2)
-        high_t, low_t = high.T, low.T
+        high_t = high.T
         found = [
-            dot(high_t[left], high[:, left], NN) + dot(low_t[left], low[:, left], NN),
-            dot(high_t[left], high[:, right], NN) + dot(low_t[left], low[:, right], NN),
-            dot(high_t[right], high[:, right], NN) + dot(low_t[right], low[:, right], NN),
+            dot(high_t[left], high[:, left], NN),
+            dot(high_t[left], high[:, right], NN),
+            dot(high_t[right], high[:, right], NN),
             dot(high_t[left], low[:, left], NN),
             dot(high_t[left], low[:, right], NN),
             dot(high_t[right], low[:, left], NN),
@@ -149,7 +150,7 @@
     held = len(upper_pairs(width // BLOCK)) // 2 * BLOCK
     return pl.pallas_call(
         gram_kernel,
-        in_specs=[SMEM, pl.BlockSpec(memory_space=pl.ANY)],
+        in_specs=[SMEM, HBM],
         out_specs=VMEM,
         out_shape=jax.ShapeDtypeStruct((2, held, BLOCK), jnp.float32),
         scratch_shapes=[
@@ -214,41 +215,36 @@
     )(core, mine, other, start)
 
 
-def basis_kernel(q_ref, x_ref, near_ref, far_ref):
-    step = pl.program_id(0)
-    half = pl.num_programs(0) // 2
-    found = dot_parts(parts(q_ref[...], 2), parts(x_ref[...], 2), NT)
-
-    @pl.when(step < half)
-    def _():
-        near_ref[...] = found
-
-    @pl.when(step >= half)
-    def _():
-        far_ref[...] = found
-
-
-def group_basis(basis, snapshots):
-    rank, width = basis.shape
+def group_basis(basis, snapshots, half):
+    rank = basis.shape[0]
     rows = snapshots.shape[0]
-    steps = 4
-    deep = rows // steps
-    half = steps // 2
-    return pl.pallas_call(
-        basis_kernel,
-        grid=(steps,),
-        in_specs=[
-            pl.BlockSpec((rank, width), lambda i: (0, 0)),
-            pl.BlockSpec((deep, width), lambda i: (i, 0)),
+    deep = rows // 4
+
+    def kernel(q_ref, x_ref, o_ref, held_ref, arrived):
+        copies = [
+            pltpu.make_async_copy(
+                x_ref.at[pl.ds((half * 2 + n) * deep, deep), :], held_ref.at[n], arrived.at[n]
+            )
+            for n in range(2)
+        ]
+        for copy in copies:
+            copy.start()
+        left = parts(q_ref[...], 2)
+        for n, copy in enumerate(copies):
+            copy.wait()
+            right = parts(held_ref[n], 2)
+            o_ref[:, n * deep : (n + 1) * deep] = dot_parts(left, right, NT)
+
+    return pl.pallas_call(
+        kernel,
+        in_specs=[VMEM, HBM],
+        out_specs=VMEM,
+        out_shape=jax.ShapeDtypeStruct((rank, rows // 2), jnp.float32),
+        scratch_shapes=[
+            pltpu.VMEM((2, deep, snapshots.shape[1]), jnp.float32),
+            pltpu.SemaphoreType.DMA((2,)),
         ],
-        out_specs=[
-            pl.BlockSpec((rank, deep), lambda i: (0, jnp.minimum(i, half - 1))),
-            pl.BlockSpec((rank, deep), lambda i: (0, jnp.maximum(i - half, 0))),
-        ],
-        out_shape=[jax.ShapeDtypeStruct((rank, rows // 2), jnp.float32)] * 2,
-        compiler_params=pltpu.CompilerParams(
-            dimension_semantics=("arbitrary",), vmem_limit_bytes=48 * 2**20
-        ),
+        compiler_params=pltpu.CompilerParams(vmem_limit_bytes=48 * 2**20),
         name="group_basis",
     )(basis, snapshots)
 
@@ -282,20 +278,22 @@
             jax.ShapeDtypeStruct((wide, wide), jnp.float32),
             jax.ShapeDtypeStruct((wide, BLOCK), jnp.float32),
         ],
-        compiler_params=pltpu.CompilerParams(vmem_limit_bytes=48 * 2**20),
+        compiler_params=pltpu.CompilerParams(vmem_limit_bytes=28 * 2**20),
         name="merge_near",
     )(test_block, *joined)
 
 
 def merge_kernel(place_ref, merged_ref, side_ref, test_ref, *refs):
-    *joined_refs, o_ref = refs
-    half = joined_refs[0].shape[1]
-    rank = joined_refs[0].shape[0]
+    *all_refs, o_ref = refs
+    joined_refs, across_refs = all_refs[:-4], all_refs[-4:]
+    rank, deep = across_refs[0].shape
     cross, last = None, None
-    for h in range(2):
-        left = parts(stacked(joined_refs, h), 2)
+    for n in range(4):
+        here = slice(n % 2 * deep, (n % 2 + 1) * deep)
+        pieces = [ref[:, here] for ref in joined_refs[n // 2 :: 2]] + [across_refs[n][...]]
+        left = parts(jnp.concatenate(pieces, axis=0), 2)
         across = [piece[-rank:] for piece in left]
-        right = parts(test_ref[h * half : (h + 1) * half, :], 2)
+        right = parts(test_ref[n * deep : (n + 1) * deep, :], 2)
         own = dot_parts(left, across, NT)
         other = dot_parts(across, right, NN)
         cross = own if cross is None else cross + own
@@ -316,15 +314,15 @@
         o_ref[(n // 5) ^ place_ref[0], (n % 5) * 64 : (n % 5 + 1) * 64, :] = piece
 
 
-def merge_partials(place, joined, test_block):
+def merge_partials(place, joined, across, test_block):
     return pl.pallas_call(
         merge_kernel,
-        in_specs=[SMEM] + [VMEM] * (3 + len(joined)),
+        in_specs=[SMEM] + [VMEM] * (3 + len(joined) + len(across)),
         out_specs=VMEM,
         out_shape=jax.ShapeDtypeStruct((2, 320, BLOCK), jnp.float32),
-        compiler_params=pltpu.CompilerParams(vmem_limit_bytes=48 * 2**20),
+        compiler_params=pltpu.CompilerParams(vmem_limit_bytes=28 * 2**20),
         name="merge_partials",
-    )(place, *merge_near(joined[:-2], test_block), test_block, *joined)
+    )(place, *merge_near(joined, test_block), test_block, *joined, *across)
 
 
 def finish_kernel(row_total, place_ref, mine_ref, other_ref, start_ref, *refs):
@@ -357,28 +355,29 @@
     test_coeffs = dot_parts(parts(coef, 3), parts(side, 3), NN)
     weight = dot_parts(parts(coef.T, 3), parts(test_coeffs, 3), NN) / row_total
     weight = parts(weight.T, 2)
-    half = joined_refs[0].shape[1]
-    deep = half // 2
+    across_refs = joined_refs[-4:]
+    deep = across_refs[0].shape[1]
     for n in range(4):
         here = slice(n % 2 * deep, (n % 2 + 1) * deep)
-        joined = jnp.concatenate([r[:, here] for r in joined_refs[n // 2 :: 2]], axis=0)
+        bases = [ref[:, here] for ref in joined_refs[:-4][n // 2 :: 2]] + [across_refs[n][...]]
+        joined = jnp.concatenate(bases, axis=0)
         o_ref[n * deep : (n + 1) * deep, :] = dot_parts(weight, parts(joined, 2), NN).T
 
 
-def finish(place, mine, other, start, joined, row_total):
+def finish(place, mine, other, start, joined, across, row_total):
     rank = start.shape[-1]
     wide = start.shape[0] * start.shape[1]
     rows = 2 * joined[0].shape[1]
     return pl.pallas_call(
         lambda *refs: finish_kernel(row_total, *refs),
-        in_specs=[SMEM] + [VMEM] * (3 + len(joined)),
+        in_specs=[SMEM] + [VMEM] * (3 + len(joined) + len(across)),
         out_specs=VMEM,
         out_shape=jax.ShapeDtypeStruct((rows, BLOCK), jnp.float32),
         scratch_shapes=[pltpu.VMEM((rank, wide), jnp.float32)]
         + [pltpu.VMEM((wide, wide), jnp.bfloat16)] * 3,
-        compiler_params=pltpu.CompilerParams(vmem_limit_bytes=48 * 2**20),
+        compiler_params=pltpu.CompilerParams(vmem_limit_bytes=28 * 2**20),
         name="finish",
-    )(place, mine, other, start, *joined)
+    )(place, mine, other, start, *joined, *across)
 
 
 def swap_cores(array):
@@ -396,15 +395,14 @@
     return lax.all_to_all(copies, axis, 0, 0, tiled=True)
 
 
-def sum_over_rows(halves):
-    near, far = CHIPS
+def sum_over_rows(halves, staged):
     kept = halves[0] + swap_cores(halves[1])
-    own = reduced(kept, near)
-    if own.shape[0] > 100:
-        own = spread(reduced(own, far), far).reshape(own.shape)
+    if staged:
+        near, far = CHIPS
+        mine = spread(jnp.sum(spread(reduced(kept, near), far), axis=0), near)
     else:
-        own = jnp.sum(spread(own, far), axis=0)
-    mine = spread(own, near).reshape(kept.shape)
+        mine = spread(reduced(kept, CHIPS), CHIPS)
+    mine = mine.reshape(kept.shape)
     return mine, swap_cores(mine)
 
 
@@ -412,25 +410,30 @@
     groups = lax.axis_size("grp")
     down = [(i, (i - 1) % groups) for i in range(groups)]
     up = [(i, (i + 1) % groups) for i in range(groups)]
+    half = near.shape[1] // 2
     next_near = lax.ppermute(near, "grp", down)
+    last_near = lax.ppermute(near, "grp", up)
+    next_far = lax.ppermute(far, "grp", down)
     last_far = lax.ppermute(far, "grp", up)
-    next_far = lax.ppermute(far, "grp", down)
-    last_near = lax.ppermute(near, "grp", up)
-    across_near = lax.ppermute(next_near, "grp", down)
-    across_far = lax.ppermute(last_far, "grp", up)
-    return [near, far, next_near, next_far, last_near, last_far, across_near, across_far]
+    across = [
+        lax.ppermute(next_near[:, :half], "grp", down),
+        lax.ppermute(last_near[:, half:], "grp", up),
+        lax.ppermute(next_far[:, :half], "grp", down),
+        lax.ppermute(last_far[:, half:], "grp", up),
+    ]
+    return [near, far, next_near, next_far, last_near, last_far], across
 
 
 def on_device(snapshots, test_block, start_block, start_merge):
     row_total = snapshots.shape[0] * lax.axis_size(ROW)
     place = jnp.stack([lax.axis_index(CORE), lax.axis_index("grp")])
     groups = lax.axis_size("grp")
-    mine, other = sum_over_rows(gram(snapshots, place))
+    mine, other = sum_over_rows(gram(snapshots, place), False)
     basis = group_solve(place, mine, other, start_block, row_total)
-    joined = gathered_bases(*group_basis(basis, snapshots))
-    mine, other = sum_over_rows(merge_partials(place, joined, test_block))
+    joined, across = gathered_bases(*[group_basis(basis, snapshots, h) for h in range(2)])
+    mine, other = sum_over_rows(merge_partials(place, joined, across, test_block), True)
     start = start_merge.reshape(groups, start_merge.shape[0] // groups, start_merge.shape[1])
-    return finish(place, mine, other, start, joined, row_total)
+    return finish(place, mine, other, start, joined, across, row_total)
 
 
 def solution(mesh):

time: 176 us -> 170 us (0.966)
  waiting for transfers between devices: 27.5 us -> 19.8 us
  starting transfers between devices: 22.8 us -> 25 us
    ppermute x1, waiting for transfers between devices: 0.01 us -> 6.96 us  [gathered_bases(): last_far = lax.ppermute(far, 'grp', up)]
    ppermute x1, waiting for transfers between devices: 6.81 us -> 0.01 us  [gathered_bases(): next_near = lax.ppermute(near, 'grp', down)]
    ppermute x1, waiting for transfers between devices: 9.54 us -> 4.25 us  [gathered_bases(): last_near = lax.ppermute(near, 'grp', up)]
    ppermute x2 -> x4, waiting for transfers between devices: 7.47 us -> 4.59 us  [the longest x1 4.58 us: gathered_bases(): lax.ppermute(last_far[:, half:], 'grp', up)]
    all_to_all x3 -> x2, blocking collectives: 32.1 us -> 29.4 us  [reduced(): return jnp.sum(lax.all_to_all(cuts, axis, 0, 0, tiled=True), axis=0)]
    ppermute x2 -> x4, starting transfers between devices: 3.41 us -> 5.62 us  [the longest x1 2.73 us: gathered_bases(): lax.ppermute(next_near[:, :half], 'grp', down)]
    all_to_all x4 -> x3, blocking collectives: 39.3 us -> 40.7 us  [spread(): return lax.all_to_all(copies, axis, 0, 0, tiled=True)]
    pallas_call x3 -> x4, Pallas kernels: 16.3 us -> 16 us  [the longest x1 7.13 us: gram(): pl.pallas_call(gram_kernel, in_specs=[SMEM, HBM], out_specs=VMEM, out_sha...]
  transfers between devices with their start and end apart: 10 -> 12, of which waited for: 8 -> 7; matrix products, arithmetic and copies ran while one was open for 1% -> 1% of each run, Pallas kernels for 1% -> 3%
where the time goes in v4:
time: 170 us; the launch traced here: 169 us
  blocking collectives  70 us (41%)
  Pallas kernels  49.1 us (29%)
  starting transfers between devices  25 us (15%)
  waiting for transfers between devices  19.8 us (12%)
  local copies, waits for them, and re-layouts  2.95 us (2%)
  other arithmetic  2.1 us (1%)
    all_to_all x3, blocking collectives, spread(): return lax.all_to_all(copies, axis, 0, 0, tiled=True)  40.7 us
    all_to_all x2, blocking collectives, reduced(): return jnp.sum(lax.all_to_all(cuts, axis, 0, 0, tiled=True), axis=0)  29.4 us
    pallas_call x1, Pallas kernels, finish(): pl.pallas_call(lambda *refs: finish_kernel(row_total, *refs), in_specs=[S...  16.5 us
    pallas_call x1, Pallas kernels, group_solve(): pl.pallas_call(lambda *refs: solve_kernel(row_total, *refs), in_specs=[SM...  14.3 us
    ppermute x4, starting transfers between devices, swap_cores(): return lax.ppermute(array, CORE, [(0, 1), (1, 0)])  13.8 us
    pallas_call x1, Pallas kernels, gram(): pl.pallas_call(gram_kernel, in_specs=[SMEM, HBM], out_specs=VMEM, out_sha...  7.13 us
    ppermute x1, waiting for transfers between devices, gathered_bases(): last_far = lax.ppermute(far, 'grp', up)  6.96 us
    pallas_call x2, Pallas kernels, group_basis(): pl.pallas_call(kernel, in_specs=[VMEM, HBM], out_specs=VMEM, out_shape=ja...  6.18 us
  transfers between devices with their start and end apart: 12, of which 7 were waited for; matrix products, arithmetic and copies ran while one was open for 1% of the time, Pallas kernels for 3%

profile of v4, /device:TPU:1, one launch (start us, length us, event | category | flops | bytes accessed | tf_op | source)
XLA Modules:
  0.0 169.3 jit_solution(9294426587192126774)
XLA Ops:
  0.1 7.1 %gram.1 = f32[2,640,128]{2,1,0:T(8,128)S(1)} custom-call(s32[2]{0:T(128)S(1)} %pad_add_fusion.core_ref.refs_0_.place_ref, f32[3584,512]{1,0:T(8,128)} %x_ref.5), custom_call_target="tpu_custom_call" | custom-call | tf_op jit(solution)/shard_map/gram/pallas_call | solution.py:151
  7.2 3.3 %collective-permute-start = (f32[640,128]{1,0:T(8,128)S(1)}, f32[640,128]{1,0:T(8,128)S(1)}, u32[]{:S(2)}, u32[]{:S(2)}) collective-permute-start(f32[640,128]{1,0:T(8,128)S(1)} %slice_bitcast_fusion), channel_id=1, source_target_pairs={{0,1},{1,0},{2,3},{3,2},{4,5},{5,4},{6,7},{7,6},{8,9},{9,8},{10,11... | collective-permute-start | bytes 983048 | tf_op jit(solution)/shard_map/ppermute | solution.py:384
  10.5 1.3 collective-permute-done
  11.9 21.3 %all_to_all.25 = f32[32,20,128]{2,1,0:T(8,128)S(1)} all-to-all(f32[32,20,128]{2,1,0:T(8,128)S(1)} %reshape.15), channel_id=1, replica_groups=mesh['grp'=4,'row_0'=4,'row_1'=8,'row_2'=2] {'row_0','row_1'}, dimensions={0} | all-to-all | bytes 655360 | tf_op jit(solution)/shard_map/all_to_all | solution.py:390
  33.2 18.3 %all_to_all.26 = f32[32,20,128]{2,1,0:T(8,128)S(1)} all-to-all(f32[32,20,128]{2,1,0:T(8,128)S(1)} %broadcast_in_dim.9), channel_id=1, replica_groups=mesh['grp'=4,'row_0'=4,'row_1'=8,'row_2'=2] {'row_0','row_1'}, dimensions={0} | all-to-all | bytes 655360 | tf_op jit(solution)/shard_map/all_to_all | solution.py:395
  51.5 4.6 %collective-permute-start.1 = (f32[640,128]{1,0:T(8,128)S(1)}, f32[640,128]{1,0:T(8,128)S(1)}, u32[]{:S(2)}, u32[]{:S(2)}) collective-permute-start(f32[640,128]{1,0:T(8,128)S(1)} %reshape.16.refs_1_), channel_id=1, source_target_pairs={{0,1},{1,0},{2,3},{3,2},{4,5},{5,4},{6,7},{7,6},{8,9},{9,8},{10,11... | collective-permute-start | bytes 983048 | tf_op jit(solution)/shard_map/ppermute | solution.py:384
  56.3 1.1 collective-permute-done.1.refs_2_
  57.4 14.3 %group_solve.1.q_ref = f32[64,512]{1,0:T(8,128)S(1)} custom-call(s32[2]{0:T(128)S(1)} %pad_add_fusion.core_ref.refs_0_.place_ref, f32[640,128]{1,0:T(8,128)S(1)} %reshape.16.refs_1_, f32[640,128]{1,0:T(8,128)S(1)} %collective-permute-done.1.refs_2_, f32[512,64]{1,0:T(8,128)S(1)} %copy.9.refs_3_), custom_call_target="tpu_custom_call" | custom-call | tf_op jit(solution)/shard_map/group_solve/pallas_call | solution.py:206
  71.7 3.0 %group_basis.2.refs_0_.refs_4_ = f32[64,1792]{1,0:T(8,128)S(1)} custom-call(f32[64,512]{1,0:T(8,128)S(1)} %group_solve.1.q_ref, f32[3584,512]{1,0:T(8,128)} %x_ref.5), custom_call_target="tpu_custom_call" | custom-call | tf_op jit(solution)/shard_map/group_basis/pallas_call | solution.py:238
  74.7 1.3 collective-permute-start.4
  76.0 1.5 collective-permute-start.2
  77.6 3.2 %group_basis.3.refs_1_.refs_5_ = f32[64,1792]{1,0:T(8,128)S(1)} custom-call(f32[64,512]{1,0:T(8,128)S(1)} %group_solve.1.q_ref, f32[3584,512]{1,0:T(8,128)} %x_ref.5), custom_call_target="tpu_custom_call" | custom-call | tf_op jit(solution)/shard_map/group_basis/pallas_call | solution.py:238
  80.8 2.7 %collective-permute-start.3 = (f32[64,1792]{1,0:T(8,128)S(1)}, f32[64,1792]{1,0:T(8,128)S(1)}, u32[]{:S(2)}, u32[]{:S(2)}) collective-permute-start(f32[64,1792]{1,0:T(8,128)S(1)} %group_basis.3.refs_1_.refs_5_), channel_id=1, source_target_pairs={{0,192},{64,0},{128,64},{192,128},{1,193},{65,1},{129,65},{193,129... | collective-permute-start | bytes 1376264 | tf_op jit(solution)/shard_map/ppermute | solution.py:416
  83.5 4.3 %collective-permute-done.4.refs_4_.refs_8_ = f32[64,1792]{1,0:T(8,128)S(1)} collective-permute-done((f32[64,1792]{1,0:T(8,128)S(1)}, f32[64,1792]{1,0:T(8,128)S(1)}, u32[]{:S(2)}, u32[]{:S(2)}) %collective-permute-start.4) | collective-permute-done | bytes 458784 | tf_op jit(solution)/shard_map/ppermute | solution.py:415
  87.9 2.7 %collective-permute-start.6 = (f32[64,896]{1,0:T(8,128)S(1)}, f32[64,896]{1,0:T(8,128)S(1)}, u32[]{:S(2)}, u32[]{:S(2)}) collective-permute-start(f32[64,896]{1,0:T(8,128)S(1)} %slice.34), channel_id=1, source_target_pairs={{0,192},{64,0},{128,64},{192,128},{1,193},{65,1},{129,65},{193,129... | collective-permute-start | bytes 688136 | tf_op jit(solution)/shard_map/ppermute | solution.py:419
  90.6 7.0 %collective-permute-done.5.refs_5_.refs_9_ = f32[64,1792]{1,0:T(8,128)S(1)} collective-permute-done((f32[64,1792]{1,0:T(8,128)S(1)}, f32[64,1792]{1,0:T(8,128)S(1)}, u32[]{:S(2)}, u32[]{:S(2)}) %collective-permute-start.5) | collective-permute-done | bytes 458784 | tf_op jit(solution)/shard_map/ppermute | solution.py:417
  97.7 2.7 %collective-permute-start.8 = (f32[64,896]{1,0:T(8,128)S(1)}, f32[64,896]{1,0:T(8,128)S(1)}, u32[]{:S(2)}, u32[]{:S(2)}) collective-permute-start(f32[64,896]{1,0:T(8,128)S(1)} %slice.36), channel_id=1, source_target_pairs={{0,192},{64,0},{128,64},{192,128},{1,193},{65,1},{129,65},{193,129... | collective-permute-start | bytes 688136 | tf_op jit(solution)/shard_map/ppermute | solution.py:421
  100.4 2.3 %merge_near.1 = (f32[192,192]{1,0:T(8,128)S(1)}, f32[192,128]{1,0:T(8,128)S(1)}) custom-call(f32[3584,128]{1,0:T(8,128)S(1)} %copy-done, f32[64,1792]{1,0:T(8,128)S(1)} %group_basis.2.refs_0_.refs_4_, f32[64,1792]{1,0:T(8,128)S(1)} %group_basis.3.refs_1_.refs_5_, f32[64,1792]{1,0:T(8,128)S(1)} %collective-permute-done.2.refs_2_.refs_6_, ...), custom_call_target="tpu_custom_call" | custom-call | tf_op jit(solution)/shard_map/merge_near/pallas_call | solution.py:273
  102.8 4.6 %collective-permute-done.9.refs_9_.refs_13_ = f32[64,896]{1,0:T(8,128)S(1)} collective-permute-done((f32[64,896]{1,0:T(8,128)S(1)}, f32[64,896]{1,0:T(8,128)S(1)}, u32[]{:S(2)}, u32[]{:S(2)}) %collective-permute-start.9) | collective-permute-done | bytes 229408 | tf_op jit(solution)/shard_map/ppermute | solution.py:422
  107.4 2.7 %merge_partials.1 = f32[2,320,128]{2,1,0:T(8,128)S(1)} custom-call(s32[2]{0:T(128)S(1)} %pad_add_fusion.core_ref.refs_0_.place_ref, f32[192,192]{1,0:T(8,128)S(1)} %get-tuple-element.7.merged_ref, f32[192,128]{1,0:T(8,128)S(1)} %get-tuple-element.8.side_ref, f32[3584,128]{1,0:T(8,128)S(1)} %copy-done, f32[64,1792]{1,0:T(8,128)S(1)} %group_basis.2.refs_0_.refs_4_, ...), custom_call_target="tpu_custom_call" | custom-call | tf_op jit(solution)/shard_map/merge_partials/pallas_call | solution.py:318
  110.1 1.3 collective-permute-start.10
  111.4 1.0 collective-permute-done.10
  112.5 8.1 %all_to_all.27 = f32[4,80,128]{2,1,0:T(8,128)} all-to-all(f32[4,80,128]{2,1,0:T(8,128)S(1)} %bitcast.18), channel_id=1, replica_groups=mesh['grp'=4,'row_0'=4,'row_1'=8,'row_2'=2] {'row_0'}, dimensions={0} | all-to-all | bytes 327680 | tf_op jit(solution)/shard_map/all_to_all | solution.py:390
  120.6 0.9 reduce_sum.28
  121.5 14.3 %all_to_all.28 = f32[8,80,128]{2,1,0:T(8,128)} all-to-all(f32[8,80,128]{2,1,0:T(8,128)S(1)} %broadcast_in_dim.10), channel_id=1, replica_groups=mesh['grp'=4,'row_0'=4,'row_1'=8,'row_2'=2] {'row_1'}, dimensions={0} | all-to-all | bytes 655360 | tf_op jit(solution)/shard_map/all_to_all | solution.py:395
  135.9 1.0 reduce_sum.29
  136.9 8.1 %all_to_all.29 = f32[4,80,128]{2,1,0:T(8,128)} all-to-all(f32[4,80,128]{2,1,0:T(8,128)S(1)} %broadcast_in_dim.11), channel_id=1, replica_groups=mesh['grp'=4,'row_0'=4,'row_1'=8,'row_2'=2] {'row_0'}, dimensions={0} | all-to-all | bytes 327680 | tf_op jit(solution)/shard_map/all_to_all | solution.py:395
  145.0 4.6 %collective-permute-start.11 = (f32[320,128]{1,0:T(8,128)}, f32[320,128]{1,0:T(8,128)}, u32[]{:S(2)}, u32[]{:S(2)}) collective-permute-start(f32[320,128]{1,0:T(8,128)} %bitcast.7.refs_1_), channel_id=1, source_target_pairs={{0,1},{1,0},{2,3},{3,2},{4,5},{5,4},{6,7},{7,6},{8,9},{9,8},{10,11... | collective-permute-start | bytes 491528 | tf_op jit(solution)/shard_map/ppermute | solution.py:384
  149.6 0.8 copy.10
  150.9 0.9 copy-done.2
  151.9 0.9 copy-done.3
  152.8 16.5 %finish.1 = f32[3584,128]{1,0:T(8,128)} custom-call(s32[2]{0:T(128)S(1)} %pad_add_fusion.core_ref.refs_0_.place_ref, f32[320,128]{1,0:T(8,128)} %bitcast.7.refs_1_, f32[320,128]{1,0:T(8,128)} %collective-permute-done.11.refs_2_, f32[4,64,64]{2,1,0:T(8,128)S(1)} %bitcast.17, f32[64,1792]{1,0:T(8,128)S(1)} %group_basis.2.refs_0_.refs_4_, ...), custom_call_target="tpu_custom_call" | custom-call | tf_op jit(solution)/shard_map/finish/pallas_call | solution.py:371
  (35 shorter events, 1.4 us)
Async XLA Ops:
  7.2 4.6 %collective-permute-start = (f32[640,128]{1,0:T(8,128)S(1)}, f32[640,128]{1,0:T(8,128)S(1)}, u32[]{:S(2)}, u32[]{:S(2)}) collective-permute-start(f32[640,128]{1,0:T(8,128)S(1)} %slice_bitcast_fusion), channel_id=1, source_target_pairs={{0,1},{1,0},{2,3},{3,2},{4,5},{5,4},{6,7},{7,6},{8,9},{9,8},{10,11... | collective-permute-start | bytes 983048 | tf_op jit(solution)/shard_map/ppermute | solution.py:384
  11.8 44.3 %copy-start.4 = (f32[512,64]{0,1:T(8,128)S(1)}, f32[512,64]{0,1:T(8,128)}, u32[]{:S(2)}) copy-start(f32[512,64]{0,1:T(8,128)} %param.6) | copy-start | bytes 393220
  51.5 5.9 %collective-permute-start.1 = (f32[640,128]{1,0:T(8,128)S(1)}, f32[640,128]{1,0:T(8,128)S(1)}, u32[]{:S(2)}, u32[]{:S(2)}) collective-permute-start(f32[640,128]{1,0:T(8,128)S(1)} %reshape.16.refs_1_), channel_id=1, source_target_pairs={{0,1},{1,0},{2,3},{3,2},{4,5},{5,4},{6,7},{7,6},{8,9},{9,8},{10,11... | collective-permute-start | bytes 983048 | tf_op jit(solution)/shard_map/ppermute | solution.py:384
  74.7 13.0 %collective-permute-start.4 = (f32[64,1792]{1,0:T(8,128)S(1)}, f32[64,1792]{1,0:T(8,128)S(1)}, u32[]{:S(2)}, u32[]{:S(2)}) collective-permute-start(f32[64,1792]{1,0:T(8,128)S(1)} %group_basis.2.refs_0_.refs_4_), channel_id=1, source_target_pairs={{0,64},{64,128},{128,192},{192,0},{1,65},{65,129},{129,193},{193,1... | collective-permute-start | bytes 1376264 | tf_op jit(solution)/shard_map/ppermute | solution.py:415
  76.0 11.8 %collective-permute-start.2 = (f32[64,1792]{1,0:T(8,128)S(1)}, f32[64,1792]{1,0:T(8,128)S(1)}, u32[]{:S(2)}, u32[]{:S(2)}) collective-permute-start(f32[64,1792]{1,0:T(8,128)S(1)} %group_basis.2.refs_0_.refs_4_), channel_id=1, source_target_pairs={{0,192},{64,0},{128,64},{192,128},{1,193},{65,1},{129,65},{193,129... | collective-permute-start | bytes 1376264 | tf_op jit(solution)/shard_map/ppermute | solution.py:414
  77.6 22.9 %copy-start = (f32[3584,128]{1,0:T(8,128)S(1)}, f32[3584,128]{1,0:T(8,128)}, u32[]{:S(2)}) copy-start(f32[3584,128]{1,0:T(8,128)} %test_ref.3) | copy-start | bytes 5505028
  80.7 16.8 %collective-permute-start.5 = (f32[64,1792]{1,0:T(8,128)S(1)}, f32[64,1792]{1,0:T(8,128)S(1)}, u32[]{:S(2)}, u32[]{:S(2)}) collective-permute-start(f32[64,1792]{1,0:T(8,128)S(1)} %group_basis.3.refs_1_.refs_5_), channel_id=1, source_target_pairs={{0,64},{64,128},{128,192},{192,0},{1,65},{65,129},{129,193},{193,1... | collective-permute-start | bytes 1376264 | tf_op jit(solution)/shard_map/ppermute | solution.py:417
  80.8 16.9 %collective-permute-start.3 = (f32[64,1792]{1,0:T(8,128)S(1)}, f32[64,1792]{1,0:T(8,128)S(1)}, u32[]{:S(2)}, u32[]{:S(2)}) collective-permute-start(f32[64,1792]{1,0:T(8,128)S(1)} %group_basis.3.refs_1_.refs_5_), channel_id=1, source_target_pairs={{0,192},{64,0},{128,64},{192,128},{1,193},{65,1},{129,65},{193,129... | collective-permute-start | bytes 1376264 | tf_op jit(solution)/shard_map/ppermute | solution.py:416
  87.8 15.0 %collective-permute-start.7 = (f32[64,896]{1,0:T(8,128)S(1)}, f32[64,896]{1,0:T(8,128)S(1)}, u32[]{:S(2)}, u32[]{:S(2)}) collective-permute-start(f32[64,896]{1,0:T(8,128)S(1)} %slice.35), channel_id=1, source_target_pairs={{0,64},{64,128},{128,192},{192,0},{1,65},{65,129},{129,193},{193,1... | collective-permute-start | bytes 688136 | tf_op jit(solution)/shard_map/ppermute | solution.py:420
  87.9 14.9 %collective-permute-start.6 = (f32[64,896]{1,0:T(8,128)S(1)}, f32[64,896]{1,0:T(8,128)S(1)}, u32[]{:S(2)}, u32[]{:S(2)}) collective-permute-start(f32[64,896]{1,0:T(8,128)S(1)} %slice.34), channel_id=1, source_target_pairs={{0,192},{64,0},{128,64},{192,128},{1,193},{65,1},{129,65},{193,129... | collective-permute-start | bytes 688136 | tf_op jit(solution)/shard_map/ppermute | solution.py:419
  97.6 9.8 %collective-permute-start.9 = (f32[64,896]{1,0:T(8,128)S(1)}, f32[64,896]{1,0:T(8,128)S(1)}, u32[]{:S(2)}, u32[]{:S(2)}) collective-permute-start(f32[64,896]{1,0:T(8,128)S(1)} %slice.37), channel_id=1, source_target_pairs={{0,64},{64,128},{128,192},{192,0},{1,65},{65,129},{129,193},{193,1... | collective-permute-start | bytes 688136 | tf_op jit(solution)/shard_map/ppermute | solution.py:422
  97.7 9.7 %collective-permute-start.8 = (f32[64,896]{1,0:T(8,128)S(1)}, f32[64,896]{1,0:T(8,128)S(1)}, u32[]{:S(2)}, u32[]{:S(2)}) collective-permute-start(f32[64,896]{1,0:T(8,128)S(1)} %slice.36), channel_id=1, source_target_pairs={{0,192},{64,0},{128,64},{192,128},{1,193},{65,1},{129,65},{193,129... | collective-permute-start | bytes 688136 | tf_op jit(solution)/shard_map/ppermute | solution.py:421
  107.4 2.7 %copy-start.1 = (f32[64,896]{1,0:T(8,128)}, f32[64,896]{1,0:T(8,128)S(1)}, u32[]{:S(2)}) copy-start(f32[64,896]{1,0:T(8,128)S(1)} %collective-permute-done.8.refs_8_.refs_12_) | copy-start | bytes 688132
  110.1 39.5 %copy-start.5 = (f32[256,64]{0,1:T(8,128)S(1)}, f32[256,64]{0,1:T(8,128)}, u32[]{:S(2)}) copy-start(f32[256,64]{0,1:T(8,128)} %param.7) | copy-start | bytes 196612
  110.1 2.3 %collective-permute-start.10 = (f32[320,128]{1,0:T(8,128)S(1)}, f32[320,128]{1,0:T(8,128)S(1)}, u32[]{:S(2)}, u32[]{:S(2)}) collective-permute-start(f32[320,128]{1,0:T(8,128)S(1)} %slice_bitcast_fusion.2), channel_id=1, source_target_pairs={{0,1},{1,0},{2,3},{3,2},{4,5},{5,4},{6,7},{7,6},{8,9},{9,8},{10,11... | collective-permute-start | bytes 491528 | tf_op jit(solution)/shard_map/ppermute | solution.py:384
  145.0 6.0 %collective-permute-start.11 = (f32[320,128]{1,0:T(8,128)}, f32[320,128]{1,0:T(8,128)}, u32[]{:S(2)}, u32[]{:S(2)}) collective-permute-start(f32[320,128]{1,0:T(8,128)} %bitcast.7.refs_1_), channel_id=1, source_target_pairs={{0,1},{1,0},{2,3},{3,2},{4,5},{5,4},{6,7},{7,6},{8,9},{9,8},{10,11... | collective-permute-start | bytes 491528 | tf_op jit(solution)/shard_map/ppermute | solution.py:384
  150.9 0.9 copy-start.2
  151.9 0.9 copy-start.3

commit v5 on v4

--- a/solution.py
+++ b/solution.py
@@ -191,7 +191,7 @@
         if a != b:
             for ref, piece in zip(gram_refs, parts(block.T, 3)):
                 ref[cut(b), cut(a)] = piece
-    next_ref[...] = start_ref[...].T
+    next_ref[...] = start_ref[...]
 
     def step(index, carry):
         next_ref[...] = normalised(*sweep(next_ref[...], gram_refs))
@@ -202,7 +202,7 @@
 
 
 def group_solve(core, mine, other, start, row_total):
-    width, rank = start.shape
+    rank, width = start.shape
     return pl.pallas_call(
         lambda *refs: solve_kernel(row_total, *refs),
         in_specs=[SMEM, VMEM, VMEM, VMEM],
@@ -253,8 +253,27 @@
     return jnp.concatenate([ref[...] for ref in refs[h::2]], axis=0)
 
 
+def across_products(joined_refs, across_refs, test_ref, h):
+    rank, deep = across_refs[0].shape
+    cross, last = None, None
+    for n in range(2):
+        here = slice(n * deep, (n + 1) * deep)
+        pieces = [ref[:, here] for ref in joined_refs[h::2]] + [across_refs[2 * h + n][...]]
+        left = parts(jnp.concatenate(pieces, axis=0), 2)
+        across = [piece[-rank:] for piece in left]
+        first = (2 * h + n) * deep
+        right = parts(test_ref[first : first + deep, :], 2)
+        own = dot_parts(left, across, NT)
+        other = dot_parts(across, right, NN)
+        cross = own if cross is None else cross + own
+        last = other if last is None else last + other
+    return cross, last
+
+
 def merge_near_kernel(test_ref, *refs):
-    *joined_refs, merged_ref, side_ref = refs
+    *all_refs, merged_ref, side_ref, cross_ref, last_ref = refs
+    joined_refs, across_refs = all_refs[:-2], all_refs[-2:]
+    cross_ref[...], last_ref[...] = across_products(joined_refs, across_refs, test_ref, 0)
     half = joined_refs[0].shape[1]
     merged, side = None, None
     for h in range(2):
@@ -268,36 +287,30 @@
     side_ref[...] = side
 
 
-def merge_near(joined, test_block):
-    wide = len(joined) // 2 * joined[0].shape[0]
+def merge_near(joined, across, test_block):
+    rank = joined[0].shape[0]
+    wide = len(joined) // 2 * rank
     return pl.pallas_call(
         merge_near_kernel,
-        in_specs=[VMEM] * (1 + len(joined)),
-        out_specs=[VMEM, VMEM],
+        in_specs=[VMEM] * (1 + len(joined) + len(across)),
+        out_specs=[VMEM] * 4,
         out_shape=[
             jax.ShapeDtypeStruct((wide, wide), jnp.float32),
             jax.ShapeDtypeStruct((wide, BLOCK), jnp.float32),
+            jax.ShapeDtypeStruct((wide + rank, rank), jnp.float32),
+            jax.ShapeDtypeStruct((rank, BLOCK), jnp.float32),
         ],
         compiler_params=pltpu.CompilerParams(vmem_limit_bytes=28 * 2**20),
         name="merge_near",
-    )(test_block, *joined)
-
-
-def merge_kernel(place_ref, merged_ref, side_ref, test_ref, *refs):
+    )(test_block, *joined, *across)
+
+
+def merge_kernel(place_ref, merged_ref, side_ref, cross_ref, last_ref, test_ref, *refs):
     *all_refs, o_ref = refs
     joined_refs, across_refs = all_refs[:-4], all_refs[-4:]
-    rank, deep = across_refs[0].shape
-    cross, last = None, None
-    for n in range(4):
-        here = slice(n % 2 * deep, (n % 2 + 1) * deep)
-        pieces = [ref[:, here] for ref in joined_refs[n // 2 :: 2]] + [across_refs[n][...]]
-        left = parts(jnp.concatenate(pieces, axis=0), 2)
-        across = [piece[-rank:] for piece in left]
-        right = parts(test_ref[n * deep : (n + 1) * deep, :], 2)
-        own = dot_parts(left, across, NT)
-        other = dot_parts(across, right, NN)
-        cross = own if cross is None else cross + own
-        last = other if last is None else last + other
+    rank = across_refs[0].shape[0]
+    cross, last = across_products(joined_refs, across_refs, test_ref, 1)
+    cross, last = cross + cross_ref[...], last + last_ref[...]
     merged, side = merged_ref[...], side_ref[...]
     blocks = [
         merged[:BLOCK, :BLOCK],
@@ -317,12 +330,12 @@
 def merge_partials(place, joined, across, test_block):
     return pl.pallas_call(
         merge_kernel,
-        in_specs=[SMEM] + [VMEM] * (3 + len(joined) + len(across)),
+        in_specs=[SMEM] + [VMEM] * (5 + len(joined) + len(across)),
         out_specs=VMEM,
         out_shape=jax.ShapeDtypeStruct((2, 320, BLOCK), jnp.float32),
         compiler_params=pltpu.CompilerParams(vmem_limit_bytes=28 * 2**20),
         name="merge_partials",
-    )(place, *merge_near(joined, test_block), test_block, *joined, *across)
+    )(place, *merge_near(joined, across[:2], test_block), test_block, *joined, *across)
 
 
 def finish_kernel(row_total, place_ref, mine_ref, other_ref, start_ref, *refs):
@@ -338,9 +351,16 @@
         if a != b:
             for ref, piece in zip(gram_refs, parts(block.T, 3)):
                 ref[cut(b), cut(a)] = piece
-    groups = start_ref.shape[0]
-    turned = [start_ref[(place_ref[1] + k) % groups] for k in SHIFTS]
-    next_ref[...] = jnp.concatenate(turned, axis=0).T
+    start = start_ref[...]
+    rank, wide = start.shape
+    groups = len(SHIFTS)
+    each = wide // groups
+    turned = None
+    for g in range(groups):
+        firsts = [(g + k) % groups * each for k in SHIFTS]
+        order = jnp.concatenate([start[:, f : f + each] for f in firsts], axis=1)
+        turned = order if turned is None else jnp.where(place_ref[1] == g, order, turned)
+    next_ref[...] = turned
 
     def step(index, carry):
         next_ref[...] = normalised(*sweep(next_ref[...], gram_refs))
@@ -365,8 +385,7 @@
 
 
 def finish(place, mine, other, start, joined, across, row_total):
-    rank = start.shape[-1]
-    wide = start.shape[0] * start.shape[1]
+    rank, wide = start.shape
     rows = 2 * joined[0].shape[1]
     return pl.pallas_call(
         lambda *refs: finish_kernel(row_total, *refs),
@@ -427,13 +446,11 @@
 def on_device(snapshots, test_block, start_block, start_merge):
     row_total = snapshots.shape[0] * lax.axis_size(ROW)
     place = jnp.stack([lax.axis_index(CORE), lax.axis_index("grp")])
-    groups = lax.axis_size("grp")
     mine, other = sum_over_rows(gram(snapshots, place), False)
-    basis = group_solve(place, mine, other, start_block, row_total)
+    basis = group_solve(place, mine, other, start_block.T, row_total)
     joined, across = gathered_bases(*[group_basis(basis, snapshots, h) for h in range(2)])
     mine, other = sum_over_rows(merge_partials(place, joined, across, test_block), True)
-    start = start_merge.reshape(groups, start_merge.shape[0] // groups, start_merge.shape[1])
-    return finish(place, mine, other, start, joined, across, row_total)
+    return finish(place, mine, other, start_merge.T, joined, across, row_total)
 
 
 def solution(mesh):

time: 170 us -> 166 us (0.976)
  local copies, waits for them, and re-layouts: 2.95 us -> 1.17 us
    ppermute x1, waiting for transfers between devices: 4.58 us -> 1.56 us  [gathered_bases(): lax.ppermute(last_far[:, half:], 'grp', up)]
    ppermute x1, waiting for transfers between devices: 0.01 us -> 2.04 us  [gathered_bases(): lax.ppermute(last_near[:, half:], 'grp', up)]
    unnamed x14 -> x10, local copies, waits for them, and re-layouts: 2.73 us -> 0.96 us
  transfers between devices with their start and end apart: 12 -> 12, of which waited for: 7 -> 8; matrix products, arithmetic and copies ran while one was open for 1% -> 0% of each run, Pallas kernels for 3% -> 4%
where the time goes in v5:
time: 166 us
  blocking collectives  69.4 us (42%)
  Pallas kernels  48.7 us (29%)
  starting transfers between devices  25 us (15%)
  waiting for transfers between devices  19.4 us (12%)
  other arithmetic  2.1 us (1%)
    all_to_all x3, blocking collectives, spread(): return lax.all_to_all(copies, axis, 0, 0, tiled=True)  40 us
    all_to_all x2, blocking collectives, reduced(): return jnp.sum(lax.all_to_all(cuts, axis, 0, 0, tiled=True), axis=0)  29.4 us
    pallas_call x1, Pallas kernels, finish(): pl.pallas_call(lambda *refs: finish_kernel(row_total, *refs), in_specs=[S...  16.1 us
    pallas_call x1, Pallas kernels, group_solve(): pl.pallas_call(lambda *refs: solve_kernel(row_total, *refs), in_specs=[SM...  14.3 us
    ppermute x4, starting transfers between devices, swap_cores(): return lax.ppermute(array, CORE, [(0, 1), (1, 0)])  13.8 us
    pallas_call x1, Pallas kernels, gram(): pl.pallas_call(gram_kernel, in_specs=[SMEM, HBM], out_specs=VMEM, out_sha...  7.13 us
    ppermute x1, waiting for transfers between devices, gathered_bases(): last_far = lax.ppermute(far, 'grp', up)  6.96 us
    pallas_call x2, Pallas kernels, group_basis(): pl.pallas_call(kernel, in_specs=[VMEM, HBM], out_specs=VMEM, out_shape=ja...  6.18 us
  transfers between devices with their start and end apart: 12, of which 8 were waited for; matrix products, arithmetic and copies ran while one was open for 0% of the time, Pallas kernels for 4%

profile of v5, /device:TPU:1, one launch (start us, length us, event | category | flops | bytes accessed | tf_op | source)
XLA Modules:
  0.0 166.0 jit_solution(8701293890142190399)
XLA Ops:
  0.1 7.1 %gram.1 = f32[2,640,128]{2,1,0:T(8,128)S(1)} custom-call(s32[2]{0:T(128)S(1)} %pad_add_fusion.core_ref.refs_0_.place_ref, f32[3584,512]{1,0:T(8,128)} %x_ref.5), custom_call_target="tpu_custom_call" | custom-call | tf_op jit(solution)/shard_map/gram/pallas_call | solution.py:151
  7.2 3.3 %collective-permute-start = (f32[640,128]{1,0:T(8,128)S(1)}, f32[640,128]{1,0:T(8,128)S(1)}, u32[]{:S(2)}, u32[]{:S(2)}) collective-permute-start(f32[640,128]{1,0:T(8,128)S(1)} %slice_bitcast_fusion), channel_id=1, source_target_pairs={{0,1},{1,0},{2,3},{3,2},{4,5},{5,4},{6,7},{7,6},{8,9},{9,8},{10,11... | collective-permute-start | bytes 983048 | tf_op jit(solution)/shard_map/ppermute | solution.py:403
  10.5 1.3 collective-permute-done
  11.9 21.3 %all_to_all.25 = f32[32,20,128]{2,1,0:T(8,128)S(1)} all-to-all(f32[32,20,128]{2,1,0:T(8,128)S(1)} %reshape.12), channel_id=1, replica_groups=mesh['grp'=4,'row_0'=4,'row_1'=8,'row_2'=2] {'row_0','row_1'}, dimensions={0} | all-to-all | bytes 655360 | tf_op jit(solution)/shard_map/all_to_all | solution.py:409
  33.2 18.3 %all_to_all.26 = f32[32,20,128]{2,1,0:T(8,128)S(1)} all-to-all(f32[32,20,128]{2,1,0:T(8,128)S(1)} %broadcast_in_dim.9), channel_id=1, replica_groups=mesh['grp'=4,'row_0'=4,'row_1'=8,'row_2'=2] {'row_0','row_1'}, dimensions={0} | all-to-all | bytes 655360 | tf_op jit(solution)/shard_map/all_to_all | solution.py:414
  51.5 4.6 %collective-permute-start.1 = (f32[640,128]{1,0:T(8,128)S(1)}, f32[640,128]{1,0:T(8,128)S(1)}, u32[]{:S(2)}, u32[]{:S(2)}) collective-permute-start(f32[640,128]{1,0:T(8,128)S(1)} %reshape.13.refs_1_), channel_id=1, source_target_pairs={{0,1},{1,0},{2,3},{3,2},{4,5},{5,4},{6,7},{7,6},{8,9},{9,8},{10,11... | collective-permute-start | bytes 983048 | tf_op jit(solution)/shard_map/ppermute | solution.py:403
  56.2 1.3 collective-permute-done.1.refs_2_
  57.4 14.3 %group_solve.1.q_ref = f32[64,512]{1,0:T(8,128)S(1)} custom-call(s32[2]{0:T(128)S(1)} %pad_add_fusion.core_ref.refs_0_.place_ref, f32[640,128]{1,0:T(8,128)S(1)} %reshape.13.refs_1_, f32[640,128]{1,0:T(8,128)S(1)} %collective-permute-done.1.refs_2_, f32[64,512]{1,0:T(8,128)S(1)} %bitcast.20), custom_call_target="tpu_custom_call" | custom-call | tf_op jit(solution)/shard_map/group_solve/pallas_call | solution.py:206
  71.7 3.0 %group_basis.2.refs_0_.refs_4_ = f32[64,1792]{1,0:T(8,128)S(1)} custom-call(f32[64,512]{1,0:T(8,128)S(1)} %group_solve.1.q_ref, f32[3584,512]{1,0:T(8,128)} %x_ref.5), custom_call_target="tpu_custom_call" | custom-call | tf_op jit(solution)/shard_map/group_basis/pallas_call | solution.py:238
  74.7 1.3 collective-permute-start.4
  76.0 1.5 collective-permute-start.2
  77.6 3.2 %group_basis.3.refs_1_.refs_5_ = f32[64,1792]{1,0:T(8,128)S(1)} custom-call(f32[64,512]{1,0:T(8,128)S(1)} %group_solve.1.q_ref, f32[3584,512]{1,0:T(8,128)} %x_ref.5), custom_call_target="tpu_custom_call" | custom-call | tf_op jit(solution)/shard_map/group_basis/pallas_call | solution.py:238
  80.8 2.7 %collective-permute-start.3 = (f32[64,1792]{1,0:T(8,128)S(1)}, f32[64,1792]{1,0:T(8,128)S(1)}, u32[]{:S(2)}, u32[]{:S(2)}) collective-permute-start(f32[64,1792]{1,0:T(8,128)S(1)} %group_basis.3.refs_1_.refs_5_), channel_id=1, source_target_pairs={{0,192},{64,0},{128,64},{192,128},{1,193},{65,1},{129,65},{193,129... | collective-permute-start | bytes 1376264 | tf_op jit(solution)/shard_map/ppermute | solution.py:435
  83.5 4.3 %collective-permute-done.4.refs_4_.refs_8_ = f32[64,1792]{1,0:T(8,128)S(1)} collective-permute-done((f32[64,1792]{1,0:T(8,128)S(1)}, f32[64,1792]{1,0:T(8,128)S(1)}, u32[]{:S(2)}, u32[]{:S(2)}) %collective-permute-start.4) | collective-permute-done | bytes 458784 | tf_op jit(solution)/shard_map/ppermute | solution.py:434
  87.9 2.7 %collective-permute-start.6 = (f32[64,896]{1,0:T(8,128)S(1)}, f32[64,896]{1,0:T(8,128)S(1)}, u32[]{:S(2)}, u32[]{:S(2)}) collective-permute-start(f32[64,896]{1,0:T(8,128)S(1)} %slice.34), channel_id=1, source_target_pairs={{0,192},{64,0},{128,64},{192,128},{1,193},{65,1},{129,65},{193,129... | collective-permute-start | bytes 688136 | tf_op jit(solution)/shard_map/ppermute | solution.py:438
  90.6 7.0 %collective-permute-done.5.refs_5_.refs_9_ = f32[64,1792]{1,0:T(8,128)S(1)} collective-permute-done((f32[64,1792]{1,0:T(8,128)S(1)}, f32[64,1792]{1,0:T(8,128)S(1)}, u32[]{:S(2)}, u32[]{:S(2)}) %collective-permute-start.5) | collective-permute-done | bytes 458784 | tf_op jit(solution)/shard_map/ppermute | solution.py:436
  97.7 2.7 %collective-permute-start.8 = (f32[64,896]{1,0:T(8,128)S(1)}, f32[64,896]{1,0:T(8,128)S(1)}, u32[]{:S(2)}, u32[]{:S(2)}) collective-permute-start(f32[64,896]{1,0:T(8,128)S(1)} %slice.36), channel_id=1, source_target_pairs={{0,192},{64,0},{128,64},{192,128},{1,193},{65,1},{129,65},{193,129... | collective-permute-start | bytes 688136 | tf_op jit(solution)/shard_map/ppermute | solution.py:440
  100.4 2.0 %collective-permute-done.7.refs_7_.refs_11_ = f32[64,896]{1,0:T(8,128)S(1)} collective-permute-done((f32[64,896]{1,0:T(8,128)S(1)}, f32[64,896]{1,0:T(8,128)S(1)}, u32[]{:S(2)}, u32[]{:S(2)}) %collective-permute-start.7) | collective-permute-done | bytes 229408 | tf_op jit(solution)/shard_map/ppermute | solution.py:439
  102.5 3.3 %merge_near.1 = (f32[192,192]{1,0:T(8,128)S(1)}, f32[192,128]{1,0:T(8,128)S(1)}, f32[256,64]{1,0:T(8,128)S(1)}, f32[64,128]{1,0:T(8,128)S(1)}) custom-call(f32[3584,128]{1,0:T(8,128)S(1)} %copy-done, f32[64,1792]{1,0:T(8,128)S(1)} %group_basis.2.refs_0_.refs_4_, f32[64,1792]{1,0:T(8,128)S(1)} %group_basis.3.refs_1_.refs_5_, ...), custom_call_target="tpu_custom_call" | custom-call | tf_op jit(solution)/shard_map/merge_near/pallas_call | solution.py:293
  105.8 1.6 collective-permute-done.9.refs_9_.refs_13_
  107.4 1.7 %merge_partials.1 = f32[2,320,128]{2,1,0:T(8,128)S(1)} custom-call(s32[2]{0:T(128)S(1)} %pad_add_fusion.core_ref.refs_0_.place_ref, f32[192,192]{1,0:T(8,128)S(1)} %get-tuple-element.9.merged_ref, f32[192,128]{1,0:T(8,128)S(1)} %get-tuple-element.10.side_ref, f32[256,64]{1,0:T(8,128)S(1)} %get-tuple-element.11.cross_ref, ...), custom_call_target="tpu_custom_call" | custom-call | tf_op jit(solution)/shard_map/merge_partials/pallas_call | solution.py:331
  109.1 1.3 collective-permute-start.10
  110.5 1.0 collective-permute-done.10
  111.5 8.1 %all_to_all.27 = f32[4,80,128]{2,1,0:T(8,128)} all-to-all(f32[4,80,128]{2,1,0:T(8,128)S(1)} %bitcast.22), channel_id=1, replica_groups=mesh['grp'=4,'row_0'=4,'row_1'=8,'row_2'=2] {'row_0'}, dimensions={0} | all-to-all | bytes 327680 | tf_op jit(solution)/shard_map/all_to_all | solution.py:409
  119.6 0.9 reduce_sum.28
  120.6 14.3 %all_to_all.28 = f32[8,80,128]{2,1,0:T(8,128)} all-to-all(f32[8,80,128]{2,1,0:T(8,128)S(1)} %broadcast_in_dim.10), channel_id=1, replica_groups=mesh['grp'=4,'row_0'=4,'row_1'=8,'row_2'=2] {'row_1'}, dimensions={0} | all-to-all | bytes 655360 | tf_op jit(solution)/shard_map/all_to_all | solution.py:414
  134.9 1.0 reduce_sum.29
  135.9 7.4 %all_to_all.29 = f32[4,80,128]{2,1,0:T(8,128)S(1)} all-to-all(f32[4,80,128]{2,1,0:T(8,128)S(1)} %broadcast_in_dim.11), channel_id=1, replica_groups=mesh['grp'=4,'row_0'=4,'row_1'=8,'row_2'=2] {'row_0'}, dimensions={0} | all-to-all | bytes 327680 | tf_op jit(solution)/shard_map/all_to_all | solution.py:414
  143.3 4.6 %collective-permute-start.11 = (f32[320,128]{1,0:T(8,128)S(1)}, f32[320,128]{1,0:T(8,128)S(1)}, u32[]{:S(2)}, u32[]{:S(2)}) collective-permute-start(f32[320,128]{1,0:T(8,128)S(1)} %bitcast.18), channel_id=1, source_target_pairs={{0,1},{1,0},{2,3},{3,2},{4,5},{5,4},{6,7},{7,6},{8,9},{9,8},{10,11... | collective-permute-start | bytes 491528 | tf_op jit(solution)/shard_map/ppermute | solution.py:403
  147.9 1.0 collective-permute-done.11.refs_2_
  149.0 0.9 copy-done.2
  149.9 16.1 %finish.1 = f32[3584,128]{1,0:T(8,128)} custom-call(s32[2]{0:T(128)S(1)} %pad_add_fusion.core_ref.refs_0_.place_ref, f32[320,128]{1,0:T(8,128)S(1)} %bitcast.19, f32[320,128]{1,0:T(8,128)S(1)} %collective-permute-done.11.refs_2_, f32[64,256]{1,0:T(8,128)S(1)} %bitcast.21, f32[64,1792]{1,0:T(8,128)S(1)} %group_basis.2.refs_0_.refs_4_, ...), custom_call_target="tpu_custom_call" | custom-call | tf_op jit(solution)/shard_map/finish/pallas_call | solution.py:390
  (31 shorter events, 0.7 us)
Async XLA Ops:
  7.2 4.6 %collective-permute-start = (f32[640,128]{1,0:T(8,128)S(1)}, f32[640,128]{1,0:T(8,128)S(1)}, u32[]{:S(2)}, u32[]{:S(2)}) collective-permute-start(f32[640,128]{1,0:T(8,128)S(1)} %slice_bitcast_fusion), channel_id=1, source_target_pairs={{0,1},{1,0},{2,3},{3,2},{4,5},{5,4},{6,7},{7,6},{8,9},{9,8},{10,11... | collective-permute-start | bytes 983048 | tf_op jit(solution)/shard_map/ppermute | solution.py:403
  11.8 45.6 %copy-start.3 = (f32[512,64]{0,1:T(8,128)S(1)}, f32[512,64]{0,1:T(8,128)}, u32[]{:S(2)}) copy-start(f32[512,64]{0,1:T(8,128)} %param.6) | copy-start | bytes 393220
  51.5 5.9 %collective-permute-start.1 = (f32[640,128]{1,0:T(8,128)S(1)}, f32[640,128]{1,0:T(8,128)S(1)}, u32[]{:S(2)}, u32[]{:S(2)}) collective-permute-start(f32[640,128]{1,0:T(8,128)S(1)} %reshape.13.refs_1_), channel_id=1, source_target_pairs={{0,1},{1,0},{2,3},{3,2},{4,5},{5,4},{6,7},{7,6},{8,9},{9,8},{10,11... | collective-permute-start | bytes 983048 | tf_op jit(solution)/shard_map/ppermute | solution.py:403
  74.7 13.0 %collective-permute-start.4 = (f32[64,1792]{1,0:T(8,128)S(1)}, f32[64,1792]{1,0:T(8,128)S(1)}, u32[]{:S(2)}, u32[]{:S(2)}) collective-permute-start(f32[64,1792]{1,0:T(8,128)S(1)} %group_basis.2.refs_0_.refs_4_), channel_id=1, source_target_pairs={{0,64},{64,128},{128,192},{192,0},{1,65},{65,129},{129,193},{193,1... | collective-permute-start | bytes 1376264 | tf_op jit(solution)/shard_map/ppermute | solution.py:434
  76.0 11.8 %collective-permute-start.2 = (f32[64,1792]{1,0:T(8,128)S(1)}, f32[64,1792]{1,0:T(8,128)S(1)}, u32[]{:S(2)}, u32[]{:S(2)}) collective-permute-start(f32[64,1792]{1,0:T(8,128)S(1)} %group_basis.2.refs_0_.refs_4_), channel_id=1, source_target_pairs={{0,192},{64,0},{128,64},{192,128},{1,193},{65,1},{129,65},{193,129... | collective-permute-start | bytes 1376264 | tf_op jit(solution)/shard_map/ppermute | solution.py:433
  77.6 24.9 %copy-start = (f32[3584,128]{1,0:T(8,128)S(1)}, f32[3584,128]{1,0:T(8,128)}, u32[]{:S(2)}) copy-start(f32[3584,128]{1,0:T(8,128)} %test_ref.3) | copy-start | bytes 5505028
  80.7 16.8 %collective-permute-start.5 = (f32[64,1792]{1,0:T(8,128)S(1)}, f32[64,1792]{1,0:T(8,128)S(1)}, u32[]{:S(2)}, u32[]{:S(2)}) collective-permute-start(f32[64,1792]{1,0:T(8,128)S(1)} %group_basis.3.refs_1_.refs_5_), channel_id=1, source_target_pairs={{0,64},{64,128},{128,192},{192,0},{1,65},{65,129},{129,193},{193,1... | collective-permute-start | bytes 1376264 | tf_op jit(solution)/shard_map/ppermute | solution.py:436
  80.8 16.9 %collective-permute-start.3 = (f32[64,1792]{1,0:T(8,128)S(1)}, f32[64,1792]{1,0:T(8,128)S(1)}, u32[]{:S(2)}, u32[]{:S(2)}) collective-permute-start(f32[64,1792]{1,0:T(8,128)S(1)} %group_basis.3.refs_1_.refs_5_), channel_id=1, source_target_pairs={{0,192},{64,0},{128,64},{192,128},{1,193},{65,1},{129,65},{193,129... | collective-permute-start | bytes 1376264 | tf_op jit(solution)/shard_map/ppermute | solution.py:435
  87.8 14.7 %collective-permute-start.7 = (f32[64,896]{1,0:T(8,128)S(1)}, f32[64,896]{1,0:T(8,128)S(1)}, u32[]{:S(2)}, u32[]{:S(2)}) collective-permute-start(f32[64,896]{1,0:T(8,128)S(1)} %slice.35), channel_id=1, source_target_pairs={{0,64},{64,128},{128,192},{192,0},{1,65},{65,129},{129,193},{193,1... | collective-permute-start | bytes 688136 | tf_op jit(solution)/shard_map/ppermute | solution.py:439
  87.9 14.6 %collective-permute-start.6 = (f32[64,896]{1,0:T(8,128)S(1)}, f32[64,896]{1,0:T(8,128)S(1)}, u32[]{:S(2)}, u32[]{:S(2)}) collective-permute-start(f32[64,896]{1,0:T(8,128)S(1)} %slice.34), channel_id=1, source_target_pairs={{0,192},{64,0},{128,64},{192,128},{1,193},{65,1},{129,65},{193,129... | collective-permute-start | bytes 688136 | tf_op jit(solution)/shard_map/ppermute | solution.py:438
  97.6 9.8 %collective-permute-start.9 = (f32[64,896]{1,0:T(8,128)S(1)}, f32[64,896]{1,0:T(8,128)S(1)}, u32[]{:S(2)}, u32[]{:S(2)}) collective-permute-start(f32[64,896]{1,0:T(8,128)S(1)} %slice.37), channel_id=1, source_target_pairs={{0,64},{64,128},{128,192},{192,0},{1,65},{65,129},{129,193},{193,1... | collective-permute-start | bytes 688136 | tf_op jit(solution)/shard_map/ppermute | solution.py:441
  97.7 9.7 %collective-permute-start.8 = (f32[64,896]{1,0:T(8,128)S(1)}, f32[64,896]{1,0:T(8,128)S(1)}, u32[]{:S(2)}, u32[]{:S(2)}) collective-permute-start(f32[64,896]{1,0:T(8,128)S(1)} %slice.36), channel_id=1, source_target_pairs={{0,192},{64,0},{128,64},{192,128},{1,193},{65,1},{129,65},{193,129... | collective-permute-start | bytes 688136 | tf_op jit(solution)/shard_map/ppermute | solution.py:440
  107.4 1.7 %copy-start.1 = (f32[64,896]{1,0:T(8,128)}, f32[64,896]{1,0:T(8,128)S(1)}, u32[]{:S(2)}) copy-start(f32[64,896]{1,0:T(8,128)S(1)} %collective-permute-done.8.refs_8_.refs_12_) | copy-start | bytes 688132
  109.1 39.9 %copy-start.4 = (f32[256,64]{0,1:T(8,128)S(1)}, f32[256,64]{0,1:T(8,128)}, u32[]{:S(2)}) copy-start(f32[256,64]{0,1:T(8,128)} %param.7) | copy-start | bytes 196612
  109.1 2.3 %collective-permute-start.10 = (f32[320,128]{1,0:T(8,128)S(1)}, f32[320,128]{1,0:T(8,128)S(1)}, u32[]{:S(2)}, u32[]{:S(2)}) collective-permute-start(f32[320,128]{1,0:T(8,128)S(1)} %slice_bitcast_fusion.2), channel_id=1, source_target_pairs={{0,1},{1,0},{2,3},{3,2},{4,5},{5,4},{6,7},{7,6},{8,9},{9,8},{10,11... | collective-permute-start | bytes 491528 | tf_op jit(solution)/shard_map/ppermute | solution.py:403
  143.3 5.6 %collective-permute-start.11 = (f32[320,128]{1,0:T(8,128)S(1)}, f32[320,128]{1,0:T(8,128)S(1)}, u32[]{:S(2)}, u32[]{:S(2)}) collective-permute-start(f32[320,128]{1,0:T(8,128)S(1)} %bitcast.18), channel_id=1, source_target_pairs={{0,1},{1,0},{2,3},{3,2},{4,5},{5,4},{6,7},{7,6},{8,9},{9,8},{10,11... | collective-permute-start | bytes 491528 | tf_op jit(solution)/shard_map/ppermute | solution.py:403
  149.0 0.9 copy-start.2

commit v6 on v5

--- a/solution.py
+++ b/solution.py
@@ -146,7 +146,7 @@
 
 def gram(snapshots, core):
     rows, width = snapshots.shape
-    steps = 4
+    steps = 7
     held = len(upper_pairs(width // BLOCK)) // 2 * BLOCK
     return pl.pallas_call(
         gram_kernel,
@@ -218,22 +218,26 @@
 def group_basis(basis, snapshots, half):
     rank = basis.shape[0]
     rows = snapshots.shape[0]
-    deep = rows // 4
+    deep = rows // 2
+    edges = [0, deep // 7 * 2, deep // 7 * 4, deep]
+    spans = list(zip(edges, edges[1:]))
 
     def kernel(q_ref, x_ref, o_ref, held_ref, arrived):
         copies = [
             pltpu.make_async_copy(
-                x_ref.at[pl.ds((half * 2 + n) * deep, deep), :], held_ref.at[n], arrived.at[n]
+                x_ref.at[pl.ds(half * deep + first, end - first), :],
+                held_ref.at[pl.ds(first, end - first), :],
+                arrived.at[n],
             )
-            for n in range(2)
+            for n, (first, end) in enumerate(spans)
         ]
         for copy in copies:
             copy.start()
         left = parts(q_ref[...], 2)
-        for n, copy in enumerate(copies):
+        for copy, (first, end) in zip(copies, spans):
             copy.wait()
-            right = parts(held_ref[n], 2)
-            o_ref[:, n * deep : (n + 1) * deep] = dot_parts(left, right, NT)
+            right = parts(held_ref[first:end, :], 2)
+            o_ref[:, first:end] = dot_parts(left, right, NT)
 
     return pl.pallas_call(
         kernel,
@@ -241,8 +245,8 @@
         out_specs=VMEM,
         out_shape=jax.ShapeDtypeStruct((rank, rows // 2), jnp.float32),
         scratch_shapes=[
-            pltpu.VMEM((2, deep, snapshots.shape[1]), jnp.float32),
-            pltpu.SemaphoreType.DMA((2,)),
+            pltpu.VMEM((deep, snapshots.shape[1]), jnp.float32),
+            pltpu.SemaphoreType.DMA((len(spans),)),
         ],
         compiler_params=pltpu.CompilerParams(vmem_limit_bytes=48 * 2**20),
         name="group_basis",
@@ -255,19 +259,11 @@
 
 def across_products(joined_refs, across_refs, test_ref, h):
     rank, deep = across_refs[0].shape
-    cross, last = None, None
-    for n in range(2):
-        here = slice(n * deep, (n + 1) * deep)
-        pieces = [ref[:, here] for ref in joined_refs[h::2]] + [across_refs[2 * h + n][...]]
-        left = parts(jnp.concatenate(pieces, axis=0), 2)
-        across = [piece[-rank:] for piece in left]
-        first = (2 * h + n) * deep
-        right = parts(test_ref[first : first + deep, :], 2)
-        own = dot_parts(left, across, NT)
-        other = dot_parts(across, right, NN)
-        cross = own if cross is None else cross + own
-        last = other if last is None else last + other
-    return cross, last
+    across = jnp.concatenate([ref[...] for ref in across_refs[2 * h : 2 * h + 2]], axis=1)
+    left = parts(jnp.concatenate([ref[...] for ref in joined_refs[h::2]] + [across], axis=0), 2)
+    across = [piece[-rank:] for piece in left]
+    right = parts(test_ref[2 * h * deep : 2 * (h + 1) * deep, :], 2)
+    return dot_parts(left, across, NT), dot_parts(across, right, NN)
 
 
 def merge_near_kernel(test_ref, *refs):
@@ -376,12 +372,12 @@
     weight = dot_parts(parts(coef.T, 3), parts(test_coeffs, 3), NN) / row_total
     weight = parts(weight.T, 2)
     across_refs = joined_refs[-4:]
-    deep = across_refs[0].shape[1]
-    for n in range(4):
-        here = slice(n % 2 * deep, (n % 2 + 1) * deep)
-        bases = [ref[:, here] for ref in joined_refs[:-4][n // 2 :: 2]] + [across_refs[n][...]]
-        joined = jnp.concatenate(bases, axis=0)
-        o_ref[n * deep : (n + 1) * deep, :] = dot_parts(weight, parts(joined, 2), NN).T
+    half = joined_refs[0].shape[1]
+    for h in range(2):
+        across = jnp.concatenate([ref[...] for ref in across_refs[2 * h : 2 * h + 2]], axis=1)
+        bases = [ref[...] for ref in joined_refs[:-4][h::2]] + [across]
+        joined = parts(jnp.concatenate(bases, axis=0), 2)
+        o_ref[h * half : (h + 1) * half, :] = dot_parts(weight, joined, NN).T
 
 
 def finish(place, mine, other, start, joined, across, row_total):

time: 166 us -> 166 us (level)
  no operation moved by 1% of the time
where the time goes in v6:
time: 166 us
  blocking collectives  69.4 us (42%)
  Pallas kernels  48.1 us (29%)
  starting transfers between devices  25.1 us (15%)
  waiting for transfers between devices  19.5 us (12%)
  other arithmetic  2.1 us (1%)
    all_to_all x3, blocking collectives, spread(): return lax.all_to_all(copies, axis, 0, 0, tiled=True)  40 us
    all_to_all x2, blocking collectives, reduced(): return jnp.sum(lax.all_to_all(cuts, axis, 0, 0, tiled=True), axis=0)  29.4 us
    pallas_call x1, Pallas kernels, finish(): pl.pallas_call(lambda *refs: finish_kernel(row_total, *refs), in_specs=[S...  16 us
    pallas_call x1, Pallas kernels, group_solve(): pl.pallas_call(lambda *refs: solve_kernel(row_total, *refs), in_specs=[SM...  14.3 us
    ppermute x4, starting transfers between devices, swap_cores(): return lax.ppermute(array, CORE, [(0, 1), (1, 0)])  13.8 us
    ppermute x1, waiting for transfers between devices, gathered_bases(): last_far = lax.ppermute(far, 'grp', up)  6.96 us
    pallas_call x1, Pallas kernels, gram(): pl.pallas_call(gram_kernel, in_specs=[SMEM, HBM], out_specs=VMEM, out_sha...  6.83 us
    pallas_call x2, Pallas kernels, group_basis(): pl.pallas_call(kernel, in_specs=[VMEM, HBM], out_specs=VMEM, out_shape=ja...  6.12 us
  transfers between devices with their start and end apart: 12, of which 8 were waited for; matrix products, arithmetic and copies ran while one was open for 0% of the time, Pallas kernels for 4%

profile of v6, /device:TPU:1, one launch (start us, length us, event | category | flops | bytes accessed | tf_op | source)
XLA Modules:
  0.0 165.5 jit_solution(1591683519774117552)
XLA Ops:
  0.1 6.8 %gram.1 = f32[2,640,128]{2,1,0:T(8,128)S(1)} custom-call(s32[2]{0:T(128)S(1)} %pad_add_fusion.core_ref.refs_0_.place_ref, f32[3584,512]{1,0:T(8,128)} %x_ref.5), custom_call_target="tpu_custom_call" | custom-call | tf_op jit(solution)/shard_map/gram/pallas_call | solution.py:151
  6.9 3.3 %collective-permute-start = (f32[640,128]{1,0:T(8,128)S(1)}, f32[640,128]{1,0:T(8,128)S(1)}, u32[]{:S(2)}, u32[]{:S(2)}) collective-permute-start(f32[640,128]{1,0:T(8,128)S(1)} %slice_bitcast_fusion), channel_id=1, source_target_pairs={{0,1},{1,0},{2,3},{3,2},{4,5},{5,4},{6,7},{7,6},{8,9},{9,8},{10,11... | collective-permute-start | bytes 983048 | tf_op jit(solution)/shard_map/ppermute | solution.py:399
  10.2 1.3 collective-permute-done
  11.6 21.3 %all_to_all.25 = f32[32,20,128]{2,1,0:T(8,128)S(1)} all-to-all(f32[32,20,128]{2,1,0:T(8,128)S(1)} %reshape.12), channel_id=1, replica_groups=mesh['grp'=4,'row_0'=4,'row_1'=8,'row_2'=2] {'row_0','row_1'}, dimensions={0} | all-to-all | bytes 655360 | tf_op jit(solution)/shard_map/all_to_all | solution.py:405
  32.9 18.3 %all_to_all.26 = f32[32,20,128]{2,1,0:T(8,128)S(1)} all-to-all(f32[32,20,128]{2,1,0:T(8,128)S(1)} %broadcast_in_dim.9), channel_id=1, replica_groups=mesh['grp'=4,'row_0'=4,'row_1'=8,'row_2'=2] {'row_0','row_1'}, dimensions={0} | all-to-all | bytes 655360 | tf_op jit(solution)/shard_map/all_to_all | solution.py:410
  51.2 4.6 %collective-permute-start.1 = (f32[640,128]{1,0:T(8,128)S(1)}, f32[640,128]{1,0:T(8,128)S(1)}, u32[]{:S(2)}, u32[]{:S(2)}) collective-permute-start(f32[640,128]{1,0:T(8,128)S(1)} %reshape.13.refs_1_), channel_id=1, source_target_pairs={{0,1},{1,0},{2,3},{3,2},{4,5},{5,4},{6,7},{7,6},{8,9},{9,8},{10,11... | collective-permute-start | bytes 983048 | tf_op jit(solution)/shard_map/ppermute | solution.py:399
  55.8 1.3 collective-permute-done.1.refs_2_
  57.1 14.3 %group_solve.1.q_ref = f32[64,512]{1,0:T(8,128)S(1)} custom-call(s32[2]{0:T(128)S(1)} %pad_add_fusion.core_ref.refs_0_.place_ref, f32[640,128]{1,0:T(8,128)S(1)} %reshape.13.refs_1_, f32[640,128]{1,0:T(8,128)S(1)} %collective-permute-done.1.refs_2_, f32[64,512]{1,0:T(8,128)S(1)} %bitcast.20), custom_call_target="tpu_custom_call" | custom-call | tf_op jit(solution)/shard_map/group_solve/pallas_call | solution.py:206
  71.4 3.0 %group_basis.2.refs_0_.refs_4_ = f32[64,1792]{1,0:T(8,128)S(1)} custom-call(f32[64,512]{1,0:T(8,128)S(1)} %group_solve.1.q_ref, f32[3584,512]{1,0:T(8,128)} %x_ref.5), custom_call_target="tpu_custom_call" | custom-call | tf_op jit(solution)/shard_map/group_basis/pallas_call | solution.py:242
  74.4 1.3 collective-permute-start.4
  75.7 1.5 collective-permute-start.2
  77.2 3.1 %group_basis.3.refs_1_.refs_5_ = f32[64,1792]{1,0:T(8,128)S(1)} custom-call(f32[64,512]{1,0:T(8,128)S(1)} %group_solve.1.q_ref, f32[3584,512]{1,0:T(8,128)} %x_ref.5), custom_call_target="tpu_custom_call" | custom-call | tf_op jit(solution)/shard_map/group_basis/pallas_call | solution.py:242
  80.4 2.7 %collective-permute-start.3 = (f32[64,1792]{1,0:T(8,128)S(1)}, f32[64,1792]{1,0:T(8,128)S(1)}, u32[]{:S(2)}, u32[]{:S(2)}) collective-permute-start(f32[64,1792]{1,0:T(8,128)S(1)} %group_basis.3.refs_1_.refs_5_), channel_id=1, source_target_pairs={{0,192},{64,0},{128,64},{192,128},{1,193},{65,1},{129,65},{193,129... | collective-permute-start | bytes 1376264 | tf_op jit(solution)/shard_map/ppermute | solution.py:431
  83.1 4.3 %collective-permute-done.4.refs_4_.refs_8_ = f32[64,1792]{1,0:T(8,128)S(1)} collective-permute-done((f32[64,1792]{1,0:T(8,128)S(1)}, f32[64,1792]{1,0:T(8,128)S(1)}, u32[]{:S(2)}, u32[]{:S(2)}) %collective-permute-start.4) | collective-permute-done | bytes 458784 | tf_op jit(solution)/shard_map/ppermute | solution.py:430
  87.5 2.7 %collective-permute-start.6 = (f32[64,896]{1,0:T(8,128)S(1)}, f32[64,896]{1,0:T(8,128)S(1)}, u32[]{:S(2)}, u32[]{:S(2)}) collective-permute-start(f32[64,896]{1,0:T(8,128)S(1)} %slice.34), channel_id=1, source_target_pairs={{0,192},{64,0},{128,64},{192,128},{1,193},{65,1},{129,65},{193,129... | collective-permute-start | bytes 688136 | tf_op jit(solution)/shard_map/ppermute | solution.py:434
  90.2 7.0 %collective-permute-done.5.refs_5_.refs_9_ = f32[64,1792]{1,0:T(8,128)S(1)} collective-permute-done((f32[64,1792]{1,0:T(8,128)S(1)}, f32[64,1792]{1,0:T(8,128)S(1)}, u32[]{:S(2)}, u32[]{:S(2)}) %collective-permute-start.5) | collective-permute-done | bytes 458784 | tf_op jit(solution)/shard_map/ppermute | solution.py:432
  97.4 2.7 %collective-permute-start.8 = (f32[64,896]{1,0:T(8,128)S(1)}, f32[64,896]{1,0:T(8,128)S(1)}, u32[]{:S(2)}, u32[]{:S(2)}) collective-permute-start(f32[64,896]{1,0:T(8,128)S(1)} %slice.36), channel_id=1, source_target_pairs={{0,192},{64,0},{128,64},{192,128},{1,193},{65,1},{129,65},{193,129... | collective-permute-start | bytes 688136 | tf_op jit(solution)/shard_map/ppermute | solution.py:436
  100.1 2.0 %collective-permute-done.7.refs_7_.refs_11_ = f32[64,896]{1,0:T(8,128)S(1)} collective-permute-done((f32[64,896]{1,0:T(8,128)S(1)}, f32[64,896]{1,0:T(8,128)S(1)}, u32[]{:S(2)}, u32[]{:S(2)}) %collective-permute-start.7) | collective-permute-done | bytes 229408 | tf_op jit(solution)/shard_map/ppermute | solution.py:435
  102.1 3.3 %merge_near.1 = (f32[192,192]{1,0:T(8,128)S(1)}, f32[192,128]{1,0:T(8,128)S(1)}, f32[256,64]{1,0:T(8,128)S(1)}, f32[64,128]{1,0:T(8,128)S(1)}) custom-call(f32[3584,128]{1,0:T(8,128)S(1)} %copy-done, f32[64,1792]{1,0:T(8,128)S(1)} %group_basis.2.refs_0_.refs_4_, f32[64,1792]{1,0:T(8,128)S(1)} %group_basis.3.refs_1_.refs_5_, ...), custom_call_target="tpu_custom_call" | custom-call | tf_op jit(solution)/shard_map/merge_near/pallas_call | solution.py:289
  105.4 1.6 collective-permute-done.9.refs_9_.refs_13_
  107.0 1.7 %merge_partials.1 = f32[2,320,128]{2,1,0:T(8,128)S(1)} custom-call(s32[2]{0:T(128)S(1)} %pad_add_fusion.core_ref.refs_0_.place_ref, f32[192,192]{1,0:T(8,128)S(1)} %get-tuple-element.9.merged_ref, f32[192,128]{1,0:T(8,128)S(1)} %get-tuple-element.10.side_ref, f32[256,64]{1,0:T(8,128)S(1)} %get-tuple-element.11.cross_ref, ...), custom_call_target="tpu_custom_call" | custom-call | tf_op jit(solution)/shard_map/merge_partials/pallas_call | solution.py:327
  108.8 1.3 collective-permute-start.10
  110.1 1.0 collective-permute-done.10
  111.1 8.1 %all_to_all.27 = f32[4,80,128]{2,1,0:T(8,128)} all-to-all(f32[4,80,128]{2,1,0:T(8,128)S(1)} %bitcast.22), channel_id=1, replica_groups=mesh['grp'=4,'row_0'=4,'row_1'=8,'row_2'=2] {'row_0'}, dimensions={0} | all-to-all | bytes 327680 | tf_op jit(solution)/shard_map/all_to_all | solution.py:405
  119.2 0.9 reduce_sum.28
  120.2 14.3 %all_to_all.28 = f32[8,80,128]{2,1,0:T(8,128)} all-to-all(f32[8,80,128]{2,1,0:T(8,128)S(1)} %broadcast_in_dim.10), channel_id=1, replica_groups=mesh['grp'=4,'row_0'=4,'row_1'=8,'row_2'=2] {'row_1'}, dimensions={0} | all-to-all | bytes 655360 | tf_op jit(solution)/shard_map/all_to_all | solution.py:410
  134.5 1.0 reduce_sum.29
  135.6 7.4 %all_to_all.29 = f32[4,80,128]{2,1,0:T(8,128)S(1)} all-to-all(f32[4,80,128]{2,1,0:T(8,128)S(1)} %broadcast_in_dim.11), channel_id=1, replica_groups=mesh['grp'=4,'row_0'=4,'row_1'=8,'row_2'=2] {'row_0'}, dimensions={0} | all-to-all | bytes 327680 | tf_op jit(solution)/shard_map/all_to_all | solution.py:410
  143.0 4.6 %collective-permute-start.11 = (f32[320,128]{1,0:T(8,128)S(1)}, f32[320,128]{1,0:T(8,128)S(1)}, u32[]{:S(2)}, u32[]{:S(2)}) collective-permute-start(f32[320,128]{1,0:T(8,128)S(1)} %bitcast.18), channel_id=1, source_target_pairs={{0,1},{1,0},{2,3},{3,2},{4,5},{5,4},{6,7},{7,6},{8,9},{9,8},{10,11... | collective-permute-start | bytes 491528 | tf_op jit(solution)/shard_map/ppermute | solution.py:399
  147.6 1.0 collective-permute-done.11.refs_2_
  148.6 0.9 copy-done.2
  149.5 16.0 %finish.1 = f32[3584,128]{1,0:T(8,128)} custom-call(s32[2]{0:T(128)S(1)} %pad_add_fusion.core_ref.refs_0_.place_ref, f32[320,128]{1,0:T(8,128)S(1)} %bitcast.19, f32[320,128]{1,0:T(8,128)S(1)} %collective-permute-done.11.refs_2_, f32[64,256]{1,0:T(8,128)S(1)} %bitcast.21, f32[64,1792]{1,0:T(8,128)S(1)} %group_basis.2.refs_0_.refs_4_, ...), custom_call_target="tpu_custom_call" | custom-call | tf_op jit(solution)/shard_map/finish/pallas_call | solution.py:386
  (31 shorter events, 0.7 us)
Async XLA Ops:
  6.9 4.5 %collective-permute-start = (f32[640,128]{1,0:T(8,128)S(1)}, f32[640,128]{1,0:T(8,128)S(1)}, u32[]{:S(2)}, u32[]{:S(2)}) collective-permute-start(f32[640,128]{1,0:T(8,128)S(1)} %slice_bitcast_fusion), channel_id=1, source_target_pairs={{0,1},{1,0},{2,3},{3,2},{4,5},{5,4},{6,7},{7,6},{8,9},{9,8},{10,11... | collective-permute-start | bytes 983048 | tf_op jit(solution)/shard_map/ppermute | solution.py:399
  11.5 45.6 %copy-start.3 = (f32[512,64]{0,1:T(8,128)S(1)}, f32[512,64]{0,1:T(8,128)}, u32[]{:S(2)}) copy-start(f32[512,64]{0,1:T(8,128)} %param.6) | copy-start | bytes 393220
  51.2 5.9 %collective-permute-start.1 = (f32[640,128]{1,0:T(8,128)S(1)}, f32[640,128]{1,0:T(8,128)S(1)}, u32[]{:S(2)}, u32[]{:S(2)}) collective-permute-start(f32[640,128]{1,0:T(8,128)S(1)} %reshape.13.refs_1_), channel_id=1, source_target_pairs={{0,1},{1,0},{2,3},{3,2},{4,5},{5,4},{6,7},{7,6},{8,9},{9,8},{10,11... | collective-permute-start | bytes 983048 | tf_op jit(solution)/shard_map/ppermute | solution.py:399
  74.4 13.0 %collective-permute-start.4 = (f32[64,1792]{1,0:T(8,128)S(1)}, f32[64,1792]{1,0:T(8,128)S(1)}, u32[]{:S(2)}, u32[]{:S(2)}) collective-permute-start(f32[64,1792]{1,0:T(8,128)S(1)} %group_basis.2.refs_0_.refs_4_), channel_id=1, source_target_pairs={{0,64},{64,128},{128,192},{192,0},{1,65},{65,129},{129,193},{193,1... | collective-permute-start | bytes 1376264 | tf_op jit(solution)/shard_map/ppermute | solution.py:430
  75.7 11.8 %collective-permute-start.2 = (f32[64,1792]{1,0:T(8,128)S(1)}, f32[64,1792]{1,0:T(8,128)S(1)}, u32[]{:S(2)}, u32[]{:S(2)}) collective-permute-start(f32[64,1792]{1,0:T(8,128)S(1)} %group_basis.2.refs_0_.refs_4_), channel_id=1, source_target_pairs={{0,192},{64,0},{128,64},{192,128},{1,193},{65,1},{129,65},{193,129... | collective-permute-start | bytes 1376264 | tf_op jit(solution)/shard_map/ppermute | solution.py:429
  77.2 24.9 %copy-start = (f32[3584,128]{1,0:T(8,128)S(1)}, f32[3584,128]{1,0:T(8,128)}, u32[]{:S(2)}) copy-start(f32[3584,128]{1,0:T(8,128)} %test_ref.3) | copy-start | bytes 5505028
  80.4 16.9 %collective-permute-start.5 = (f32[64,1792]{1,0:T(8,128)S(1)}, f32[64,1792]{1,0:T(8,128)S(1)}, u32[]{:S(2)}, u32[]{:S(2)}) collective-permute-start(f32[64,1792]{1,0:T(8,128)S(1)} %group_basis.3.refs_1_.refs_5_), channel_id=1, source_target_pairs={{0,64},{64,128},{128,192},{192,0},{1,65},{65,129},{129,193},{193,1... | collective-permute-start | bytes 1376264 | tf_op jit(solution)/shard_map/ppermute | solution.py:432
  80.4 16.9 %collective-permute-start.3 = (f32[64,1792]{1,0:T(8,128)S(1)}, f32[64,1792]{1,0:T(8,128)S(1)}, u32[]{:S(2)}, u32[]{:S(2)}) collective-permute-start(f32[64,1792]{1,0:T(8,128)S(1)} %group_basis.3.refs_1_.refs_5_), channel_id=1, source_target_pairs={{0,192},{64,0},{128,64},{192,128},{1,193},{65,1},{129,65},{193,129... | collective-permute-start | bytes 1376264 | tf_op jit(solution)/shard_map/ppermute | solution.py:431
  87.4 14.7 %collective-permute-start.7 = (f32[64,896]{1,0:T(8,128)S(1)}, f32[64,896]{1,0:T(8,128)S(1)}, u32[]{:S(2)}, u32[]{:S(2)}) collective-permute-start(f32[64,896]{1,0:T(8,128)S(1)} %slice.35), channel_id=1, source_target_pairs={{0,64},{64,128},{128,192},{192,0},{1,65},{65,129},{129,193},{193,1... | collective-permute-start | bytes 688136 | tf_op jit(solution)/shard_map/ppermute | solution.py:435
  87.5 14.6 %collective-permute-start.6 = (f32[64,896]{1,0:T(8,128)S(1)}, f32[64,896]{1,0:T(8,128)S(1)}, u32[]{:S(2)}, u32[]{:S(2)}) collective-permute-start(f32[64,896]{1,0:T(8,128)S(1)} %slice.34), channel_id=1, source_target_pairs={{0,192},{64,0},{128,64},{192,128},{1,193},{65,1},{129,65},{193,129... | collective-permute-start | bytes 688136 | tf_op jit(solution)/shard_map/ppermute | solution.py:434
  97.2 9.8 %collective-permute-start.9 = (f32[64,896]{1,0:T(8,128)S(1)}, f32[64,896]{1,0:T(8,128)S(1)}, u32[]{:S(2)}, u32[]{:S(2)}) collective-permute-start(f32[64,896]{1,0:T(8,128)S(1)} %slice.37), channel_id=1, source_target_pairs={{0,64},{64,128},{128,192},{192,0},{1,65},{65,129},{129,193},{193,1... | collective-permute-start | bytes 688136 | tf_op jit(solution)/shard_map/ppermute | solution.py:437
  97.4 9.7 %collective-permute-start.8 = (f32[64,896]{1,0:T(8,128)S(1)}, f32[64,896]{1,0:T(8,128)S(1)}, u32[]{:S(2)}, u32[]{:S(2)}) collective-permute-start(f32[64,896]{1,0:T(8,128)S(1)} %slice.36), channel_id=1, source_target_pairs={{0,192},{64,0},{128,64},{192,128},{1,193},{65,1},{129,65},{193,129... | collective-permute-start | bytes 688136 | tf_op jit(solution)/shard_map/ppermute | solution.py:436
  107.0 1.7 %copy-start.1 = (f32[64,896]{1,0:T(8,128)}, f32[64,896]{1,0:T(8,128)S(1)}, u32[]{:S(2)}) copy-start(f32[64,896]{1,0:T(8,128)S(1)} %collective-permute-done.8.refs_8_.refs_12_) | copy-start | bytes 688132
  108.7 39.9 %copy-start.4 = (f32[256,64]{0,1:T(8,128)S(1)}, f32[256,64]{0,1:T(8,128)}, u32[]{:S(2)}) copy-start(f32[256,64]{0,1:T(8,128)} %param.7) | copy-start | bytes 196612
  108.8 2.4 %collective-permute-start.10 = (f32[320,128]{1,0:T(8,128)S(1)}, f32[320,128]{1,0:T(8,128)S(1)}, u32[]{:S(2)}, u32[]{:S(2)}) collective-permute-start(f32[320,128]{1,0:T(8,128)S(1)} %slice_bitcast_fusion.2), channel_id=1, source_target_pairs={{0,1},{1,0},{2,3},{3,2},{4,5},{5,4},{6,7},{7,6},{8,9},{9,8},{10,11... | collective-permute-start | bytes 491528 | tf_op jit(solution)/shard_map/ppermute | solution.py:399
  143.0 5.6 %collective-permute-start.11 = (f32[320,128]{1,0:T(8,128)S(1)}, f32[320,128]{1,0:T(8,128)S(1)}, u32[]{:S(2)}, u32[]{:S(2)}) collective-permute-start(f32[320,128]{1,0:T(8,128)S(1)} %bitcast.18), channel_id=1, source_target_pairs={{0,1},{1,0},{2,3},{3,2},{4,5},{5,4},{6,7},{7,6},{8,9},{9,8},{10,11... | collective-permute-start | bytes 491528 | tf_op jit(solution)/shard_map/ppermute | solution.py:399
  148.6 0.9 copy-start.2
